TPU v7x, 32 devices: a whole 2x2x4 slice. The times are simulated.
32 devices in a mesh: dp: 4 (over x, y), seq: 8 (over z, core).
Axes of the slice: x: 2, y: 2, z: 4, core: 2. Of those that a mesh axis runs over, the one named last changes fastest.
Arguments:
- hidden: bfloat16 [65536, 2048], P(('dp', 'seq')), parts along dimension 0
- w_query: bfloat16 [2048, 8, 256], replicated
- w_key: bfloat16 [2048, 8, 256], replicated
- w_value: bfloat16 [2048, 8, 256], replicated
- w_out: bfloat16 [8, 256, 2048], replicated
Outputs:
- output: bfloat16 [65536, 2048], P(('dp', 'seq')), parts along dimension 0
There are 4 independent parts. A program takes and returns all parts, laid end to end along the dimension named above; an argument that names none is the same for every part.
All inputs are finite; a program needn't handle non-finite values.
Results may differ from a plain program's by a relative error of at most 0.00368.
Values are sent between devices in bfloat16 or wider.
A program may use at most 1 GiB of HBM per device.

v0:
```python
import math
import jax
import jax.numpy as jnp
from jax import lax
from jax.sharding import PartitionSpec as P

SEG_BASE = 2048
BRANCHES = 4


def thin_rows(array_in, dilation):
    n_rows, num_heads, head_width = array_in.shape
    row_grid = array_in.reshape(n_rows // dilation, dilation, num_heads // dilation, dilation, head_width)
    picked = jnp.stack([row_grid[:, head_slot, :, head_slot, :] for head_slot in range(dilation)], axis=2)
    return picked.reshape(n_rows // dilation, num_heads, head_width)


def group_gather(block, group_size, axis_size):
    seq_index = lax.axis_index('seq')
    gathered = block[None]
    for level_bit in range(int(math.log2(group_size))):
        step_size = 2 ** level_bit
        perm_pairs = [(source, source ^ step_size) for source in range(axis_size)]
        received = lax.ppermute(gathered, 'seq', perm_pairs)
        upper_half = (seq_index // step_size) % 2 == 1
        gathered = jnp.where(upper_half, jnp.concatenate([received, gathered]), jnp.concatenate([gathered, received]))
    return gathered


def head_attention(q_blocks, k_blocks, v_blocks, q_start):
    allowed = (q_start + jnp.arange(q_blocks.shape[1]))[:, None] >= jnp.arange(k_blocks.shape[1])[None, :]
    logits = jnp.einsum('nqe,nke->nqk', q_blocks, k_blocks, preferred_element_type=jnp.float32)
    logits = jnp.where(allowed[None], logits, -jnp.inf)
    row_max = jnp.max(logits, axis=2, keepdims=True)
    exp_scores = jnp.exp(logits - row_max)
    row_sum = jnp.sum(exp_scores, axis=2)
    weighted = jnp.einsum('nqk,nke->nqe', exp_scores.astype(jnp.bfloat16), v_blocks, preferred_element_type=jnp.float32)
    return weighted / row_sum[:, :, None], row_max[:, :, 0] + jnp.log(row_sum)


def spread_rows(branch_out, branch_lse, dilation, head_slot):
    chosen = jnp.arange(dilation) == head_slot
    n_rows, head_width = branch_out.shape
    dense_out = (branch_out[:, None, :] * chosen[None, :, None].astype(jnp.float32)).reshape(n_rows * dilation, head_width)
    dense_lse = jnp.where(chosen[None, :], branch_lse[:, None], -jnp.inf).reshape(n_rows * dilation)
    return dense_out, dense_lse


def merge_branches(dense_outs, dense_lses):
    lse_all = jnp.stack(dense_lses)
    lse_max = jnp.max(lse_all, axis=0)
    branch_weights = jnp.exp(lse_all - lse_max[None, :])
    merged = jnp.sum(branch_weights[:, :, None] * jnp.stack(dense_outs), axis=0)
    return (merged / jnp.sum(branch_weights, axis=0)[:, None]).astype(jnp.bfloat16)


def attend_all(branch_plans, num_heads, head_dim):
    def one_head(head_idx):
        dense_outs = []
        dense_lses = []
        for branch, branch_plan in enumerate(branch_plans):
            q_blocks, k_blocks, v_blocks, q_start = branch_plan
            dilation = 2 ** branch
            branch_out, branch_lse = head_attention(
                lax.dynamic_index_in_dim(q_blocks, head_idx, axis=2, keepdims=False),
                lax.dynamic_index_in_dim(k_blocks, head_idx, axis=2, keepdims=False),
                lax.dynamic_index_in_dim(v_blocks, head_idx, axis=2, keepdims=False),
                q_start)
            dense_out, dense_lse = spread_rows(branch_out.reshape(-1, head_dim), branch_lse.reshape(-1), dilation, head_idx % dilation)
            dense_outs.append(dense_out)
            dense_lses.append(dense_lse)
        return merge_branches(dense_outs, dense_lses)
    return lax.map(one_head, jnp.arange(num_heads))


def solution(mesh):
    axis_size = mesh.shape['seq']
    row_spec = P(('dp', 'seq'), None)

    def device_program(hidden, w_query, w_key, w_value, w_out):
        tokens = hidden.shape[0]
        num_heads = w_query.shape[1]
        head_dim = w_query.shape[2]
        seq_index = lax.axis_index('seq')
        q_rows = (jnp.einsum('td,dhe->the', hidden, w_query, preferred_element_type=jnp.float32) * head_dim ** -0.5).astype(jnp.bfloat16)
        k_rows = jnp.einsum('td,dhe->the', hidden, w_key, preferred_element_type=jnp.float32).astype(jnp.bfloat16)
        v_rows = jnp.einsum('td,dhe->the', hidden, w_value, preferred_element_type=jnp.float32).astype(jnp.bfloat16)
        branch_plans = []
        for branch in range(BRANCHES):
            dilation = 2 ** branch
            seg_len = SEG_BASE * dilation
            kept_len = tokens // dilation
            q_thin = thin_rows(q_rows, dilation)
            k_thin = thin_rows(k_rows, dilation)
            v_thin = thin_rows(v_rows, dilation)
            if seg_len <= tokens:
                blocks = tokens // seg_len
                block_shape = (blocks, SEG_BASE, num_heads, head_dim)
                branch_plans.append((q_thin.reshape(block_shape), k_thin.reshape(block_shape), v_thin.reshape(block_shape), 0))
            else:
                group_size = seg_len // tokens
                kv_gathered = group_gather(jnp.stack([k_thin, v_thin]), group_size, axis_size)
                key_shape = (1, group_size * kept_len, num_heads, head_dim)
                branch_plans.append((q_thin.reshape(1, kept_len, num_heads, head_dim), kv_gathered[:, 0].reshape(key_shape), kv_gathered[:, 1].reshape(key_shape), (seq_index % group_size) * kept_len))
        mixed = attend_all(branch_plans, num_heads, head_dim)
        return jnp.einsum('hte,hed->td', mixed, w_out, preferred_element_type=jnp.float32).astype(jnp.bfloat16)

    return jax.shard_map(device_program, mesh=mesh, in_specs=(row_spec, P(), P(), P(), P()), out_specs=row_spec, check_vma=False)
```

profile of v0, /device:TPU:0, one launch (start us, length us, event | category | flops | bytes accessed | tf_op | source)
XLA Modules:
  0.0 1334.8 jit_solution(13369851524711112238)
XLA Ops:
  0.0 23.5 %fusion.91 = bf16[2048,8,256]{2,0,1:T(8,128)(2,1)} fusion(bf16[2048,8,256]{2,1,0:T(8,128)(2,1)} %param.9, bf16[2048,2048]{1,0:T(8,128)(2,1)} %param.7), kind=kOutput, calls=%fused_computation.116 | convolution fusion | flops 17184063488 | bytes 25165824 | tf_op jit(solution)/shard_map/td,dhe->the/dot_general | solution.py:86
  23.5 20.5 %fusion.96 = bf16[2048,8,256]{2,0,1:T(8,128)(2,1)} fusion(bf16[2048,8,256]{2,1,0:T(8,128)(2,1)S(1)} %copy-done.5, bf16[2048,2048]{1,0:T(8,128)(2,1)S(1)} %copy-done.6), kind=kOutput, calls=%fused_computation.117 | convolution fusion | flops 17184063488 | bytes 25165824 | tf_op jit(solution)/shard_map/td,dhe->the/dot_general | solution.py:87
  44.1 13.1 reshape.846
  57.1 8.8 fusion.142
  68.0 13.1 reshape.845
  81.1 9.0 fusion.141
  94.4 6.2 maximum_bitcast_fusion
  110.8 12.5 reshape.849
  123.3 7.2 fusion.139
  130.5 12.5 reshape.848
  145.7 6.3 fusion.138
  155.9 4.7 maximum_select_fusion.5
  163.2 23.4 %multiply_convert_fusion = bf16[2048,8,256]{2,0,1:T(8,128)(2,1)} fusion(bf16[2048,8,256]{2,1,0:T(8,128)(2,1)} %param.8, bf16[2048,2048]{1,0:T(8,128)(2,1)} %param.7), kind=kOutput, calls=%fused_computation.103 | convolution fusion | flops 17188257792 | bytes 25165824 | tf_op jit(solution)/shard_map/td,dhe->the/dot_general | solution.py:85
  186.6 13.1 reshape.844
  199.8 10.5 maximum_select_fusion.3
  211.1 8.4 fusion.143
  219.5 12.5 reshape.847
  237.1 7.1 fusion.140
  254.6 9.1 maximum_select_fusion.4
  276.7 10.5 maximum_select_fusion
  287.2 6.5 fusion.134
  293.6 11.4 copy.105
  305.0 8.3 copy.147
  313.4 11.4 copy.144
  324.7 8.5 copy.150
  333.2 269.5 %collective-permute-done.2 = bf16[2,2,512,8,256]{4,2,3,1,0:T(8,128)(2,1)} collective-permute-done((bf16[2,2,512,8,256]{4,2,3,1,0:T(8,128)(2,1)}, bf16[2,2,512,8,256]{4,2,3,1,0:T(8,128)(2,1)}, u32[]{:S(2)}, u32[]{:S(2)}) %collective-permute-start.2) | collective-permute-done | bytes 8388640 | tf_op jit(solution)/shard_map/ppermute | solution.py:24
  602.7 11.9 maximum_select_fusion.1
  614.6 6.1 fusion.133
  620.7 11.4 copy.118
  632.2 8.3 copy.148
  640.5 11.4 copy.145
  652.0 8.3 copy.151
  660.3 11.9 maximum_select_fusion.2
  672.2 6.5 fusion.132
  678.7 11.8 copy.143
  690.5 8.4 copy.149
  698.9 11.8 copy.146
  710.7 8.3 copy.152
  719.0 592.1 %while.15 = (s32[]{:T(128)}, bf16[8,2048,256]{2,1,0:T(8,128)(2,1)}, s32[8]{0:T(128)S(1)}, bf16[1,2048,8,256]{3,1,2,0:T(8,128)(2,1)}, bf16[1,2048,8,256]{3,1,2,0:...) while((s32[]{:T(128)}, bf16[8,2048,256]{2,1,0:T(8,128)(2,1)}, ...), condition=%wide.region_11.12_spmd, body=%wide.region_0.11_spmd.sunk | while | flops 8151088640 | bytes 147732176 | solution.py:73
  758.9 9.7 fusion.183
  768.6 7.3 fusion.184
  775.9 10.0 divide_bitcast_fusion.2
  832.9 9.7 fusion.183
  842.5 7.3 fusion.184
  849.9 10.0 divide_bitcast_fusion.2
  906.8 9.7 fusion.183
  916.5 7.3 fusion.184
  923.8 10.0 divide_bitcast_fusion.2
  980.8 9.7 fusion.183
  990.4 7.3 fusion.184
  997.8 10.0 divide_bitcast_fusion.2
  1054.8 9.7 fusion.183
  1064.5 7.3 fusion.184
  1071.8 10.0 divide_bitcast_fusion.2
  1128.8 9.7 fusion.183
  1138.4 7.3 fusion.184
  1145.7 10.0 divide_bitcast_fusion.2
  1202.7 9.7 fusion.183
  1212.3 7.3 fusion.184
  1219.7 10.0 divide_bitcast_fusion.2
  1276.6 9.7 fusion.183
  1286.3 7.3 fusion.184
  1293.6 10.0 divide_bitcast_fusion.2
  1311.1 23.5 %bitcast_convert_fusion = bf16[2048,2048]{1,0:T(8,128)(2,1)} fusion(bf16[8,2048,256]{2,1,0:T(8,128)(2,1)} %get-tuple-element.410, bf16[8,256,2048]{2,1,0:T(8,128)(2,1)} %param.11), kind=kOutput, calls=%fused_computation.102 | convolution fusion | flops 17184063488 | bytes 25165824 | tf_op jit(solution)/shard_map/hte,hed->td/dot_general | solution.py:106
  (442 shorter events, 406.6 us)
Async XLA Ops:
  0.0 23.5 %copy-start.6 = (bf16[2048,2048]{1,0:T(8,128)(2,1)S(1)}, bf16[2048,2048]{1,0:T(8,128)(2,1)}, u32[]{:S(2)}) copy-start(bf16[2048,2048]{1,0:T(8,128)(2,1)} %param.7) | copy-start | bytes 25165828
  0.0 23.5 %copy-start.5 = (bf16[2048,8,256]{2,1,0:T(8,128)(2,1)S(1)}, bf16[2048,8,256]{2,1,0:T(8,128)(2,1)}, u32[]{:S(2)}) copy-start(bf16[2048,8,256]{2,1,0:T(8,128)(2,1)} %param.10) | copy-start | bytes 25165828
  90.1 1.6 copy-start.3
  100.6 176.1 %collective-permute-start = (bf16[1,2,1024,8,256]{4,2,3,1,0:T(8,128)(2,1)}, bf16[1,2,1024,8,256]{4,2,3,1,0:T(8,128)(2,1)}, u32[]{:S(2)}, u32[]{:S(2)}) collective-permute-start(bf16[1,2,1024,8,256]{4,2,3,1,0:T(8,128)(2,1)} %maximum_bitcast_fusion), channel_id=1, source_target_pairs={{0,1},{1,0},{2,3},{3,2},{4,5},{5,4},{6,7},{7,6},{8,9},{9,8},{10,11... | collective-permute-start | bytes 25165832 | tf_op jit(solution)/shard_map/ppermute | solution.py:24
  110.7 45.2 %collective-permute-start.3 = (bf16[1,2,256,8,256]{4,2,3,1,0:T(8,128)(2,1)S(1)}, bf16[1,2,256,8,256]{4,2,3,1,0:T(8,128)(2,1)}, u32[]{:S(2)}, u32[]{:S(2)}) collective-permute-start(bf16[1,2,256,8,256]{4,2,3,1,0:T(8,128)(2,1)S(1)} %maximum_bitcast_fusion.2), channel_id=1, source_target_pairs={{0,1},{1,0},{2,3},{3,2},{4,5},{5,4},{6,7},{7,6},{8,9},{9,8},{10,11... | collective-permute-start | bytes 6291464 | tf_op jit(solution)/shard_map/ppermute | solution.py:24
  143.0 9.2 copy-start.4
  155.4 44.3 %collective-permute-start.1 = (bf16[1,2,512,8,256]{4,2,3,1,0:T(8,128)(2,1)}, bf16[1,2,512,8,256]{4,2,3,1,0:T(8,128)(2,1)}, u32[]{:S(2)}, u32[]{:S(2)}) collective-permute-start(bf16[1,2,512,8,256]{4,2,3,1,0:T(8,128)(2,1)} %maximum_bitcast_fusion.1), channel_id=1, source_target_pairs={{0,1},{1,0},{2,3},{3,2},{4,5},{5,4},{6,7},{7,6},{8,9},{9,8},{10,11... | collective-permute-start | bytes 12582920 | tf_op jit(solution)/shard_map/ppermute | solution.py:24
  160.6 94.0 %collective-permute-start.4 = (bf16[2,2,256,8,256]{4,2,3,1,0:T(8,128)(2,1)}, bf16[2,2,256,8,256]{4,2,3,1,0:T(8,128)(2,1)}, u32[]{:S(2)}, u32[]{:S(2)}) collective-permute-start(bf16[2,2,256,8,256]{4,2,3,1,0:T(8,128)(2,1)} %maximum_select_fusion.5), channel_id=1, source_target_pairs={{0,2},{1,3},{2,0},{3,1},{4,6},{5,7},{6,4},{7,5},{8,10},{9,11},{10,... | collective-permute-start | bytes 12582920 | tf_op jit(solution)/shard_map/ppermute | solution.py:24
  199.8 11.3 copy-start
  210.3 392.4 %collective-permute-start.2 = (bf16[2,2,512,8,256]{4,2,3,1,0:T(8,128)(2,1)}, bf16[2,2,512,8,256]{4,2,3,1,0:T(8,128)(2,1)}, u32[]{:S(2)}, u32[]{:S(2)}) collective-permute-start(bf16[2,2,512,8,256]{4,2,3,1,0:T(8,128)(2,1)} %maximum_select_fusion.3), channel_id=1, source_target_pairs={{0,2},{1,3},{2,0},{3,1},{4,6},{5,7},{6,4},{7,5},{8,10},{9,11},{10,... | collective-permute-start | bytes 25165832 | tf_op jit(solution)/shard_map/ppermute | solution.py:24
  232.0 3.4 copy-start.1
  246.0 4.4 copy-start.2
  250.4 26.3 %slice-start = ((s8[8388608]{0:T(1024)(128)(4,1)}), s8[4194304]{0:T(1024)(128)(4,1)S(1)}, s32[]{:S(2)}) async-start(s8[8388608]{0:T(1024)(128)(4,1)} %bitcast.308), calls=%async_computation | async-start | bytes 8388608
  252.9 23.8 %slice-start.1 = ((s8[8388608]{0:T(1024)(128)(4,1)}), s8[4194304]{0:T(1024)(128)(4,1)S(1)}, s32[]{:S(2)}) async-start(s8[8388608]{0:T(1024)(128)(4,1)} %bitcast.308), calls=%async_computation.1 | async-start | bytes 8388608
  263.8 396.5 %collective-permute-start.5 = (bf16[4,2,256,8,256]{4,2,3,1,0:T(8,128)(2,1)}, bf16[4,2,256,8,256]{4,2,3,1,0:T(8,128)(2,1)}, u32[]{:S(2)}, u32[]{:S(2)}) collective-permute-start(bf16[4,2,256,8,256]{4,2,3,1,0:T(8,128)(2,1)} %maximum_select_fusion.4), channel_id=1, source_target_pairs={{0,4},{1,5},{2,6},{3,7},{4,0},{5,1},{6,2},{7,3},{8,12},{9,13},{10,... | collective-permute-start | bytes 25165832 | tf_op jit(solution)/shard_map/ppermute | solution.py:24
where the time goes:
time: 1350 us; the launch traced here: 1330 us
  local copies, waits for them, and re-layouts  398 us (29%)
  matrix products  364 us (27%)
  waiting for transfers between devices  271 us (20%)
  other arithmetic  270 us (20%)
  loops' own time  24.3 us (2%)
    ppermute x6, waiting for transfers between devices, group_gather(): received = lax.ppermute(gathered, 'seq', perm_pairs)  271 us
    dot_general x32, matrix products, head_attention(): jnp.einsum('nqk,nke->nqe', exp_scores.astype(jnp.bfloat16), v_blocks, pre...  139 us
    dot_general x32, matrix products, head_attention(): jnp.einsum('nqe,nke->nqk', q_blocks, k_blocks, preferred_element_type=jnp...  134 us
    reduce_sum x32, other arithmetic, head_attention(): row_sum = jnp.sum(exp_scores, axis=2)  91 us
    mul x80, local copies, waits for them, and re-layouts, spread_rows(): branch_out[:, None, :] * chosen[None, :, None].astype(jnp.float32)  87 us
    reshape x6, local copies, waits for them, and re-layouts, thin_rows(): array_in.reshape(n_rows // dilation, dilation, num_heads // dilation, dil...  76.7 us
    slice x9, local copies, waits for them, and re-layouts, thin_rows(): row_grid[:, head_slot, :, head_slot, :]  60.2 us
    select_n x6, other arithmetic, group_gather(): jnp.where(upper_half, jnp.concatenate([received, gathered]), jnp.concaten...  58.6 us
  transfers between devices with their start and end apart: 6, of which 2 were waited for; matrix products, arithmetic and copies ran while one was open for 21% of the time, Pallas kernels for 0%

commit v1 on v0

v1 whole, which is shorter than its diff:
```python
import math
import jax
import jax.numpy as jnp
from jax import lax
from jax.experimental import pallas as pl
from jax.experimental.pallas import tpu as pltpu
from jax.sharding import PartitionSpec as P

CHUNK = 256
CLASSES = 8
RUN = CHUNK // CLASSES
LOG2E = math.log2(math.e)
F32 = jnp.float32
BF16 = jnp.bfloat16
VMEM_LIMIT = 60 * 1024 * 1024


def params():
    return pltpu.CompilerParams(vmem_limit_bytes=VMEM_LIMIT, dimension_semantics=("arbitrary",))


def dot_nt(a, b):
    return lax.dot_general(a, b, (((1,), (1,)), ((), ())), preferred_element_type=F32)


def dot_nn(a, b):
    return lax.dot_general(a, b, (((1,), (0,)), ((), ())), preferred_element_type=F32)


def class_of_group(head, group):
    return head ^ (0, 4, 2, 6)[group]


def run_rows(chunk, cls):
    return pl.ds(pl.multiple_of(chunk * CHUNK + cls * RUN, RUN), RUN)


def gather_class(ref, cls, n_chunks):
    return jnp.concatenate([ref[0, run_rows(i, cls), :] for i in range(n_chunks)], axis=0)


def unpermute_matrix():
    row = lax.broadcasted_iota(jnp.int32, (CHUNK, CHUNK), 0)
    col = lax.broadcasted_iota(jnp.int32, (CHUNK, CHUNK), 1)
    return (row == (col % RUN) * CLASSES + col // RUN).astype(F32).astype(BF16)


def pack_kernel(n_groups, src_ref, *out_refs):
    head = pl.program_id(0)
    n_chunks = src_ref.shape[1] // CHUNK
    rows = n_chunks * RUN
    for group in range(n_groups):
        cls = class_of_group(head, group)
        block = gather_class(src_ref, cls, n_chunks)
        for out_ref in out_refs:
            if out_ref.shape[1] > group * rows:
                out_ref[0, group * rows:(group + 1) * rows, :] = block


def pack(src, group_counts):
    num_heads, tokens, width = src.shape
    rows = tokens // CLASSES
    shapes = [(num_heads, rows * count, width) for count in group_counts]
    spec = lambda shape: pl.BlockSpec((1,) + shape[1:], lambda h: (h, 0, 0))
    return pl.pallas_call(
        lambda *refs: pack_kernel(max(group_counts), *refs),
        grid=(num_heads,),
        out_shape=[jax.ShapeDtypeStruct(s, BF16) for s in shapes],
        in_specs=[spec(src.shape)],
        out_specs=[spec(s) for s in shapes],
        compiler_params=params(),
        cost_estimate=pl.CostEstimate(flops=10 ** 8, bytes_accessed=2 * src.size * 2, transcendentals=0),
        name="pack",
    )(src)


def update(q, blocks, m, l, acc):
    scores = [dot_nt(q, keys) * LOG2E for keys, _, _ in blocks]
    m_new = m
    for s in scores:
        m_new = jnp.maximum(m_new, jnp.max(s, axis=1, keepdims=True))
    alpha = jnp.exp2(m - m_new)
    l = l * alpha
    acc = acc * alpha
    for s, (_, values, log_mult) in zip(scores, blocks):
        p = jnp.exp2(s - (m_new - log_mult))
        l = l + jnp.sum(p, axis=1, keepdims=True)
        acc = acc + dot_nn(p.astype(BF16), values)
    return m_new, l, acc


def local_kernel(flag_ref, q_ref, k_ref, v_ref, pk_ref, pv_ref, o_ref, lse_ref, pat_ref):
    head = pl.program_id(0)
    tokens = q_ref.shape[1]
    n_chunks = tokens // CHUNK
    rows = n_chunks * RUN

    row = lax.broadcasted_iota(jnp.int32, (CHUNK, CHUNK), 0)
    col = lax.broadcasted_iota(jnp.int32, (CHUNK, CHUNK), 1)
    row_x = (row // RUN) ^ head
    col_x = (col // RUN) ^ head
    both = row_x | col_x
    log_mult = jnp.where(both == 0, 2.0, jnp.where(both % 4 == 0, math.log2(3.0), jnp.where(both % 2 == 0, 1.0, 0.0)))
    causal = (row % RUN) * CLASSES + row // RUN >= (col % RUN) * CLASSES + col // RUN
    pat_ref[:, :CHUNK] = log_mult
    pat_ref[:, CHUNK:] = jnp.where(causal, log_mult, -jnp.inf)

    for i in range(n_chunks):
        q = q_ref[0, i * CHUNK:(i + 1) * CHUNK, :]
        scores = []
        m = None
        for j in range(i + 1):
            s = dot_nt(q, k_ref[0, j * CHUNK:(j + 1) * CHUNK, :])
            s = s * LOG2E + (pat_ref[:, CHUNK:] if j == i else pat_ref[:, :CHUNK])
            scores.append(s)
            m = s if m is None else jnp.maximum(m, s)
        m = jnp.max(m, axis=1, keepdims=True)
        total = None
        acc = None
        for j in range(i + 1):
            p = jnp.exp2(scores[j] - m)
            total = p if total is None else total + p
            part = dot_nn(p.astype(BF16), v_ref[0, j * CHUNK:(j + 1) * CHUNK, :])
            acc = part if acc is None else acc + part
        l = jnp.sum(total, axis=1, keepdims=True)
        o_ref[0, i * CHUNK:(i + 1) * CHUNK, :] = acc / l
        lse_ref[0, i * CHUNK:(i + 1) * CHUNK, :] = jnp.broadcast_to(m + jnp.log2(l), (CHUNK, 128))

    mult = ((3, 2, 1, 1), (2, 2, 1, 1), (1, 1, 1, 1), (1, 1, 1, 1))

    @pl.when(flag_ref[0] == 1)
    def _():
        for group in range(4):
            cls = class_of_group(head, group)
            q = gather_class(q_ref, cls, n_chunks)
            acc = gather_class(o_ref, cls, n_chunks)
            m = gather_class(lse_ref, cls, n_chunks)[:, :1]
            blocks = [(pk_ref[0, g * rows:(g + 1) * rows, :], pv_ref[0, g * rows:(g + 1) * rows, :], math.log2(mult[group][g]))
                      for g in range(4)]
            m, l, acc = update(q, blocks, m, jnp.ones_like(m), acc)
            out = acc / l
            lse = jnp.broadcast_to(m + jnp.log2(l), (rows, 128))
            for i in range(n_chunks):
                o_ref[0, run_rows(i, cls), :] = out[i * RUN:(i + 1) * RUN, :]
                lse_ref[0, run_rows(i, cls), :] = lse[i * RUN:(i + 1) * RUN, :]


def head_spec(shape):
    return pl.BlockSpec((1,) + shape[1:], lambda h, flags: (h, 0, 0))


def local_attention(flags, q, k, v, pair_k, pair_v):
    num_heads, tokens, _ = q.shape
    lse_shape = (num_heads, tokens, 128)
    return pl.pallas_call(
        local_kernel,
        grid_spec=pltpu.PrefetchScalarGridSpec(
            num_scalar_prefetch=1,
            grid=(num_heads,),
            in_specs=[head_spec(a.shape) for a in (q, k, v, pair_k, pair_v)],
            out_specs=[head_spec(q.shape), head_spec(lse_shape)],
            scratch_shapes=[pltpu.VMEM((CHUNK, 2 * CHUNK), F32)],
        ),
        out_shape=[jax.ShapeDtypeStruct(q.shape, F32), jax.ShapeDtypeStruct(lse_shape, F32)],
        compiler_params=params(),
        cost_estimate=pl.CostEstimate(flops=4 * 10 ** 10, bytes_accessed=6 * 10 ** 7, transcendentals=3 * 10 ** 7),
        name="local_attention",
    )(flags, q, k, v, pair_k, pair_v)


def far_kernel(flag_ref, qa_ref, qb_ref, *refs):
    keys, values, outs = refs[:4], refs[4:8], refs[8:]

    @pl.when(flag_ref[2] == 1)
    def _():
        for side, q_ref in enumerate((qa_ref, qb_ref)):
            q = q_ref[0]
            scores = [dot_nt(q, k_ref[0]) * LOG2E for k_ref in keys]
            m = jnp.max(jnp.maximum(jnp.maximum(scores[0], scores[1]), jnp.maximum(scores[2], scores[3])), axis=1, keepdims=True)
            probs = [jnp.exp2(s - m) for s in scores]
            l = jnp.sum(probs[0] + probs[1] + probs[2] + probs[3], axis=1, keepdims=True)
            acc = None
            for p, v_ref in zip(probs, values):
                part = dot_nn(p.astype(BF16), v_ref[0])
                acc = part if acc is None else acc + part
            outs[2 * side][0] = acc / l
            lse = jnp.broadcast_to(m + jnp.log2(l), (q.shape[0], 128))
            outs[2 * side + 1][0] = jnp.transpose(lse)[:8, :]


def far_attention(flags, q_own, q_later, keys, values):
    num_heads, rows, _ = q_own.shape
    lse_shape = (num_heads, 8, rows)
    ins = (q_own, q_later, *keys, *values)
    return pl.pallas_call(
        far_kernel,
        grid_spec=pltpu.PrefetchScalarGridSpec(
            num_scalar_prefetch=1,
            grid=(num_heads,),
            in_specs=[head_spec(a.shape) for a in ins],
            out_specs=[head_spec(q_own.shape), head_spec(lse_shape)] * 2,
        ),
        out_shape=[jax.ShapeDtypeStruct(q_own.shape, F32), jax.ShapeDtypeStruct(lse_shape, F32)] * 2,
        compiler_params=params(),
        cost_estimate=pl.CostEstimate(flops=5 * 10 ** 9, bytes_accessed=2 * 10 ** 7, transcendentals=4 * 10 ** 6),
        name="far_attention",
    )(flags, *ins)


def final_kernel(flag_ref, q_ref, o_in_ref, lse_in_ref, k0_ref, k1_ref, v0_ref, v1_ref,
                 fo0_ref, fl0_ref, fo1_ref, fl1_ref, y_ref, o_ref, lse_ref):
    head = pl.program_id(0)
    n_chunks = q_ref.shape[1] // CHUNK
    rows = n_chunks * RUN
    o_ref[...] = o_in_ref[...]
    for group in range(2):
        lse_ref[group * rows:(group + 1) * rows, :] = gather_class(lse_in_ref, class_of_group(head, group), n_chunks)

    def merge(fo_ref, fl_ref):
        cls = class_of_group(head, 0)
        acc = gather_class(o_ref, cls, n_chunks)
        m = lse_ref[:rows, :1]
        lse = fl_ref[0]
        m_far = jnp.transpose(jnp.concatenate([lse] * 16, axis=0))[:, :1]
        m_new = jnp.maximum(m, m_far)
        a, b = jnp.exp2(m - m_new), jnp.exp2(m_far - m_new)
        total = a + b
        out = (acc * a + fo_ref[0] * b) / total
        lse_ref[:rows, :] = jnp.broadcast_to(m_new + jnp.log2(total), (rows, 128))
        for i in range(n_chunks):
            o_ref[0, run_rows(i, cls), :] = out[i * RUN:(i + 1) * RUN, :]

    @pl.when(flag_ref[2] == 1)
    def _():
        merge(fo0_ref, fl0_ref)

    @pl.when(flag_ref[3] == 1)
    def _():
        merge(fo1_ref, fl1_ref)

    mult = ((2, 1), (1, 1))

    @pl.when(flag_ref[1] == 1)
    def _():
        for group in range(2):
            cls = class_of_group(head, group)
            q = gather_class(q_ref, cls, n_chunks)
            acc = gather_class(o_ref, cls, n_chunks)
            m = lse_ref[group * rows:(group + 1) * rows, :1]
            blocks = [(k_ref[0, g * rows:(g + 1) * rows, :], v_ref[0, g * rows:(g + 1) * rows, :], math.log2(mult[group][g]))
                      for k_ref, v_ref in ((k0_ref, v0_ref), (k1_ref, v1_ref)) for g in range(2)]
            m, l, acc = update(q, blocks, m, jnp.ones_like(m), acc)
            out = acc / l
            for i in range(n_chunks):
                o_ref[0, run_rows(i, cls), :] = out[i * RUN:(i + 1) * RUN, :]

    back = unpermute_matrix()
    for i in range(n_chunks):
        part = o_ref[0, i * CHUNK:(i + 1) * CHUNK, :].astype(BF16)
        y_ref[i * CHUNK:(i + 1) * CHUNK, :] = dot_nn(back, part).astype(BF16)


def final_attention(flags, q, o, lse, keys, values, far):
    num_heads, tokens, width = q.shape
    ins = (q, o, lse, *keys, *values, *far)
    return pl.pallas_call(
        final_kernel,
        grid_spec=pltpu.PrefetchScalarGridSpec(
            num_scalar_prefetch=1,
            grid=(num_heads,),
            in_specs=[head_spec(a.shape) for a in ins],
            out_specs=pl.BlockSpec((tokens, width), lambda h, flags: (0, h)),
            scratch_shapes=[pltpu.VMEM((1, tokens, width), F32), pltpu.VMEM((2 * tokens // CLASSES, 128), F32)],
        ),
        out_shape=jax.ShapeDtypeStruct((tokens, num_heads * width), BF16),
        compiler_params=params(),
        cost_estimate=pl.CostEstimate(flops=8 * 10 ** 9, bytes_accessed=6 * 10 ** 7, transcendentals=5 * 10 ** 6),
        name="final_attention",
    )(flags, *ins)


def solution(mesh):
    row_spec = P(('dp', 'seq'), None)
    pair_up = [(s, s + 1) for s in (0, 2, 4, 6)]
    next_chip = [(0, 2), (1, 3), (4, 6), (5, 7)]
    swap_upper = [(s, s ^ 1) for s in (2, 3, 6, 7)]
    from_first = [(0, 4), (1, 5)]
    from_second = [(2, 4), (3, 5)]
    swap_third = [(4, 5), (5, 4)]
    to_third = [(6, 4), (7, 5)]
    to_fourth = [(4, 6), (5, 7)]

    def send(array, pairs):
        return lax.ppermute(array, 'seq', pairs)

    def layer(hidden, w_query, w_key, w_value, w_out):
        tokens, d_model = hidden.shape
        num_heads, head_dim = w_query.shape[1:]
        index = lax.axis_index('seq')
        chip = index // 2
        flags = jnp.stack([index % 2, chip % 2, (chip == 2).astype(jnp.int32), (chip == 3).astype(jnp.int32)]).astype(jnp.int32)

        order = jnp.arange(CHUNK)
        perm = ((order % RUN) * CLASSES + order // RUN)[:, None] == order[None, :]
        x = jnp.einsum('pq,cqd->cpd', perm.astype(BF16), hidden.reshape(tokens // CHUNK, CHUNK, d_model),
                       preferred_element_type=F32).astype(BF16).reshape(tokens, d_model)

        def project(weight):
            return jnp.einsum('td,dhe->hte', x, weight, preferred_element_type=F32)

        def spread(packs):
            far_rows, quad_rows, pair_rows = packs
            first = send(far_rows, from_first)
            second = send(far_rows, from_second)
            quad = send(quad_rows, next_chip)
            pair = send(pair_rows, pair_up)
            swapped = send(first, swap_third), send(second, swap_third)
            return pair, (quad, send(quad, swap_upper)), (first, second, *swapped)

        k = project(w_key).astype(BF16)
        pair_k, quad_k, far_k = spread(pack(k, (1, 2, 4)))
        v = project(w_value).astype(BF16)
        pair_v, quad_v, far_v = spread(pack(v, (1, 2, 4)))
        q = (project(w_query) * head_dim ** -0.5).astype(BF16)
        q_far, = pack(q, (1,))
        q_later = send(q_far, to_third)

        o, lse = local_attention(flags, q, k, v, pair_k, pair_v)
        own_o, own_lse, later_o, later_lse = far_attention(flags, q_far, q_later, far_k, far_v)
        got_o, got_lse = send(later_o, to_fourth), send(later_lse, to_fourth)
        mixed = final_attention(flags, q, o, lse, quad_k, quad_v, (own_o, own_lse, got_o, got_lse))
        return jnp.dot(mixed, w_out.reshape(num_heads * head_dim, d_model), preferred_element_type=F32).astype(BF16)

    return jax.shard_map(layer, mesh=mesh, in_specs=(row_spec, P(), P(), P(), P()), out_specs=row_spec, check_vma=False)
```

time: 1350 us -> 388 us (0.29)
  the two profiles are of different devices: /device:TPU:0 before, /device:TPU:29 now
where the time goes in v1:
time: 388 us; the launch traced here: 386 us
  Pallas kernels  137 us (35%)
  waiting for transfers between devices  122 us (31%)
  matrix products  97.9 us (25%)
  starting transfers between devices  23.8 us (6%)
  local copies, waits for them, and re-layouts  5.01 us (1%)
    ppermute x17, waiting for transfers between devices, send(): return lax.ppermute(array, 'seq', pairs)  122 us
    pallas_call x1, Pallas kernels, local_attention(): pl.pallas_call(local_kernel, grid_spec=pltpu.PrefetchScalarGridSpec(num_s...  75.5 us
    dot_general x3, matrix products, project(): return jnp.einsum('td,dhe->hte', x, weight, preferred_element_type=F32)  68.2 us
    pallas_call x1, Pallas kernels, final_attention(): pl.pallas_call(final_kernel, grid_spec=pltpu.PrefetchScalarGridSpec(num_s...  29.5 us
    pallas_call x3, Pallas kernels, pack(): pl.pallas_call(lambda *refs: pack_kernel(max(group_counts), *refs), grid=...  23.8 us
    dot_general x1, matrix products, layer(): jnp.dot(mixed, w_out.reshape(num_heads * head_dim, d_model), preferred_el...  23.8 us
    ppermute x17, starting transfers between devices, send(): return lax.ppermute(array, 'seq', pairs)  23.8 us
    pallas_call x1, Pallas kernels, far_attention(): pl.pallas_call(far_kernel, grid_spec=pltpu.PrefetchScalarGridSpec(num_sca...  8.51 us
  transfers between devices with their start and end apart: 17, of which 2 were waited for; matrix products, arithmetic and copies ran while one was open for 12% of the time, Pallas kernels for 26%

profile of v1, /device:TPU:29, one launch (start us, length us, event | category | flops | bytes accessed | tf_op | source)
XLA Modules:
  0.0 386.5 jit_solution(4503525298998507654)
XLA Ops:
  0.0 5.9 %convolution_convert_fusion.1 = bf16[256,8,2048]{2,0,1:T(8,128)(2,1)S(1)} fusion(bf16[8,256,2048]{2,1,0:T(8,128)(2,1)} %bitcast.26, s32[256]{0:T(256)S(1)} %fusion.19), kind=kOutput, calls=%fused_computation.11 | convolution fusion | flops 2151743488 | bytes 16778240 | tf_op jit(solution)/shard_map/pq,cqd->cpd/dot_general | solution.py:305
  5.9 0.0 copy-start
  5.9 3.4 copy-done
  9.3 0.0 copy-done.3
  9.3 21.3 %convert_bitcast_fusion.1.refs_0_.k_ref = bf16[8,2048,256]{2,1,0:T(8,128)(2,1)} fusion(bf16[2048,2048,1]{1,0,2:T(8,128)(2,1)S(1)} %bitcast.27, bf16[2048,8,256]{2,1,0:T(8,128)(2,1)S(1)} %copy-done.3), kind=kOutput, calls=%fused_computation.9 | convolution fusion | flops 17184063488 | bytes 25165824 | tf_op jit(solution)/shard_map/td,dhe->hte/dot_general | solution.py:309
  30.7 8.6 %pack.3 = (bf16[8,256,256]{2,1,0:T(8,128)(2,1)}, bf16[8,512,256]{2,1,0:T(8,128)(2,1)}, bf16[8,1024,256]{2,1,0:T(8,128)(2,1)}) custom-call(bf16[8,2048,256]{2,1,0:T(8,128)(2,1)} %convert_bitcast_fusion.1.refs_0_.k_ref), custom_call_target="tpu_custom_call" | custom-call | flops 100000000 | bytes 16777216 | tf_op jit(solution)/shard_map/pack/pallas_call | solution.py:65
  39.2 0.7 collective-permute-start.7
  40.0 1.7 collective-permute-start.8
  41.7 23.4 %fusion.q_ref.refs_0_ = bf16[8,2048,256]{2,1,0:T(8,128)(2,1)} fusion(bf16[2048,2048,1]{1,0,2:T(8,128)(2,1)} %bitcast.28, bf16[2048,8,256]{2,1,0:T(8,128)(2,1)} %param.6), kind=kOutput, calls=%fused_computation.1 | convolution fusion | flops 17188257792 | bytes 25165824 | tf_op jit(solution)/shard_map/td,dhe->hte/dot_general | solution.py:309
  65.1 6.7 %pack.5.qa_ref = bf16[8,256,256]{2,1,0:T(8,128)(2,1)} custom-call(bf16[8,2048,256]{2,1,0:T(8,128)(2,1)} %fusion.q_ref.refs_0_), custom_call_target="tpu_custom_call" | custom-call | flops 100000000 | bytes 16777216 | tf_op jit(solution)/shard_map/pack/pallas_call | solution.py:65
  71.8 2.5 collective-permute-start.6
  74.3 23.4 %convert_bitcast_fusion.refs_0_.v_ref = bf16[8,2048,256]{2,1,0:T(8,128)(2,1)} fusion(bf16[2048,2048,1]{1,0,2:T(8,128)(2,1)} %bitcast.29, bf16[2048,8,256]{2,1,0:T(8,128)(2,1)} %param.8), kind=kOutput, calls=%fused_computation.8 | convolution fusion | flops 17184063488 | bytes 25165824 | tf_op jit(solution)/shard_map/td,dhe->hte/dot_general | solution.py:309
  97.7 8.6 %pack.4 = (bf16[8,256,256]{2,1,0:T(8,128)(2,1)}, bf16[8,512,256]{2,1,0:T(8,128)(2,1)}, bf16[8,1024,256]{2,1,0:T(8,128)(2,1)}) custom-call(bf16[8,2048,256]{2,1,0:T(8,128)(2,1)} %convert_bitcast_fusion.refs_0_.v_ref), custom_call_target="tpu_custom_call" | custom-call | flops 100000000 | bytes 16777216 | tf_op jit(solution)/shard_map/pack/pallas_call | solution.py:65
  106.2 0.7 collective-permute-start.11
  107.0 1.3 collective-permute-start
  108.3 0.0 collective-permute-done.6.qb_ref
  108.3 0.0 copy-start.5
  108.3 1.3 collective-permute-start.1
  109.6 0.0 collective-permute-done.7.refs_0_
  109.6 0.0 copy-start.4
  109.6 1.7 collective-permute-start.12
  111.3 0.0 collective-permute-done.8.refs_1_
  111.3 0.7 collective-permute-start.9
  112.0 0.0 collective-permute-done.11.refs_4_
  112.0 0.0 copy-start.6
  112.0 0.7 collective-permute-start.10
  112.8 0.0 collective-permute-done.12.refs_5_
  112.8 0.7 collective-permute-start.13
  113.5 0.0 collective-permute-done.9.refs_2_
  113.5 0.0 copy-done.5
  113.5 0.0 copy-start.7
  113.5 1.0 copy-done.7
  114.6 0.0 copy-done.6
  114.6 1.3 collective-permute-start.2
  115.8 0.0 collective-permute-done.10.refs_3_
  115.9 0.0 copy-start.8
  115.9 1.3 collective-permute-start.4
  117.2 0.0 collective-permute-done.13.refs_6_
  117.2 0.0 copy-done.8
  117.2 0.0 copy-start.9
  117.2 1.7 collective-permute-start.14
  118.9 0.0 copy-done.9
  118.9 0.6 pad_add_fusion.flag_ref
  119.5 0.0 collective-permute-done.14.refs_7_
  119.5 0.0 copy-done.4
  119.5 8.5 %far_attention.1 = (f32[8,256,256]{2,1,0:T(8,128)}, f32[8,8,256]{2,1,0:T(8,128)}, f32[8,256,256]{2,1,0:T(8,128)}, f32[8,8,256]{2,1,0:T(8,128)}) custom-call(s32[4]{0:T(128)} %pad_add_fusion.flag_ref, bf16[8,256,256]{2,1,0:T(8,128)(2,1)} %pack.5.qa_ref, bf16[8,256,256]{2,1,0:T(8,128)(2,1)} %copy-done.5, bf16[8,256,256]{2,1,0:T(8,128)(2,1)} %copy-done.4, ...), custom_call_target="tpu_custom_call" | custom-call | flops 5000000000 | bytes 20000000 | tf_op jit(solution)/shard_map/far_attention/pallas_call | solution.py:195
  128.0 1.3 collective-permute-start.15
  129.3 77.8 %collective-permute-done.2.k0_ref = bf16[8,512,256]{2,1,0:T(8,128)(2,1)S(1)} collective-permute-done((bf16[8,512,256]{2,1,0:T(8,128)(2,1)}, bf16[8,512,256]{2,1,0:T(8,128)(2,1)S(1)}, u32[]{:S(2)}, u32[]{:S(2)}) %collective-permute-start.2) | collective-permute-done | bytes 2097184 | tf_op jit(solution)/shard_map/ppermute | solution.py:294
  207.1 1.3 collective-permute-start.16
  208.4 43.8 %collective-permute-done.4.v0_ref = bf16[8,512,256]{2,1,0:T(8,128)(2,1)} collective-permute-done((bf16[8,512,256]{2,1,0:T(8,128)(2,1)}, bf16[8,512,256]{2,1,0:T(8,128)(2,1)}, u32[]{:S(2)}, u32[]{:S(2)}) %collective-permute-start.4) | collective-permute-done | bytes 2097184 | tf_op jit(solution)/shard_map/ppermute | solution.py:294
  252.2 2.7 collective-permute-start.3
  254.9 0.0 collective-permute-done.pk_ref
  254.9 2.1 collective-permute-start.5
  257.0 0.0 collective-permute-done.1.pv_ref
  257.0 75.5 %local_attention.1 = (f32[8,2048,256]{2,1,0:T(8,128)}, f32[8,2048,128]{2,1,0:T(8,128)}) custom-call(s32[4]{0:T(128)} %pad_add_fusion.flag_ref, bf16[8,2048,256]{2,1,0:T(8,128)(2,1)} %fusion.q_ref.refs_0_, bf16[8,2048,256]{2,1,0:T(8,128)(2,1)} %convert_bitcast_fusion.1.refs_0_.k_ref, bf16[8,2048,256]{2,1,0:T(8,128)(2,1)} %convert_bitcast_fusion.refs_0_.v_ref, ...), custom_call_target="tpu_custom_call" | custom-call | flops 40000000000 | bytes 60000000 | tf_op jit(solution)/shard_map/local_attention/pallas_call | solution.py:155
  332.5 0.0 copy-done.1
  332.5 0.0 collective-permute-done.16.fl1_ref
  332.5 0.0 copy-start.2
  332.6 0.0 collective-permute-done.3.k1_ref
  332.6 0.0 collective-permute-done.5.v1_ref
  332.6 0.0 collective-permute-done.15.fo1_ref
  332.6 0.6 copy-done.2
  333.2 29.5 %final_attention.1 = bf16[2048,2048]{1,0:T(8,128)(2,1)} custom-call(s32[4]{0:T(128)} %pad_add_fusion.flag_ref, bf16[8,2048,256]{2,1,0:T(8,128)(2,1)} %fusion.q_ref.refs_0_, f32[8,2048,256]{2,1,0:T(8,128)} %get-tuple-element.19.o_in_ref, f32[8,2048,128]{2,1,0:T(8,128)} %get-tuple-element.20.lse_in_ref, bf16[8,512,256]{2,1,0:T(8,128)(2,1)} %copy-done.1, ...), custom_call_target="tpu_custom_call" | custom-call | flops 8000000000 | bytes 60000000 | tf_op jit(solution)/shard_map/final_attention/pallas_call | solution.py:266
  362.7 23.8 %convolution_convert_fusion = bf16[2048,2048]{1,0:T(8,128)(2,1)} fusion(bf16[2048,2048]{1,0:T(8,128)(2,1)} %final_attention.1, bf16[2048,2048]{1,0:T(8,128)(2,1)} %bitcast.30), kind=kOutput, calls=%fused_computation.10 | convolution fusion | flops 17184063488 | bytes 25165824 | tf_op jit(solution)/shard_map/dot_general | solution.py:332
  (3 shorter events, 0.0 us)
Async XLA Ops:
  0.0 9.3 %copy-start.3 = (bf16[2048,8,256]{2,1,0:T(8,128)(2,1)S(1)}, bf16[2048,8,256]{2,1,0:T(8,128)(2,1)}, u32[]{:S(2)}) copy-start(bf16[2048,8,256]{2,1,0:T(8,128)(2,1)} %param.7) | copy-start | bytes 25165828
  5.9 3.4 copy-start
  39.2 70.3 %collective-permute-start.7 = (bf16[8,256,256]{2,1,0:T(8,128)(2,1)}, bf16[8,256,256]{2,1,0:T(8,128)(2,1)S(1)}, u32[]{:S(2)}, u32[]{:S(2)}) collective-permute-start(bf16[8,256,256]{2,1,0:T(8,128)(2,1)} %get-tuple-element.23), channel_id=1, source_target_pairs={{0,4},{1,5},{8,12},{9,13},{16,20},{17,21},{24,28},{25,29}} | collective-permute-start | bytes 3145736 | tf_op jit(solution)/shard_map/ppermute | solution.py:294
  40.0 71.3 %collective-permute-start.8 = (bf16[8,256,256]{2,1,0:T(8,128)(2,1)}, bf16[8,256,256]{2,1,0:T(8,128)(2,1)}, u32[]{:S(2)}, u32[]{:S(2)}) collective-permute-start(bf16[8,256,256]{2,1,0:T(8,128)(2,1)} %get-tuple-element.23), channel_id=1, source_target_pairs={{2,4},{3,5},{10,12},{11,13},{18,20},{19,21},{26,28},{27,29}} | collective-permute-start | bytes 3145736 | tf_op jit(solution)/shard_map/ppermute | solution.py:294
  71.8 36.5 %collective-permute-start.6 = (bf16[8,256,256]{2,1,0:T(8,128)(2,1)}, bf16[8,256,256]{2,1,0:T(8,128)(2,1)S(1)}, u32[]{:S(2)}, u32[]{:S(2)}) collective-permute-start(bf16[8,256,256]{2,1,0:T(8,128)(2,1)} %pack.5.qa_ref), channel_id=1, source_target_pairs={{6,4},{7,5},{14,12},{15,13},{22,20},{23,21},{30,28},{31,29}} | collective-permute-start | bytes 3145736 | tf_op jit(solution)/shard_map/ppermute | solution.py:294
  106.2 5.8 %collective-permute-start.11 = (bf16[8,256,256]{2,1,0:T(8,128)(2,1)}, bf16[8,256,256]{2,1,0:T(8,128)(2,1)S(1)}, u32[]{:S(2)}, u32[]{:S(2)}) collective-permute-start(bf16[8,256,256]{2,1,0:T(8,128)(2,1)} %get-tuple-element.24), channel_id=1, source_target_pairs={{0,4},{1,5},{8,12},{9,13},{16,20},{17,21},{24,28},{25,29}} | collective-permute-start | bytes 3145736 | tf_op jit(solution)/shard_map/ppermute | solution.py:294
  107.0 147.9 %collective-permute-start = (bf16[8,1024,256]{2,1,0:T(8,128)(2,1)}, bf16[8,1024,256]{2,1,0:T(8,128)(2,1)}, u32[]{:S(2)}, u32[]{:S(2)}) collective-permute-start(bf16[8,1024,256]{2,1,0:T(8,128)(2,1)} %get-tuple-element.17), channel_id=1, source_target_pairs={{0,1},{2,3},{4,5},{6,7},{8,9},{10,11},{12,13},{14,15},{16,17},{18,... | collective-permute-start | bytes 12582920 | tf_op jit(solution)/shard_map/ppermute | solution.py:294
  108.3 5.3 %copy-start.5 = (bf16[8,256,256]{2,1,0:T(8,128)(2,1)}, bf16[8,256,256]{2,1,0:T(8,128)(2,1)S(1)}, u32[]{:S(2)}) copy-start(bf16[8,256,256]{2,1,0:T(8,128)(2,1)S(1)} %collective-permute-done.6.qb_ref) | copy-start | bytes 3145732
  108.3 148.7 %collective-permute-start.1 = (bf16[8,1024,256]{2,1,0:T(8,128)(2,1)}, bf16[8,1024,256]{2,1,0:T(8,128)(2,1)}, u32[]{:S(2)}, u32[]{:S(2)}) collective-permute-start(bf16[8,1024,256]{2,1,0:T(8,128)(2,1)} %get-tuple-element.18), channel_id=1, source_target_pairs={{0,1},{2,3},{4,5},{6,7},{8,9},{10,11},{12,13},{14,15},{16,17},{18,... | collective-permute-start | bytes 12582920 | tf_op jit(solution)/shard_map/ppermute | solution.py:294
  109.6 9.9 %copy-start.4 = (bf16[8,256,256]{2,1,0:T(8,128)(2,1)}, bf16[8,256,256]{2,1,0:T(8,128)(2,1)S(1)}, u32[]{:S(2)}) copy-start(bf16[8,256,256]{2,1,0:T(8,128)(2,1)S(1)} %collective-permute-done.7.refs_0_) | copy-start | bytes 3145732
  109.6 3.2 collective-permute-start.12
  111.3 2.2 collective-permute-start.9
  112.0 2.5 copy-start.6
  112.0 3.8 collective-permute-start.10
  112.8 4.4 %collective-permute-start.13 = (bf16[8,256,256]{2,1,0:T(8,128)(2,1)S(1)}, bf16[8,256,256]{2,1,0:T(8,128)(2,1)S(1)}, u32[]{:S(2)}, u32[]{:S(2)}) collective-permute-start(bf16[8,256,256]{2,1,0:T(8,128)(2,1)S(1)} %collective-permute-done.11.refs_4_), channel_id=1, source_target_pairs={{4,5},{5,4},{12,13},{13,12},{20,21},{21,20},{28,29},{29,28}} | collective-permute-start | bytes 3145736 | tf_op jit(solution)/shard_map/ppermute | solution.py:294
  113.5 1.0 copy-start.7
  114.6 92.6 %collective-permute-start.2 = (bf16[8,512,256]{2,1,0:T(8,128)(2,1)}, bf16[8,512,256]{2,1,0:T(8,128)(2,1)S(1)}, u32[]{:S(2)}, u32[]{:S(2)}) collective-permute-start(bf16[8,512,256]{2,1,0:T(8,128)(2,1)} %get-tuple-element.21), channel_id=1, source_target_pairs={{0,2},{1,3},{4,6},{5,7},{8,10},{9,11},{12,14},{13,15},{16,18},{17,... | collective-permute-start | bytes 6291464 | tf_op jit(solution)/shard_map/ppermute | solution.py:294
  115.9 1.3 copy-start.8
  115.9 136.3 %collective-permute-start.4 = (bf16[8,512,256]{2,1,0:T(8,128)(2,1)}, bf16[8,512,256]{2,1,0:T(8,128)(2,1)}, u32[]{:S(2)}, u32[]{:S(2)}) collective-permute-start(bf16[8,512,256]{2,1,0:T(8,128)(2,1)} %get-tuple-element.22), channel_id=1, source_target_pairs={{0,2},{1,3},{4,6},{5,7},{8,10},{9,11},{12,14},{13,15},{16,18},{17,... | collective-permute-start | bytes 6291464 | tf_op jit(solution)/shard_map/ppermute | solution.py:294
  117.2 1.7 copy-start.9
  117.2 2.3 collective-permute-start.14
  128.0 204.5 %collective-permute-start.15 = (f32[8,256,256]{2,1,0:T(8,128)}, f32[8,256,256]{2,1,0:T(8,128)}, u32[]{:S(2)}, u32[]{:S(2)}) collective-permute-start(f32[8,256,256]{2,1,0:T(8,128)} %get-tuple-element.27), channel_id=1, source_target_pairs={{4,6},{5,7},{12,14},{13,15},{20,22},{21,23},{28,30},{29,31}} | collective-permute-start | bytes 6291464 | tf_op jit(solution)/shard_map/ppermute | solution.py:294
  207.1 125.4 %copy-start.1 = (bf16[8,512,256]{2,1,0:T(8,128)(2,1)}, bf16[8,512,256]{2,1,0:T(8,128)(2,1)S(1)}, u32[]{:S(2)}) copy-start(bf16[8,512,256]{2,1,0:T(8,128)(2,1)S(1)} %collective-permute-done.2.k0_ref) | copy-start | bytes 6291460
  207.1 125.4 %collective-permute-start.16 = (f32[8,8,256]{2,1,0:T(8,128)}, f32[8,8,256]{2,1,0:T(8,128)S(1)}, u32[]{:S(2)}, u32[]{:S(2)}) collective-permute-start(f32[8,8,256]{2,1,0:T(8,128)} %get-tuple-element.28), channel_id=1, source_target_pairs={{4,6},{5,7},{12,14},{13,15},{20,22},{21,23},{28,30},{29,31}} | collective-permute-start | bytes 196616 | tf_op jit(solution)/shard_map/ppermute | solution.py:294
  252.2 80.4 %collective-permute-start.3 = (bf16[8,512,256]{2,1,0:T(8,128)(2,1)S(1)}, bf16[8,512,256]{2,1,0:T(8,128)(2,1)}, u32[]{:S(2)}, u32[]{:S(2)}) collective-permute-start(bf16[8,512,256]{2,1,0:T(8,128)(2,1)S(1)} %collective-permute-done.2.k0_ref), channel_id=1, source_target_pairs={{2,3},{3,2},{6,7},{7,6},{10,11},{11,10},{14,15},{15,14},{18,19},{1... | collective-permute-start | bytes 6291464 | tf_op jit(solution)/shard_map/ppermute | solution.py:294
  254.9 77.7 %collective-permute-start.5 = (bf16[8,512,256]{2,1,0:T(8,128)(2,1)}, bf16[8,512,256]{2,1,0:T(8,128)(2,1)}, u32[]{:S(2)}, u32[]{:S(2)}) collective-permute-start(bf16[8,512,256]{2,1,0:T(8,128)(2,1)} %collective-permute-done.4.v0_ref), channel_id=1, source_target_pairs={{2,3},{3,2},{6,7},{7,6},{10,11},{11,10},{14,15},{15,14},{18,19},{1... | collective-permute-start | bytes 6291464 | tf_op jit(solution)/shard_map/ppermute | solution.py:294
  332.5 0.6 copy-start.2

commit v2 on v1

v2 whole, which is shorter than its diff:
```python
import math
import jax
import jax.numpy as jnp
from jax import lax
from jax.experimental import pallas as pl
from jax.experimental.pallas import tpu as pltpu
from jax.sharding import PartitionSpec as P

CHUNK = 256
CLASSES = 8
RUN = CHUNK // CLASSES
LOG2E = math.log2(math.e)
F32 = jnp.float32
BF16 = jnp.bfloat16
VMEM_LIMIT = 60 * 1024 * 1024


def params():
    return pltpu.CompilerParams(vmem_limit_bytes=VMEM_LIMIT, dimension_semantics=("arbitrary",))


def dot_nt(a, b):
    return lax.dot_general(a, b, (((1,), (1,)), ((), ())), preferred_element_type=F32)


def dot_nn(a, b):
    return lax.dot_general(a, b, (((1,), (0,)), ((), ())), preferred_element_type=F32)


def class_of_group(head, group):
    return head ^ (0, 4, 2, 6)[group]


def run_rows(chunk, cls):
    return pl.ds(pl.multiple_of(chunk * CHUNK + cls * RUN, RUN), RUN)


def gather_class(ref, cls, n_chunks):
    return jnp.concatenate([ref[0, run_rows(i, cls), :] for i in range(n_chunks)], axis=0)


def gather_tile(ref, pair, classes):
    return jnp.concatenate([ref[0, run_rows(2 * pair + b, cls), :] for cls in classes for b in range(2)], axis=0)


def lane_class(lane):
    group = lane // (2 * RUN)
    return (group % 2) * 4 + (group // 2) * 2


def lane_position(lane, first_class):
    return (lane // RUN) % 2 * CHUNK + lane % RUN * CLASSES + (lane_class(lane) ^ first_class)


def fold_rows(x, op):
    while x.shape[0] > 8:
        half = x.shape[0] // 2
        x = op(x[:half], x[half:])
    return x


def pack_kernel(n_groups, src_ref, *out_refs):
    head = pl.program_id(0)
    n_chunks = src_ref.shape[1] // CHUNK
    rows = n_chunks * RUN
    for group in range(n_groups):
        cls = class_of_group(head, group)
        block = gather_class(src_ref, cls, n_chunks)
        for out_ref in out_refs:
            if out_ref.shape[1] > group * rows:
                out_ref[0, group * rows:(group + 1) * rows, :] = block


def pack_query_kernel(src_ref, far_ref, late_ref):
    head = pl.program_id(0)
    far_ref[0] = gather_class(src_ref, head, src_ref.shape[1] // CHUNK)
    late = [gather_tile(src_ref, pair, [class_of_group(head, g) for g in range(2)]) for pair in range(src_ref.shape[1] // (2 * CHUNK))]
    late_ref[0] = jnp.concatenate(late, axis=0)


def pack_query(src):
    num_heads, tokens, width = src.shape
    shapes = [(num_heads, tokens // CLASSES, width), (num_heads, tokens // 4, width)]
    spec = lambda shape: pl.BlockSpec((1,) + shape[1:], lambda h: (h, 0, 0))
    return pl.pallas_call(
        pack_query_kernel,
        grid=(num_heads,),
        out_shape=[jax.ShapeDtypeStruct(s, BF16) for s in shapes],
        in_specs=[spec(src.shape)],
        out_specs=[spec(s) for s in shapes],
        compiler_params=params(),
        cost_estimate=pl.CostEstimate(flops=10 ** 8, bytes_accessed=3 * src.size, transcendentals=0),
        name="pack_query",
    )(src)


def pack(src, group_counts):
    num_heads, tokens, width = src.shape
    rows = tokens // CLASSES
    shapes = [(num_heads, rows * count, width) for count in group_counts]
    spec = lambda shape: pl.BlockSpec((1,) + shape[1:], lambda h: (h, 0, 0))
    return pl.pallas_call(
        lambda *refs: pack_kernel(max(group_counts), *refs),
        grid=(num_heads,),
        out_shape=[jax.ShapeDtypeStruct(s, BF16) for s in shapes],
        in_specs=[spec(src.shape)],
        out_specs=[spec(s) for s in shapes],
        compiler_params=params(),
        cost_estimate=pl.CostEstimate(flops=10 ** 8, bytes_accessed=2 * src.size * 2, transcendentals=0),
        name="pack",
    )(src)


def head_spec(shape, first=0, last=None):
    if last is None:
        return pl.BlockSpec((1,) + shape[1:], lambda h, flags: (h + first, 0, 0))
    return pl.BlockSpec((1,) + shape[1:], lambda h, flags: (jnp.minimum(h, last), 0, 0))


def local_kernel(first_head, flag_ref, q_ref, k_ref, v_ref, pk_ref, pv_ref, *refs):
    ot_ref, st_ref, lse_ref, vt_ref, s_ref = refs[-5:]
    head = pl.program_id(0) + first_head
    tokens = q_ref.shape[1]
    n_pairs = tokens // (2 * CHUNK)
    vt_ref[:, :tokens] = jnp.transpose(v_ref[0])
    vt_ref[:, tokens:] = jnp.transpose(pv_ref[0])

    lane = lax.broadcasted_iota(jnp.int32, (8, CHUNK), 1)
    row = lax.broadcasted_iota(jnp.int32, (8, CHUNK), 0)
    both = (row ^ head) | lane_class(lane)
    log_mult = jnp.where(both == 0, 2.0, jnp.where(both % 4 == 0, math.log2(3.0), jnp.where(both % 2 == 0, 1.0, 0.0)))
    both = lane_class(row * 2 * RUN) | lane_class(lane)
    log_mult_pair = jnp.where(both == 0, math.log2(3.0), jnp.where(both % 4 == 0, 1.0, 0.0))
    log_mult_pair = jnp.where(flag_ref[0] == 1, log_mult_pair, -jnp.inf)
    row_run = lax.broadcasted_iota(jnp.int32, (RUN, CHUNK), 0) * CLASSES
    lane_run = lax.broadcasted_iota(jnp.int32, (RUN, CHUNK), 1)

    def scores(tile):
        matched, pair, slot = tile
        first = head if matched else head ^ 1
        q = gather_tile(q_ref, pair, [class_of_group(first, g) for g in range(4)])
        limit = lane_position(lane_run, first) - row_run
        m = jnp.full((8, CHUNK), -jnp.inf, F32)
        for j in range(2 * pair + 2):
            s = dot_nt(k_ref[0, j * CHUNK:(j + 1) * CHUNK, :], q)
            for r in range(CLASSES):
                part = s[r * RUN:(r + 1) * RUN, :] * LOG2E
                if matched:
                    part = part + log_mult[r:r + 1, :]
                if j >= 2 * pair:
                    part = jnp.where(limit >= (j - 2 * pair) * CHUNK + r, part, -jnp.inf)
                s_ref[slot, j * CHUNK + r * RUN:j * CHUNK + (r + 1) * RUN, :] = part
                m = jnp.maximum(m, fold_rows(part, jnp.maximum))
        if matched:
            for g in range(4):
                s = dot_nt(pk_ref[0, g * CHUNK:(g + 1) * CHUNK, :], q) * LOG2E + log_mult_pair[g:g + 1, :]
                s_ref[slot, tokens + g * CHUNK:tokens + (g + 1) * CHUNK, :] = s
                m = jnp.maximum(m, fold_rows(s, jnp.maximum))
        return jnp.max(m, axis=0, keepdims=True)

    def values(tile, m):
        matched, pair, slot = tile
        starts = [j * CHUNK for j in range(2 * pair + 2)] + ([tokens + g * CHUNK for g in range(4)] if matched else [])
        total = jnp.zeros((8, CHUNK), F32)
        acc = None
        for start in starts:
            p = jnp.exp2(s_ref[slot, start:start + CHUNK, :] - m)
            total = total + fold_rows(p, jnp.add)
            part = dot_nn(vt_ref[:, start:start + CHUNK], p.astype(BF16))
            acc = part if acc is None else acc + part
        l = jnp.sum(total, axis=0, keepdims=True)
        out = acc * (1.0 / l)
        lanes = (2 * pair + (0 if matched else 1)) * CHUNK
        ot_ref[0, :, lanes:lanes + CHUNK] = out.astype(BF16)
        if matched:
            st_ref[0, :, pair * 128:(pair + 1) * 128] = out[:, :128]
            lse_ref[0, :, pair * 128:(pair + 1) * 128] = jnp.broadcast_to((m + jnp.log2(l))[:, :128], (8, 128))

    tiles = [(matched, pair) for pair in range(n_pairs) for matched in (True, False)]
    tiles = [(matched, pair, n % 2) for n, (matched, pair) in enumerate(tiles)]
    m = scores(tiles[0])
    for tile, following in zip(tiles, tiles[1:] + [None]):
        m_following = None if following is None else scores(following)
        values(tile, m)
        m = m_following


def local_attention(flags, q, k, v, pair_k, pair_v, first_head, count, previous, after):
    num_heads, tokens, width = q.shape
    shapes = [jax.ShapeDtypeStruct((num_heads, width, tokens), BF16),
              jax.ShapeDtypeStruct((num_heads, width, tokens // 4), F32),
              jax.ShapeDtypeStruct((num_heads, 8, tokens // 4), F32)]
    ins = (q, k, v, pair_k, pair_v)
    extra = tuple(previous) + tuple(after)
    return pl.pallas_call(
        lambda *refs: local_kernel(first_head, *refs),
        grid_spec=pltpu.PrefetchScalarGridSpec(
            num_scalar_prefetch=1,
            grid=(count,),
            in_specs=[head_spec(a.shape, first_head) for a in ins] + [pl.BlockSpec(memory_space=pl.ANY)] * len(extra),
            out_specs=[head_spec(s.shape, first_head) for s in shapes],
            scratch_shapes=[pltpu.VMEM((width, tokens + pair_k.shape[1]), BF16),
                            pltpu.VMEM((2, tokens + pair_k.shape[1], CHUNK), F32)],
        ),
        out_shape=shapes,
        input_output_aliases={len(ins) + 1 + n: n for n in range(len(previous))},
        compiler_params=params(),
        cost_estimate=pl.CostEstimate(flops=count * 5 * 10 ** 9, bytes_accessed=count * 10 ** 7, transcendentals=count * 4 * 10 ** 6),
        name="local_attention",
    )(flags, *ins, *extra)


def far_kernel(flag_ref, qa_ref, qb_ref, *refs):
    keys, values, outs = refs[:4], refs[4:8], refs[-4:]
    turned = [jnp.transpose(v_ref[0]) for v_ref in values]
    for side, q_ref in enumerate((qa_ref, qb_ref)):
        scores = [dot_nt(k_ref[0], q_ref[0]) * LOG2E for k_ref in keys]
        m = fold_rows(scores[0], jnp.maximum)
        for s in scores[1:]:
            m = jnp.maximum(m, fold_rows(s, jnp.maximum))
        m = jnp.max(m, axis=0, keepdims=True)
        total = jnp.zeros((8, CHUNK), F32)
        acc = None
        for s, vt in zip(scores, turned):
            p = jnp.exp2(s - m)
            total = total + fold_rows(p, jnp.add)
            part = dot_nn(vt, p.astype(BF16))
            acc = part if acc is None else acc + part
        l = jnp.sum(total, axis=0, keepdims=True)
        outs[2 * side][0] = acc * (1.0 / l)
        outs[2 * side + 1][0] = jnp.broadcast_to(m + jnp.log2(l), (8, CHUNK))


def far_attention(flags, q_own, q_later, keys, values, after):
    num_heads, rows, width = q_own.shape
    shapes = [jax.ShapeDtypeStruct((num_heads, width, rows), F32), jax.ShapeDtypeStruct((num_heads, 8, rows), F32)] * 2
    ins = (q_own, q_later, *keys, *values)
    return pl.pallas_call(
        far_kernel,
        grid_spec=pltpu.PrefetchScalarGridSpec(
            num_scalar_prefetch=1,
            grid=(num_heads,),
            in_specs=[head_spec(a.shape) for a in ins] + [pl.BlockSpec(memory_space=pl.ANY)] * len(after),
            out_specs=[head_spec(s.shape) for s in shapes],
        ),
        out_shape=shapes,
        compiler_params=params(),
        cost_estimate=pl.CostEstimate(flops=5 * 10 ** 9, bytes_accessed=2 * 10 ** 7, transcendentals=4 * 10 ** 6),
        name="far_attention",
    )(flags, *ins, *after)


def final_kernel(num_heads, flag_ref, q_ref, ot_ref, st_ref, lse_ref, k0_ref, k1_ref, v0_ref, v1_ref,
                 fo0_ref, fl0_ref, fo1_ref, fl1_ref, wo_ref, y_ref, o_ref):
    step = pl.program_id(0)

    @pl.when(step < num_heads)
    def _():
        head = step
        lane = lax.broadcasted_iota(jnp.int32, (8, CHUNK), 1)
        first = (lane % 128) < 64
        quad_on = jnp.where(flag_ref[1] == 1, 0.0, -jnp.inf)
        mult_a = jnp.where(first, 1.0, 0.0) + quad_on
        mult_b = jnp.zeros((8, CHUNK), F32) + quad_on
        own_on = jnp.where(flag_ref[2] == 1, 0.0, -jnp.inf)
        got_on = jnp.where(flag_ref[3] == 1, 0.0, -jnp.inf)
        far_lse = jnp.maximum(fl0_ref[0] + own_on, fl1_ref[0] + got_on)
        turned = [jnp.transpose(v_ref[0]) for v_ref in (v0_ref, v1_ref)]
        merged = []
        for half in range(2):
            lanes = slice(half * CHUNK, (half + 1) * CHUNK)
            q = q_ref[0, lanes, :]
            block = slice(half * 128, (half + 1) * 128)
            far = jnp.where(flag_ref[2] == 1, fo0_ref[0, :, block], fo1_ref[0, :, block])
            far = jnp.concatenate([far, pltpu.roll(far, 64, 1)], axis=1)
            f_lse = far_lse[:, block]
            f_lse = jnp.where(first, jnp.concatenate([f_lse, pltpu.roll(f_lse, 64, 1)], axis=1), -jnp.inf)
            lse = lse_ref[0, :, lanes]
            m = jnp.maximum(lse, f_lse)
            scores = []
            for k_ref in (k0_ref, k1_ref):
                for g, mult in enumerate((mult_a, mult_b)):
                    s = dot_nt(k_ref[0, g * CHUNK:(g + 1) * CHUNK, :], q) * LOG2E + mult[:1, :]
                    scores.append(s)
                    m = jnp.maximum(m, fold_rows(s, jnp.maximum))
            m = jnp.max(m, axis=0, keepdims=True)
            total = jnp.zeros((8, CHUNK), F32)
            acc = None
            for n, s in enumerate(scores):
                p = jnp.exp2(s - m)
                total = total + fold_rows(p, jnp.add)
                part = dot_nn(turned[n // 2][:, n % 2 * CHUNK:(n % 2 + 1) * CHUNK], p.astype(BF16))
                acc = part if acc is None else acc + part
            own_weight = jnp.exp2(lse[:1, :] - m)
            far_weight = jnp.exp2(f_lse[:1, :] - m)
            l = jnp.sum(total, axis=0, keepdims=True) + own_weight + far_weight
            out = (acc + st_ref[0, :, lanes] * own_weight + far * far_weight) * (1.0 / l)
            merged.append(out.astype(BF16))

        token = lax.broadcasted_iota(jnp.int32, (2 * CHUNK, CHUNK), 0)
        column = lax.broadcasted_iota(jnp.int32, (2 * CHUNK, CHUNK), 1)
        places = [(token == lane_position(column, c)).astype(F32).astype(BF16) for c in (head, head ^ 1)]
        for pair in range(4):
            start = 2 * pair * CHUNK
            matched = jnp.concatenate([merged[pair // 2][:, pair % 2 * 128:(pair % 2 + 1) * 128],
                                       ot_ref[0, :, start + 128:start + CHUNK]], axis=1)
            rows = dot_nt(places[0], matched) + dot_nt(places[1], ot_ref[0, :, start + CHUNK:start + 2 * CHUNK])
            columns = pl.ds(pl.multiple_of(head * CHUNK, CHUNK), CHUNK)
            o_ref[start:start + 2 * CHUNK, columns] = rows.astype(BF16)

    @pl.when(step >= num_heads)
    def _():
        y_ref[...] = dot_nn(o_ref[...], wo_ref[...]).astype(BF16)


def final_attention(flags, q, ot, st, lse, keys, values, far, w_out):
    num_heads, width, tokens = ot.shape
    d_model = w_out.shape[1]
    ins = (q, ot, st, lse, *keys, *values, *far)
    column = lambda h, flags: (0, jnp.maximum(h - num_heads, 0))
    return pl.pallas_call(
        lambda *refs: final_kernel(num_heads, *refs),
        grid_spec=pltpu.PrefetchScalarGridSpec(
            num_scalar_prefetch=1,
            grid=(num_heads + d_model // 256,),
            in_specs=[head_spec(a.shape, last=num_heads - 1) for a in ins] + [pl.BlockSpec((w_out.shape[0], 256), column)],
            out_specs=pl.BlockSpec((tokens, 256), column),
            scratch_shapes=[pltpu.VMEM((tokens, num_heads * width), BF16)],
        ),
        out_shape=jax.ShapeDtypeStruct((tokens, d_model), BF16),
        compiler_params=params(),
        cost_estimate=pl.CostEstimate(flops=3 * 10 ** 10, bytes_accessed=6 * 10 ** 7, transcendentals=5 * 10 ** 6),
        name="final_attention",
    )(flags, *ins, w_out)


def solution(mesh):
    row_spec = P(('dp', 'seq'), None)
    pair_up = [(s, s + 1) for s in (0, 2, 4, 6)]
    next_chip = [(0, 2), (1, 3), (4, 6), (5, 7)]
    swap_upper = [(s, s ^ 1) for s in (2, 3, 6, 7)]
    from_first = [(0, 4), (1, 5)]
    from_second = [(2, 4), (3, 5)]
    swap_third = [(4, 5), (5, 4)]
    to_third = [(6, 4), (7, 5)]
    to_fourth = [(4, 6), (5, 7)]

    def send(array, pairs):
        return lax.ppermute(array, 'seq', pairs)

    def layer(hidden, w_query, w_key, w_value, w_out):
        tokens, d_model = hidden.shape
        num_heads, head_dim = w_query.shape[1:]
        index = lax.axis_index('seq')
        chip = index // 2
        flags = jnp.stack([index % 2, chip % 2, (chip == 2).astype(jnp.int32), (chip == 3).astype(jnp.int32)]).astype(jnp.int32)

        order = jnp.arange(CHUNK)
        perm = ((order % RUN) * CLASSES + order // RUN)[:, None] == order[None, :]
        x = jnp.einsum('pq,cqd->cpd', perm.astype(BF16), hidden.reshape(tokens // CHUNK, CHUNK, d_model),
                       preferred_element_type=F32).astype(BF16).reshape(tokens, d_model)

        def project(weight):
            return jnp.einsum('td,dhe->hte', x, weight, preferred_element_type=F32)

        def spread(packs):
            far_rows, quad_rows, pair_rows = packs
            first = send(far_rows, from_first)
            second = send(far_rows, from_second)
            quad = send(quad_rows, next_chip)
            pair = send(pair_rows, pair_up)
            swapped = send(first, swap_third), send(second, swap_third)
            return pair, (quad, send(quad, swap_upper)), (first, second, *swapped)

        k = project(w_key).astype(BF16)
        pair_k, quad_k, far_k = spread(pack(k, (1, 2, 4)))
        v = project(w_value).astype(BF16)
        pair_v, quad_v, far_v = spread(pack(v, (1, 2, 4)))
        q = (project(w_query) * head_dim ** -0.5).astype(BF16)
        q_far, q_late = pack_query(q)
        q_later = send(q_far, to_third)

        half = num_heads // 2
        state = local_attention(flags, q, k, v, pair_k, pair_v, 0, half, (), ())
        own_o, own_lse, later_o, later_lse = far_attention(flags, q_far, q_later, far_k, far_v, (state[2],))
        got_o, got_lse = send(later_o, to_fourth), send(later_lse, to_fourth)
        ot, st, lse = local_attention(flags, q, k, v, pair_k, pair_v, half, half, state, (own_lse,))
        return final_attention(flags, q_late, ot, st, lse, quad_k, quad_v, (own_o, own_lse, got_o, got_lse),
                               w_out.reshape(num_heads * head_dim, d_model))

    return jax.shard_map(layer, mesh=mesh, in_specs=(row_spec, P(), P(), P(), P()), out_specs=row_spec, check_vma=False)
```

time: 388 us -> 383 us (0.987)
  the two profiles are of different devices: /device:TPU:29 before, /device:TPU:28 now
where the time goes in v2:
time: 383 us; the launch traced here: 381 us
  waiting for transfers between devices  138 us (36%)
  Pallas kernels  134 us (35%)
  matrix products  74.1 us (19%)
  starting transfers between devices  30 us (8%)
  local copies, waits for them, and re-layouts  5.01 us (1%)
    ppermute x17, waiting for transfers between devices, send(): return lax.ppermute(array, 'seq', pairs)  138 us
    dot_general x3, matrix products, project(): return jnp.einsum('td,dhe->hte', x, weight, preferred_element_type=F32)  68.2 us
    pallas_call x2, Pallas kernels, local_attention(): pl.pallas_call(lambda *refs: local_kernel(first_head, *refs), grid_spec=p...  56.9 us
    pallas_call x1, Pallas kernels, final_attention(): pl.pallas_call(lambda *refs: final_kernel(num_heads, *refs), grid_spec=pl...  37.8 us
    ppermute x17, starting transfers between devices, send(): return lax.ppermute(array, 'seq', pairs)  30 us
    pallas_call x2, Pallas kernels, pack(): pl.pallas_call(lambda *refs: pack_kernel(max(group_counts), *refs), grid=...  17.3 us
    pallas_call x1, Pallas kernels, far_attention(): pl.pallas_call(far_kernel, grid_spec=pltpu.PrefetchScalarGridSpec(num_sca...  14.3 us
  transfers between devices with their start and end apart: 17, of which 4 were waited for; matrix products, arithmetic and copies ran while one was open for 12% of the time, Pallas kernels for 23%

profile of v2, /device:TPU:28, one launch (start us, length us, event | category | flops | bytes accessed | tf_op | source)
XLA Modules:
  0.0 381.5 jit_solution(11566341592958680838)
XLA Ops:
  0.0 0.0 copy-start.1
  0.0 5.9 %convolution_convert_fusion = bf16[256,8,2048]{2,0,1:T(8,128)(2,1)S(1)} fusion(bf16[8,256,2048]{2,1,0:T(8,128)(2,1)} %bitcast.24, s32[256]{0:T(256)S(1)} %fusion.19), kind=kOutput, calls=%fused_computation.10 | convolution fusion | flops 2151743488 | bytes 16778240 | tf_op jit(solution)/shard_map/pq,cqd->cpd/dot_general | solution.py:360
  5.9 0.0 copy-start
  5.9 3.4 copy-done
  9.3 0.0 copy-done.1
  9.3 21.4 %convert_bitcast_fusion.1.refs_0_.refs_2_ = bf16[8,2048,256]{2,1,0:T(8,128)(2,1)} fusion(bf16[2048,2048,1]{1,0,2:T(8,128)(2,1)S(1)} %bitcast.25, bf16[2048,8,256]{2,1,0:T(8,128)(2,1)S(1)} %copy-done.1), kind=kOutput, calls=%fused_computation.9 | convolution fusion | flops 17184063488 | bytes 25165824 | tf_op jit(solution)/shard_map/td,dhe->hte/dot_general | solution.py:364
  30.7 8.7 %pack.2 = (bf16[8,256,256]{2,1,0:T(8,128)(2,1)}, bf16[8,512,256]{2,1,0:T(8,128)(2,1)}, bf16[8,1024,256]{2,1,0:T(8,128)(2,1)}) custom-call(bf16[8,2048,256]{2,1,0:T(8,128)(2,1)} %convert_bitcast_fusion.1.refs_0_.refs_2_), custom_call_target="tpu_custom_call" | custom-call | flops 100000000 | bytes 16777216 | tf_op jit(solution)/shard_map/pack/pallas_call | solution.py:102
  39.4 3.8 collective-permute-start
  43.2 23.4 %convert_bitcast_fusion.refs_0_.refs_3_ = bf16[8,2048,256]{2,1,0:T(8,128)(2,1)} fusion(bf16[2048,2048,1]{1,0,2:T(8,128)(2,1)} %bitcast.26, bf16[2048,8,256]{2,1,0:T(8,128)(2,1)} %param.8), kind=kOutput, calls=%fused_computation.8 | convolution fusion | flops 17184063488 | bytes 25165824 | tf_op jit(solution)/shard_map/td,dhe->hte/dot_general | solution.py:364
  66.5 8.6 %pack.3 = (bf16[8,256,256]{2,1,0:T(8,128)(2,1)}, bf16[8,512,256]{2,1,0:T(8,128)(2,1)}, bf16[8,1024,256]{2,1,0:T(8,128)(2,1)}) custom-call(bf16[8,2048,256]{2,1,0:T(8,128)(2,1)} %convert_bitcast_fusion.refs_0_.refs_3_), custom_call_target="tpu_custom_call" | custom-call | flops 100000000 | bytes 16777216 | tf_op jit(solution)/shard_map/pack/pallas_call | solution.py:102
  75.1 3.3 collective-permute-start.1
  78.4 23.4 %fusion.src_ref.refs_1_ = bf16[8,2048,256]{2,1,0:T(8,128)(2,1)} fusion(bf16[2048,2048,1]{1,0,2:T(8,128)(2,1)} %bitcast.27, bf16[2048,8,256]{2,1,0:T(8,128)(2,1)} %param.6), kind=kOutput, calls=%fused_computation.1 | convolution fusion | flops 17188257792 | bytes 25165824 | tf_op jit(solution)/shard_map/td,dhe->hte/dot_general | solution.py:364
  101.8 0.0 copy-start.6
  101.8 7.3 %pack_query.1 = (bf16[8,256,256]{2,1,0:T(8,128)(2,1)}, bf16[8,512,256]{2,1,0:T(8,128)(2,1)}) custom-call(bf16[8,2048,256]{2,1,0:T(8,128)(2,1)} %fusion.src_ref.refs_1_), custom_call_target="tpu_custom_call" | custom-call | flops 100000000 | bytes 12582912 | tf_op jit(solution)/shard_map/pack_query/pallas_call | solution.py:85
  109.1 2.4 collective-permute-start.2
  111.6 0.0 copy-done.6
  111.6 1.6 collective-permute-start.3
  113.2 0.7 collective-permute-start.4
  113.9 16.0 %collective-permute-done.2.qb_ref = bf16[8,256,256]{2,1,0:T(8,128)(2,1)S(1)} collective-permute-done((bf16[8,256,256]{2,1,0:T(8,128)(2,1)}, bf16[8,256,256]{2,1,0:T(8,128)(2,1)S(1)}, u32[]{:S(2)}, u32[]{:S(2)}) %collective-permute-start.2) | collective-permute-done | bytes 1048608 | tf_op jit(solution)/shard_map/ppermute | solution.py:349
  129.9 0.0 copy-start.3
  129.9 0.7 collective-permute-start.7
  130.6 0.0 collective-permute-done.3.refs_0_
  130.6 1.6 collective-permute-start.8
  132.3 0.0 collective-permute-done.4.refs_1_
  132.3 0.0 copy-start.4
  132.3 1.7 collective-permute-start.5
  133.9 0.0 collective-permute-done.7.refs_4_
  133.9 0.0 copy-done.4
  133.9 0.0 copy-start.5
  133.9 1.0 copy-done.5
  134.9 1.3 collective-permute-start.11
  136.2 0.0 collective-permute-done.8.refs_5_
  136.2 1.3 collective-permute-start.13
  137.6 0.7 pad_add_fusion.refs_0_.flag_ref
  138.2 0.0 collective-permute-done.5.refs_2_
  138.2 1.6 collective-permute-start.6
  139.9 0.0 collective-permute-done.refs_4_
  139.9 1.7 collective-permute-start.9
  141.5 0.0 collective-permute-done.1.refs_5_
  141.5 1.6 collective-permute-start.10
  143.2 28.4 %local_attention.2 = (bf16[8,256,2048]{2,1,0:T(8,128)(2,1)}, f32[8,256,512]{2,1,0:T(8,128)}, f32[8,8,512]{2,1,0:T(8,128)}) custom-call(s32[4]{0:T(128)} %pad_add_fusion.refs_0_.flag_ref, bf16[8,2048,256]{2,1,0:T(8,128)(2,1)} %fusion.src_ref.refs_1_, bf16[8,2048,256]{2,1,0:T(8,128)(2,1)} %convert_bitcast_fusion.1.refs_0_.refs_2_, ...), custom_call_target="tpu_custom_call" | custom-call | flops 20000000000 | bytes 40000000 | tf_op jit(solution)/shard_map/local_attention/pallas_call | solution.py:195
  171.6 0.0 copy-done.3
  171.6 58.6 %collective-permute-done.11.refs_5_ = bf16[8,512,256]{2,1,0:T(8,128)(2,1)S(1)} collective-permute-done((bf16[8,512,256]{2,1,0:T(8,128)(2,1)}, bf16[8,512,256]{2,1,0:T(8,128)(2,1)S(1)}, u32[]{:S(2)}, u32[]{:S(2)}) %collective-permute-start.11) | collective-permute-done | bytes 2097184 | tf_op jit(solution)/shard_map/ppermute | solution.py:349
  230.2 0.0 copy-start.2
  230.2 1.9 collective-permute-start.12
  232.1 42.9 %collective-permute-done.13.refs_7_ = bf16[8,512,256]{2,1,0:T(8,128)(2,1)} collective-permute-done((bf16[8,512,256]{2,1,0:T(8,128)(2,1)}, bf16[8,512,256]{2,1,0:T(8,128)(2,1)}, u32[]{:S(2)}, u32[]{:S(2)}) %collective-permute-start.13) | collective-permute-done | bytes 2097184 | tf_op jit(solution)/shard_map/ppermute | solution.py:349
  275.0 2.1 collective-permute-start.14
  277.2 0.0 collective-permute-done.6.refs_3_
  277.2 0.0 collective-permute-done.9.refs_6_
  277.2 0.0 collective-permute-done.10.refs_7_
  277.2 14.3 %far_attention.1 = (f32[8,256,256]{2,1,0:T(8,128)}, f32[8,8,256]{2,1,0:T(8,128)}, f32[8,256,256]{2,1,0:T(8,128)}, f32[8,8,256]{2,1,0:T(8,128)}) custom-call(s32[4]{0:T(128)} %pad_add_fusion.refs_0_.flag_ref, bf16[8,256,256]{2,1,0:T(8,128)(2,1)} %get-tuple-element.29.qa_ref, bf16[8,256,256]{2,1,0:T(8,128)(2,1)} %copy-done.3, ...), custom_call_target="tpu_custom_call" | custom-call | flops 5000000000 | bytes 20000000 | tf_op jit(solution)/shard_map/far_attention/pallas_call | solution.py:238
  291.5 0.0 copy-done.2
  291.5 1.3 collective-permute-start.15
  292.8 1.3 collective-permute-start.16
  294.1 28.5 %local_attention.3 = (bf16[8,256,2048]{2,1,0:T(8,128)(2,1)}, f32[8,256,512]{2,1,0:T(8,128)}, f32[8,8,512]{2,1,0:T(8,128)}) custom-call(s32[4]{0:T(128)} %pad_add_fusion.refs_0_.flag_ref, bf16[8,2048,256]{2,1,0:T(8,128)(2,1)} %fusion.src_ref.refs_1_, ...), custom_call_target="tpu_custom_call", output_to_operand_aliasing={{0}: (6, {}), {1}: (7, {}), {2}: (8, {})} | custom-call | flops 20000000000 | bytes 40000000 | tf_op jit(solution)/shard_map/local_attention/pallas_call | solution.py:195
  322.5 0.0 collective-permute-done.12.refs_6_
  322.6 0.0 collective-permute-done.14.refs_8_
  322.6 20.5 %collective-permute-done.16.refs_12_ = f32[8,8,256]{2,1,0:T(8,128)S(1)} collective-permute-done((f32[8,8,256]{2,1,0:T(8,128)}, f32[8,8,256]{2,1,0:T(8,128)S(1)}, u32[]{:S(2)}, u32[]{:S(2)}) %collective-permute-start.16) | collective-permute-done | bytes 65568 | tf_op jit(solution)/shard_map/ppermute | solution.py:349
  343.0 0.0 copy-start.7
  343.0 0.0 collective-permute-done.15.refs_11_
  343.0 0.6 copy-done.7
  343.6 37.8 %final_attention.1 = bf16[2048,2048]{1,0:T(8,128)(2,1)} custom-call(s32[4]{0:T(128)} %pad_add_fusion.refs_0_.flag_ref, bf16[8,512,256]{2,1,0:T(8,128)(2,1)} %get-tuple-element.23.refs_1_, bf16[8,256,2048]{2,1,0:T(8,128)(2,1)} %get-tuple-element.33.refs_2_, f32[8,256,512]{2,1,0:T(8,128)} %get-tuple-element.34.refs_3_, ...), custom_call_target="tpu_custom_call" | custom-call | flops 30000001024 | bytes 60000000 | tf_op jit(solution)/shard_map/final_attention/pallas_call | solution.py:321
  (1 shorter events, 0.0 us)
Async XLA Ops:
  0.0 9.3 %copy-start.1 = (bf16[2048,8,256]{2,1,0:T(8,128)(2,1)S(1)}, bf16[2048,8,256]{2,1,0:T(8,128)(2,1)}, u32[]{:S(2)}) copy-start(bf16[2048,8,256]{2,1,0:T(8,128)(2,1)} %param.7) | copy-start | bytes 25165828
  5.9 3.4 copy-start
  39.4 100.5 %collective-permute-start = (bf16[8,1024,256]{2,1,0:T(8,128)(2,1)}, bf16[8,1024,256]{2,1,0:T(8,128)(2,1)}, u32[]{:S(2)}, u32[]{:S(2)}) collective-permute-start(bf16[8,1024,256]{2,1,0:T(8,128)(2,1)} %get-tuple-element.24), channel_id=1, source_target_pairs={{0,1},{2,3},{4,5},{6,7},{8,9},{10,11},{12,13},{14,15},{16,17},{18,... | collective-permute-start | bytes 12582920 | tf_op jit(solution)/shard_map/ppermute | solution.py:349
  75.1 66.4 %collective-permute-start.1 = (bf16[8,1024,256]{2,1,0:T(8,128)(2,1)}, bf16[8,1024,256]{2,1,0:T(8,128)(2,1)}, u32[]{:S(2)}, u32[]{:S(2)}) collective-permute-start(bf16[8,1024,256]{2,1,0:T(8,128)(2,1)} %get-tuple-element.25), channel_id=1, source_target_pairs={{0,1},{2,3},{4,5},{6,7},{8,9},{10,11},{12,13},{14,15},{16,17},{18,... | collective-permute-start | bytes 12582920 | tf_op jit(solution)/shard_map/ppermute | solution.py:349
  101.8 9.7 %copy-start.6 = (bf16[8,256,256]{2,1,0:T(8,128)(2,1)S(1)}, bf16[8,256,256]{2,1,0:T(8,128)(2,1)}, u32[]{:S(2)}) copy-start(bf16[8,256,256]{2,1,0:T(8,128)(2,1)} %get-tuple-element.30) | copy-start | bytes 3145732
  109.1 20.8 %collective-permute-start.2 = (bf16[8,256,256]{2,1,0:T(8,128)(2,1)}, bf16[8,256,256]{2,1,0:T(8,128)(2,1)S(1)}, u32[]{:S(2)}, u32[]{:S(2)}) collective-permute-start(bf16[8,256,256]{2,1,0:T(8,128)(2,1)} %get-tuple-element.29.qa_ref), channel_id=1, source_target_pairs={{6,4},{7,5},{14,12},{15,13},{22,20},{23,21},{30,28},{31,29}} | collective-permute-start | bytes 3145736 | tf_op jit(solution)/shard_map/ppermute | solution.py:349
  111.6 19.1 %collective-permute-start.3 = (bf16[8,256,256]{2,1,0:T(8,128)(2,1)S(1)}, bf16[8,256,256]{2,1,0:T(8,128)(2,1)}, u32[]{:S(2)}, u32[]{:S(2)}) collective-permute-start(bf16[8,256,256]{2,1,0:T(8,128)(2,1)S(1)} %copy-done.6), channel_id=1, source_target_pairs={{0,4},{1,5},{8,12},{9,13},{16,20},{17,21},{24,28},{25,29}} | collective-permute-start | bytes 3145736 | tf_op jit(solution)/shard_map/ppermute | solution.py:349
  113.2 19.1 %collective-permute-start.4 = (bf16[8,256,256]{2,1,0:T(8,128)(2,1)S(1)}, bf16[8,256,256]{2,1,0:T(8,128)(2,1)S(1)}, u32[]{:S(2)}, u32[]{:S(2)}) collective-permute-start(bf16[8,256,256]{2,1,0:T(8,128)(2,1)S(1)} %copy-done.6), channel_id=1, source_target_pairs={{2,4},{3,5},{10,12},{11,13},{18,20},{19,21},{26,28},{27,29}} | collective-permute-start | bytes 3145736 | tf_op jit(solution)/shard_map/ppermute | solution.py:349
  129.9 41.7 %copy-start.3 = (bf16[8,256,256]{2,1,0:T(8,128)(2,1)}, bf16[8,256,256]{2,1,0:T(8,128)(2,1)S(1)}, u32[]{:S(2)}) copy-start(bf16[8,256,256]{2,1,0:T(8,128)(2,1)S(1)} %collective-permute-done.2.qb_ref) | copy-start | bytes 3145732
  129.9 4.0 %collective-permute-start.7 = (bf16[8,256,256]{2,1,0:T(8,128)(2,1)}, bf16[8,256,256]{2,1,0:T(8,128)(2,1)S(1)}, u32[]{:S(2)}, u32[]{:S(2)}) collective-permute-start(bf16[8,256,256]{2,1,0:T(8,128)(2,1)} %get-tuple-element.31), channel_id=1, source_target_pairs={{0,4},{1,5},{8,12},{9,13},{16,20},{17,21},{24,28},{25,29}} | collective-permute-start | bytes 3145736 | tf_op jit(solution)/shard_map/ppermute | solution.py:349
  130.6 5.6 %collective-permute-start.8 = (bf16[8,256,256]{2,1,0:T(8,128)(2,1)}, bf16[8,256,256]{2,1,0:T(8,128)(2,1)}, u32[]{:S(2)}, u32[]{:S(2)}) collective-permute-start(bf16[8,256,256]{2,1,0:T(8,128)(2,1)} %get-tuple-element.31), channel_id=1, source_target_pairs={{2,4},{3,5},{10,12},{11,13},{18,20},{19,21},{26,28},{27,29}} | collective-permute-start | bytes 3145736 | tf_op jit(solution)/shard_map/ppermute | solution.py:349
  132.3 1.7 copy-start.4
  132.3 5.9 %collective-permute-start.5 = (bf16[8,256,256]{2,1,0:T(8,128)(2,1)}, bf16[8,256,256]{2,1,0:T(8,128)(2,1)}, u32[]{:S(2)}, u32[]{:S(2)}) collective-permute-start(bf16[8,256,256]{2,1,0:T(8,128)(2,1)} %collective-permute-done.3.refs_0_), channel_id=1, source_target_pairs={{4,5},{5,4},{12,13},{13,12},{20,21},{21,20},{28,29},{29,28}} | collective-permute-start | bytes 3145736 | tf_op jit(solution)/shard_map/ppermute | solution.py:349
  133.9 1.0 copy-start.5
  134.9 95.3 %collective-permute-start.11 = (bf16[8,512,256]{2,1,0:T(8,128)(2,1)}, bf16[8,512,256]{2,1,0:T(8,128)(2,1)S(1)}, u32[]{:S(2)}, u32[]{:S(2)}) collective-permute-start(bf16[8,512,256]{2,1,0:T(8,128)(2,1)} %get-tuple-element.36), channel_id=1, source_target_pairs={{0,2},{1,3},{4,6},{5,7},{8,10},{9,11},{12,14},{13,15},{16,18},{17,... | collective-permute-start | bytes 6291464 | tf_op jit(solution)/shard_map/ppermute | solution.py:349
  136.2 138.8 %collective-permute-start.13 = (bf16[8,512,256]{2,1,0:T(8,128)(2,1)}, bf16[8,512,256]{2,1,0:T(8,128)(2,1)}, u32[]{:S(2)}, u32[]{:S(2)}) collective-permute-start(bf16[8,512,256]{2,1,0:T(8,128)(2,1)} %get-tuple-element.37), channel_id=1, source_target_pairs={{0,2},{1,3},{4,6},{5,7},{8,10},{9,11},{12,14},{13,15},{16,18},{17,... | collective-permute-start | bytes 6291464 | tf_op jit(solution)/shard_map/ppermute | solution.py:349
  138.2 139.0 %collective-permute-start.6 = (bf16[8,256,256]{2,1,0:T(8,128)(2,1)}, bf16[8,256,256]{2,1,0:T(8,128)(2,1)}, u32[]{:S(2)}, u32[]{:S(2)}) collective-permute-start(bf16[8,256,256]{2,1,0:T(8,128)(2,1)} %copy-done.4), channel_id=1, source_target_pairs={{4,5},{5,4},{12,13},{13,12},{20,21},{21,20},{28,29},{29,28}} | collective-permute-start | bytes 3145736 | tf_op jit(solution)/shard_map/ppermute | solution.py:349
  139.9 137.3 %collective-permute-start.9 = (bf16[8,256,256]{2,1,0:T(8,128)(2,1)}, bf16[8,256,256]{2,1,0:T(8,128)(2,1)}, u32[]{:S(2)}, u32[]{:S(2)}) collective-permute-start(bf16[8,256,256]{2,1,0:T(8,128)(2,1)} %copy-done.5), channel_id=1, source_target_pairs={{4,5},{5,4},{12,13},{13,12},{20,21},{21,20},{28,29},{29,28}} | collective-permute-start | bytes 3145736 | tf_op jit(solution)/shard_map/ppermute | solution.py:349
  141.5 135.7 %collective-permute-start.10 = (bf16[8,256,256]{2,1,0:T(8,128)(2,1)}, bf16[8,256,256]{2,1,0:T(8,128)(2,1)}, u32[]{:S(2)}, u32[]{:S(2)}) collective-permute-start(bf16[8,256,256]{2,1,0:T(8,128)(2,1)} %collective-permute-done.8.refs_5_), channel_id=1, source_target_pairs={{4,5},{5,4},{12,13},{13,12},{20,21},{21,20},{28,29},{29,28}} | collective-permute-start | bytes 3145736 | tf_op jit(solution)/shard_map/ppermute | solution.py:349
  230.2 61.3 %copy-start.2 = (bf16[8,512,256]{2,1,0:T(8,128)(2,1)}, bf16[8,512,256]{2,1,0:T(8,128)(2,1)S(1)}, u32[]{:S(2)}) copy-start(bf16[8,512,256]{2,1,0:T(8,128)(2,1)S(1)} %collective-permute-done.11.refs_5_) | copy-start | bytes 6291460
  230.2 92.4 %collective-permute-start.12 = (bf16[8,512,256]{2,1,0:T(8,128)(2,1)S(1)}, bf16[8,512,256]{2,1,0:T(8,128)(2,1)}, u32[]{:S(2)}, u32[]{:S(2)}) collective-permute-start(bf16[8,512,256]{2,1,0:T(8,128)(2,1)S(1)} %collective-permute-done.11.refs_5_), channel_id=1, source_target_pairs={{2,3},{3,2},{6,7},{7,6},{10,11},{11,10},{14,15},{15,14},{18,19},{1... | collective-permute-start | bytes 6291464 | tf_op jit(solution)/shard_map/ppermute | solution.py:349
  275.0 47.5 %collective-permute-start.14 = (bf16[8,512,256]{2,1,0:T(8,128)(2,1)}, bf16[8,512,256]{2,1,0:T(8,128)(2,1)}, u32[]{:S(2)}, u32[]{:S(2)}) collective-permute-start(bf16[8,512,256]{2,1,0:T(8,128)(2,1)} %collective-permute-done.13.refs_7_), channel_id=1, source_target_pairs={{2,3},{3,2},{6,7},{7,6},{10,11},{11,10},{14,15},{15,14},{18,19},{1... | collective-permute-start | bytes 6291464 | tf_op jit(solution)/shard_map/ppermute | solution.py:349
  291.5 51.5 %collective-permute-start.15 = (f32[8,256,256]{2,1,0:T(8,128)}, f32[8,256,256]{2,1,0:T(8,128)}, u32[]{:S(2)}, u32[]{:S(2)}) collective-permute-start(f32[8,256,256]{2,1,0:T(8,128)} %get-tuple-element.39), channel_id=1, source_target_pairs={{4,6},{5,7},{12,14},{13,15},{20,22},{21,23},{28,30},{29,31}} | collective-permute-start | bytes 6291464 | tf_op jit(solution)/shard_map/ppermute | solution.py:349
  292.8 50.2 %collective-permute-start.16 = (f32[8,8,256]{2,1,0:T(8,128)}, f32[8,8,256]{2,1,0:T(8,128)S(1)}, u32[]{:S(2)}, u32[]{:S(2)}) collective-permute-start(f32[8,8,256]{2,1,0:T(8,128)} %get-tuple-element.40), channel_id=1, source_target_pairs={{4,6},{5,7},{12,14},{13,15},{20,22},{21,23},{28,30},{29,31}} | collective-permute-start | bytes 196616 | tf_op jit(solution)/shard_map/ppermute | solution.py:349
  343.0 0.6 copy-start.7

commit v3 on v2

v3 whole, which is shorter than its diff:
```python
import math
import jax
import jax.numpy as jnp
from jax import lax
from jax.experimental import pallas as pl
from jax.experimental.pallas import tpu as pltpu
from jax.sharding import PartitionSpec as P

CHUNK = 256
CLASSES = 8
RUN = CHUNK // CLASSES
LOG2E = math.log2(math.e)
F32 = jnp.float32
BF16 = jnp.bfloat16
VMEM_LIMIT = 60 * 1024 * 1024


def params():
    return pltpu.CompilerParams(vmem_limit_bytes=VMEM_LIMIT, dimension_semantics=("arbitrary",))


def dot_nt(a, b):
    return lax.dot_general(a, b, (((1,), (1,)), ((), ())), preferred_element_type=F32)


def dot_nn(a, b):
    return lax.dot_general(a, b, (((1,), (0,)), ((), ())), preferred_element_type=F32)


def class_of_group(head, group):
    return head ^ (0, 4, 2, 6)[group]


def run_rows(chunk, cls):
    return pl.ds(pl.multiple_of(chunk * CHUNK + cls * RUN, RUN), RUN)


def gather_tile(ref, pair, classes):
    return jnp.concatenate([ref[0, run_rows(2 * pair + b, cls), :] for cls in classes for b in range(2)], axis=0)


def lane_class(lane):
    group = lane // (2 * RUN)
    return (group % 2) * 4 + (group // 2) * 2


def lane_position(lane, first_class):
    return (lane // RUN) % 2 * CHUNK + lane % RUN * CLASSES + (lane_class(lane) ^ first_class)


def fold_rows(x, op):
    while x.shape[0] > 8:
        half = x.shape[0] // 2
        x = op(x[:half], x[half:])
    return x


def pack_kernel(n_groups, *refs):
    src_refs, out_refs = refs[:n_groups], refs[n_groups:]
    for group, src_ref in enumerate(src_refs):
        rows = src_ref.shape[1] * RUN
        block = src_ref[...].reshape(rows, src_ref.shape[-1])
        for out_ref in out_refs:
            if out_ref.shape[1] > group * rows:
                out_ref[0, group * rows:(group + 1) * rows, :] = block


def pack(src, group_counts):
    num_heads, tokens, width = src.shape
    n_chunks = tokens // CHUNK
    shapes = [(num_heads, tokens // CLASSES * count, width) for count in group_counts]
    n_groups = max(group_counts)
    runs = src.reshape(num_heads, n_chunks, CLASSES, RUN, width)

    def run_spec(group):
        return pl.BlockSpec((1, n_chunks, 1, RUN, width), lambda h: (h, 0, class_of_group(h, group), 0, 0))

    return pl.pallas_call(
        lambda *refs: pack_kernel(n_groups, *refs),
        grid=(num_heads,),
        out_shape=[jax.ShapeDtypeStruct(s, BF16) for s in shapes],
        in_specs=[run_spec(group) for group in range(n_groups)],
        out_specs=[pl.BlockSpec((1,) + s[1:], lambda h: (h, 0, 0)) for s in shapes],
        compiler_params=params(),
        cost_estimate=pl.CostEstimate(flops=10 ** 8, bytes_accessed=3 * src.size, transcendentals=0),
        name="pack",
    )(*[runs] * n_groups)


def sort_kernel(x_ref, y_ref):
    row = lax.broadcasted_iota(jnp.int32, (CHUNK, CHUNK), 0)
    col = lax.broadcasted_iota(jnp.int32, (CHUNK, CHUNK), 1)
    perm = (col == (row % RUN) * CLASSES + row // RUN).astype(F32).astype(BF16)
    y_ref[...] = dot_nn(perm, x_ref[...]).astype(BF16)


def sort_by_class(x):
    tokens, width = x.shape
    spec = pl.BlockSpec((CHUNK, width), lambda i: (i, 0))
    return pl.pallas_call(
        sort_kernel,
        grid=(tokens // CHUNK,),
        out_shape=jax.ShapeDtypeStruct(x.shape, BF16),
        in_specs=[spec],
        out_specs=spec,
        compiler_params=params(),
        cost_estimate=pl.CostEstimate(flops=2 * 10 ** 9, bytes_accessed=4 * x.size, transcendentals=0),
        name="sort_by_class",
    )(x)


def head_spec(shape, first=0, last=None):
    if last is None:
        return pl.BlockSpec((1,) + shape[1:], lambda h, flags: (h + first, 0, 0))
    return pl.BlockSpec((1,) + shape[1:], lambda h, flags: (jnp.minimum(h, last), 0, 0))


def local_kernel(first_head, flag_ref, q_ref, k_ref, v_ref, pk_ref, pv_ref, *refs):
    ot_ref, st_ref, lse_ref, late_ref, vt_ref, s_ref = refs[-6:]
    head = pl.program_id(0) + first_head
    tokens = q_ref.shape[1]
    n_pairs = tokens // (2 * CHUNK)
    vt_ref[:, :tokens] = jnp.transpose(v_ref[0])
    vt_ref[:, tokens:] = jnp.transpose(pv_ref[0])

    lane = lax.broadcasted_iota(jnp.int32, (8, CHUNK), 1)
    row = lax.broadcasted_iota(jnp.int32, (8, CHUNK), 0)
    both = (row ^ head) | lane_class(lane)
    log_mult = jnp.where(both == 0, 2.0, jnp.where(both % 4 == 0, math.log2(3.0), jnp.where(both % 2 == 0, 1.0, 0.0)))
    both = lane_class(row * 2 * RUN) | lane_class(lane)
    log_mult_pair = jnp.where(both == 0, math.log2(3.0), jnp.where(both % 4 == 0, 1.0, 0.0))
    log_mult_pair = jnp.where(flag_ref[0] == 1, log_mult_pair, -jnp.inf)
    row_run = lax.broadcasted_iota(jnp.int32, (RUN, CHUNK), 0) * CLASSES
    lane_run = lax.broadcasted_iota(jnp.int32, (RUN, CHUNK), 1)

    def scores(tile):
        matched, pair, slot = tile
        first = head if matched else head ^ 1
        q = gather_tile(q_ref, pair, [class_of_group(first, g) for g in range(4)])
        if matched:
            late_ref[0, pair * 128:(pair + 1) * 128, :] = q[:128, :]
        limit = lane_position(lane_run, first) - row_run
        m = jnp.full((8, CHUNK), -jnp.inf, F32)
        for j in range(2 * pair + 2):
            s = dot_nt(k_ref[0, j * CHUNK:(j + 1) * CHUNK, :], q)
            for r in range(CLASSES):
                part = s[r * RUN:(r + 1) * RUN, :]
                if j >= 2 * pair:
                    part = jnp.where(limit >= (j - 2 * pair) * CHUNK + r, part, -jnp.inf)
                s_ref[slot, j * CHUNK + r * RUN:j * CHUNK + (r + 1) * RUN, :] = part
                m = jnp.maximum(m, fold_rows(part, jnp.maximum))
        if matched:
            m_pair = jnp.full((8, CHUNK), -jnp.inf, F32)
            for g in range(4):
                s = dot_nt(pk_ref[0, g * CHUNK:(g + 1) * CHUNK, :], q)
                s_ref[slot, tokens + g * CHUNK:tokens + (g + 1) * CHUNK, :] = s
                m_pair = jnp.maximum(m_pair, fold_rows(s, jnp.maximum))
            m = jnp.maximum(m, jnp.where(flag_ref[0] == 1, m_pair, -jnp.inf))
        return jnp.max(m, axis=0, keepdims=True) * LOG2E

    def values(tile, m):
        matched, pair, slot = tile
        starts = [j * CHUNK for j in range(2 * pair + 2)] + ([tokens + g * CHUNK for g in range(4)] if matched else [])
        total = jnp.zeros((8, CHUNK), F32)
        acc = None
        for start in starts:
            if not matched:
                p = jnp.exp2(s_ref[slot, start:start + CHUNK, :] * LOG2E - m)
            elif start >= tokens:
                g = (start - tokens) // CHUNK
                p = jnp.exp2(s_ref[slot, start:start + CHUNK, :] * LOG2E + (log_mult_pair[g:g + 1, :] - m))
            else:
                p = jnp.concatenate([jnp.exp2(s_ref[slot, start + r * RUN:start + (r + 1) * RUN, :] * LOG2E + (log_mult[r:r + 1, :] - m))
                                     for r in range(CLASSES)], axis=0)
            total = total + fold_rows(p, jnp.add)
            part = dot_nn(vt_ref[:, start:start + CHUNK], p.astype(BF16))
            acc = part if acc is None else acc + part
        l = jnp.sum(total, axis=0, keepdims=True)
        out = acc * (1.0 / l)
        lanes = (2 * pair + (0 if matched else 1)) * CHUNK
        ot_ref[0, :, lanes:lanes + CHUNK] = out.astype(BF16)
        if matched:
            st_ref[0, :, pair * 128:(pair + 1) * 128] = out[:, :128]
            lse_ref[0, :, pair * 128:(pair + 1) * 128] = jnp.broadcast_to((m + jnp.log2(l))[:, :128], (8, 128))

    tiles = [(matched, pair) for pair in range(n_pairs) for matched in (True, False)]
    tiles = [(matched, pair, n % 2) for n, (matched, pair) in enumerate(tiles)]
    m = scores(tiles[0])
    for tile, following in zip(tiles, tiles[1:] + [None]):
        m_following = None if following is None else scores(following)
        values(tile, m)
        m = m_following


def local_attention(flags, q, k, v, pair_k, pair_v, first_head, count, previous, after):
    num_heads, tokens, width = q.shape
    shapes = [jax.ShapeDtypeStruct((num_heads, width, tokens), BF16),
              jax.ShapeDtypeStruct((num_heads, width, tokens // 4), F32),
              jax.ShapeDtypeStruct((num_heads, 8, tokens // 4), F32),
              jax.ShapeDtypeStruct((num_heads, tokens // 4, width), BF16)]
    ins = (q, k, v, pair_k, pair_v)
    extra = tuple(previous) + tuple(after)
    return pl.pallas_call(
        lambda *refs: local_kernel(first_head, *refs),
        grid_spec=pltpu.PrefetchScalarGridSpec(
            num_scalar_prefetch=1,
            grid=(count,),
            in_specs=[head_spec(a.shape, first_head) for a in ins] + [pl.BlockSpec(memory_space=pl.ANY)] * len(extra),
            out_specs=[head_spec(s.shape, first_head) for s in shapes],
            scratch_shapes=[pltpu.VMEM((width, tokens + pair_k.shape[1]), BF16),
                            pltpu.VMEM((2, tokens + pair_k.shape[1], CHUNK), F32)],
        ),
        out_shape=shapes,
        input_output_aliases={len(ins) + 1 + n: n for n in range(len(previous))},
        compiler_params=params(),
        cost_estimate=pl.CostEstimate(flops=count * 5 * 10 ** 9, bytes_accessed=count * 10 ** 7, transcendentals=count * 4 * 10 ** 6),
        name="local_attention",
    )(flags, *ins, *extra)


def far_kernel(flag_ref, qa_ref, qb_ref, *refs):
    keys, values, outs = refs[:4], refs[4:8], refs[-4:]

    @pl.when(flag_ref[2] == 1)
    def _():
        turned = [jnp.transpose(v_ref[0]) for v_ref in values]
        for side, q_ref in enumerate((qa_ref, qb_ref)):
            scores = [dot_nt(k_ref[0], q_ref[0]) for k_ref in keys]
            m = fold_rows(scores[0], jnp.maximum)
            for s in scores[1:]:
                m = jnp.maximum(m, fold_rows(s, jnp.maximum))
            m = jnp.max(m, axis=0, keepdims=True) * LOG2E
            total = jnp.zeros((8, CHUNK), F32)
            acc = None
            for s, vt in zip(scores, turned):
                p = jnp.exp2(s * LOG2E - m)
                total = total + fold_rows(p, jnp.add)
                part = dot_nn(vt, p.astype(BF16))
                acc = part if acc is None else acc + part
            l = jnp.sum(total, axis=0, keepdims=True)
            outs[2 * side][0] = acc * (1.0 / l)
            outs[2 * side + 1][0] = jnp.broadcast_to(m + jnp.log2(l), (8, CHUNK))


def far_attention(flags, q_own, q_later, keys, values, after):
    num_heads, rows, width = q_own.shape
    shapes = [jax.ShapeDtypeStruct((num_heads, width, rows), F32), jax.ShapeDtypeStruct((num_heads, 8, rows), F32)] * 2
    ins = (q_own, q_later, *keys, *values)
    return pl.pallas_call(
        far_kernel,
        grid_spec=pltpu.PrefetchScalarGridSpec(
            num_scalar_prefetch=1,
            grid=(num_heads,),
            in_specs=[head_spec(a.shape) for a in ins] + [pl.BlockSpec(memory_space=pl.ANY)] * len(after),
            out_specs=[head_spec(s.shape) for s in shapes],
        ),
        out_shape=shapes,
        compiler_params=params(),
        cost_estimate=pl.CostEstimate(flops=5 * 10 ** 9, bytes_accessed=2 * 10 ** 7, transcendentals=4 * 10 ** 6),
        name="far_attention",
    )(flags, *ins, *after)


def final_kernel(num_heads, flag_ref, q_ref, ot_ref, st_ref, lse_ref, k0_ref, k1_ref, v0_ref, v1_ref,
                 fo0_ref, fl0_ref, fo1_ref, fl1_ref, wo_ref, y_ref, o_ref, merged_ref):
    step = pl.program_id(0)

    @pl.when(step < num_heads)
    def _():
        head = step
        lane = lax.broadcasted_iota(jnp.int32, (8, CHUNK), 1)
        first = (lane % 128) < 64

        def merge(with_quad):
            far_lse = jnp.where(flag_ref[2] == 1, fl0_ref[0], jnp.where(flag_ref[3] == 1, fl1_ref[0], -jnp.inf))
            for half in range(2):
                lanes = slice(half * CHUNK, (half + 1) * CHUNK)
                block = slice(half * 128, (half + 1) * 128)
                far = jnp.where(flag_ref[2] == 1, fo0_ref[0, :, block], jnp.where(flag_ref[3] == 1, fo1_ref[0, :, block], 0.0))
                far = jnp.concatenate([far, pltpu.roll(far, 64, 1)], axis=1)
                f_lse = far_lse[:, block]
                f_lse = jnp.where(first, jnp.concatenate([f_lse, pltpu.roll(f_lse, 64, 1)], axis=1), -jnp.inf)
                lse = lse_ref[0, :, lanes]
                m = jnp.maximum(lse, f_lse)
                scores = []
                if with_quad:
                    q = q_ref[0, lanes, :]
                    for k_ref in (k0_ref, k1_ref):
                        for g in range(2):
                            s = dot_nt(k_ref[0, g * CHUNK:(g + 1) * CHUNK, :], q) * LOG2E
                            if g == 0:
                                s = s + jnp.where(first, 1.0, 0.0)[:1, :]
                            scores.append(s)
                            m = jnp.maximum(m, fold_rows(s, jnp.maximum))
                m = jnp.max(m, axis=0, keepdims=True)
                own_weight = jnp.exp2(lse[:1, :] - m)
                far_weight = jnp.exp2(f_lse[:1, :] - m)
                out = st_ref[0, :, lanes] * own_weight + far * far_weight
                l = own_weight + far_weight
                total = jnp.zeros((8, CHUNK), F32)
                acc = None
                for n, s in enumerate(scores):
                    p = jnp.exp2(s - m)
                    total = total + fold_rows(p, jnp.add)
                    values = jnp.transpose((v0_ref, v1_ref)[n // 2][0, n % 2 * CHUNK:(n % 2 + 1) * CHUNK, :])
                    part = dot_nn(values, p.astype(BF16))
                    acc = part if acc is None else acc + part
                if with_quad:
                    out = out + acc
                    l = l + jnp.sum(total, axis=0, keepdims=True)
                merged_ref[:, lanes] = (out * (1.0 / l)).astype(BF16)

        @pl.when(flag_ref[1] == 1)
        def _():
            merge(True)

        @pl.when(flag_ref[1] == 0)
        def _():
            merge(False)

        token = lax.broadcasted_iota(jnp.int32, (2 * CHUNK, CHUNK), 0)
        column = lax.broadcasted_iota(jnp.int32, (2 * CHUNK, CHUNK), 1)
        places = [(token == lane_position(column, c)).astype(F32).astype(BF16) for c in (head, head ^ 1)]
        for pair in range(4):
            start = 2 * pair * CHUNK
            matched = jnp.concatenate([merged_ref[:, pair * 128:(pair + 1) * 128],
                                       ot_ref[0, :, start + 128:start + CHUNK]], axis=1)
            rows = dot_nt(places[0], matched) + dot_nt(places[1], ot_ref[0, :, start + CHUNK:start + 2 * CHUNK])
            columns = pl.ds(pl.multiple_of(head * CHUNK, CHUNK), CHUNK)
            o_ref[start:start + 2 * CHUNK, columns] = rows.astype(BF16)

    @pl.when(step >= num_heads)
    def _():
        y_ref[...] = dot_nn(o_ref[...], wo_ref[...]).astype(BF16)


def final_attention(flags, q, ot, st, lse, keys, values, far, w_out):
    num_heads, width, tokens = ot.shape
    d_model = w_out.shape[1]
    ins = (q, ot, st, lse, *keys, *values, *far)
    column = lambda h, flags: (0, jnp.maximum(h - num_heads, 0))
    return pl.pallas_call(
        lambda *refs: final_kernel(num_heads, *refs),
        grid_spec=pltpu.PrefetchScalarGridSpec(
            num_scalar_prefetch=1,
            grid=(num_heads + d_model // 256,),
            in_specs=[head_spec(a.shape, last=num_heads - 1) for a in ins] + [pl.BlockSpec((w_out.shape[0], 256), column)],
            out_specs=pl.BlockSpec((tokens, 256), column),
            scratch_shapes=[pltpu.VMEM((tokens, num_heads * width), BF16), pltpu.VMEM((width, tokens // 4), BF16)],
        ),
        out_shape=jax.ShapeDtypeStruct((tokens, d_model), BF16),
        compiler_params=params(),
        cost_estimate=pl.CostEstimate(flops=3 * 10 ** 10, bytes_accessed=6 * 10 ** 7, transcendentals=5 * 10 ** 6),
        name="final_attention",
    )(flags, *ins, w_out)


def solution(mesh):
    row_spec = P(('dp', 'seq'), None)
    pair_up = [(s, s + 1) for s in (0, 2, 4, 6)]
    next_chip = [(0, 2), (1, 3), (4, 6), (5, 7)]
    swap_upper = [(s, s ^ 1) for s in (2, 3, 6, 7)]
    from_first = [(0, 4), (1, 5)]
    from_second = [(2, 4), (3, 5)]
    swap_third = [(4, 5), (5, 4)]
    to_third = [(6, 4), (7, 5)]
    to_fourth = [(4, 6), (5, 7)]

    def send(array, pairs):
        return lax.ppermute(array, 'seq', pairs)

    def layer(hidden, w_query, w_key, w_value, w_out):
        _, d_model = hidden.shape
        num_heads, head_dim = w_query.shape[1:]
        index = lax.axis_index('seq')
        chip = index // 2
        flags = jnp.stack([index % 2, chip % 2, (chip == 2).astype(jnp.int32), (chip == 3).astype(jnp.int32)]).astype(jnp.int32)

        x = sort_by_class(hidden)

        def project(weight):
            return jnp.einsum('td,dhe->hte', x, weight, preferred_element_type=F32)

        def spread(packs):
            far_rows, quad_rows, pair_rows = packs
            first = send(far_rows, from_first)
            second = send(far_rows, from_second)
            quad = send(quad_rows, next_chip)
            pair = send(pair_rows, pair_up)
            swapped = send(first, swap_third), send(second, swap_third)
            return pair, (quad, send(quad, swap_upper)), (first, second, *swapped)

        k = project(w_key).astype(BF16)
        pair_k, quad_k, far_k = spread(pack(k, (1, 2, 4)))
        v = project(w_value).astype(BF16)
        pair_v, quad_v, far_v = spread(pack(v, (1, 2, 4)))
        q = (project(w_query) * head_dim ** -0.5).astype(BF16)
        q_far, = pack(q, (1,))
        q_later = send(q_far, to_third)

        early = 2
        state = local_attention(flags, q, k, v, pair_k, pair_v, 0, early, (), ())
        own_o, own_lse, later_o, later_lse = far_attention(flags, q_far, q_later, far_k, far_v, (state[2],))
        got_o, got_lse = send(later_o, to_fourth), send(later_lse, to_fourth)
        ot, st, lse, q_late = local_attention(flags, q, k, v, pair_k, pair_v, early, num_heads - early, state, (own_lse,))
        return final_attention(flags, q_late, ot, st, lse, quad_k, quad_v, (own_o, own_lse, got_o, got_lse),
                               w_out.reshape(num_heads * head_dim, d_model))

    return jax.shard_map(layer, mesh=mesh, in_specs=(row_spec, P(), P(), P(), P()), out_specs=row_spec, check_vma=False)
```

time: 383 us -> 342 us (0.89)
  the two profiles are of different devices: /device:TPU:28 before, /device:TPU:30 now
where the time goes in v3:
time: 342 us; the launch traced here: 340 us
  Pallas kernels  136 us (40%)
  waiting for transfers between devices  93 us (27%)
  matrix products  70.3 us (21%)
  starting transfers between devices  39.2 us (11%)
    ppermute x17, waiting for transfers between devices, send(): return lax.ppermute(array, 'seq', pairs)  93 us
    dot_general x3, matrix products, project(): return jnp.einsum('td,dhe->hte', x, weight, preferred_element_type=F32)  70.3 us
    pallas_call x2, Pallas kernels, local_attention(): pl.pallas_call(lambda *refs: local_kernel(first_head, *refs), grid_spec=p...  55.7 us
    pallas_call x1, Pallas kernels, final_attention(): pl.pallas_call(lambda *refs: final_kernel(num_heads, *refs), grid_spec=pl...  41.1 us
    ppermute x17, starting transfers between devices, send(): return lax.ppermute(array, 'seq', pairs)  39.2 us
    pallas_call x3, Pallas kernels, pack(): pl.pallas_call(lambda *refs: pack_kernel(n_groups, *refs), grid=(num_head...  19.9 us
    pallas_call x1, Pallas kernels, sort_by_class(): pl.pallas_call(sort_kernel, grid=(tokens // CHUNK,), out_shape=jax.ShapeD...  10.4 us
    pallas_call x1, Pallas kernels, far_attention(): pl.pallas_call(far_kernel, grid_spec=pltpu.PrefetchScalarGridSpec(num_sca...  8.46 us
  transfers between devices with their start and end apart: 17, of which 4 were waited for; matrix products, arithmetic and copies ran while one was open for 14% of the time, Pallas kernels for 23%

profile of v3, /device:TPU:30, one launch (start us, length us, event | category | flops | bytes accessed | tf_op | source)
XLA Modules:
  0.0 340.5 jit_solution(10118191662134151974)
XLA Ops:
  0.0 10.4 %sort_by_class.1 = bf16[2048,2048]{1,0:T(8,128)(2,1)} custom-call(bf16[2048,2048]{1,0:T(8,128)(2,1)} %x_ref.1), custom_call_target="tpu_custom_call" | custom-call | flops 2000000000 | bytes 16777216 | tf_op jit(solution)/shard_map/sort_by_class/pallas_call | solution.py:100
  10.4 23.4 %fusion.14 = bf16[8,256,2048]{1,2,0:T(8,128)(2,1)} fusion(bf16[2048,8,256]{2,1,0:T(8,128)(2,1)} %param.7, bf16[2048,2048]{1,0:T(8,128)(2,1)} %sort_by_class.1), kind=kOutput, calls=%fused_computation.11 | convolution fusion | flops 17184063488 | bytes 25165824 | tf_op jit(solution)/shard_map/td,dhe->hte/dot_general | solution.py:382
  33.8 7.3 %pack.3 = (bf16[8,256,256]{2,1,0:T(8,128)(2,1)}, bf16[8,512,256]{2,1,0:T(8,128)(2,1)}, bf16[8,1024,256]{2,1,0:T(8,128)(2,1)}) custom-call(bf16[8,8,8,32,256]{4,3,2,1,0:T(8,128)(2,1)} %bitcast.27, bf16[8,8,8,32,256]{4,3,2,1,0:T(8,128)(2,1)} %bitcast.28, bf16[8,8,8,32,256]{4,3,2,1,0:T(8,128)(2,1)} %bitcast.29, bf16[8,8,8,32,256]{4,3,2,1,0:T(8,128)(2,1)} %bitcast.30), custom_call_target="tpu_custom_call" | custom-call | flops 100000000 | bytes 12582912 | tf_op jit(solution)/shard_map/pack/pallas_call | solution.py:78
  41.1 0.7 collective-permute-start.3
  41.8 0.7 collective-permute-start.4
  42.6 3.8 %collective-permute-start = (bf16[8,1024,256]{2,1,0:T(8,128)(2,1)}, bf16[8,1024,256]{2,1,0:T(8,128)(2,1)}, u32[]{:S(2)}, u32[]{:S(2)}) collective-permute-start(bf16[8,1024,256]{2,1,0:T(8,128)(2,1)} %get-tuple-element.23), channel_id=1, source_target_pairs={{0,1},{2,3},{4,5},{6,7},{8,9},{10,11},{12,13},{14,15},{16,17},{18,... | collective-permute-start | bytes 12582920 | tf_op jit(solution)/shard_map/ppermute | solution.py:370
  46.4 23.4 %fusion.9 = bf16[8,256,2048]{1,2,0:T(8,128)(2,1)} fusion(bf16[2048,8,256]{2,1,0:T(8,128)(2,1)} %param.8, bf16[2048,2048]{1,0:T(8,128)(2,1)} %sort_by_class.1), kind=kOutput, calls=%fused_computation.10 | convolution fusion | flops 17184063488 | bytes 25165824 | tf_op jit(solution)/shard_map/td,dhe->hte/dot_general | solution.py:382
  69.8 7.4 %pack.4 = (bf16[8,256,256]{2,1,0:T(8,128)(2,1)}, bf16[8,512,256]{2,1,0:T(8,128)(2,1)}, bf16[8,1024,256]{2,1,0:T(8,128)(2,1)}) custom-call(bf16[8,8,8,32,256]{4,3,2,1,0:T(8,128)(2,1)} %bitcast.33, bf16[8,8,8,32,256]{4,3,2,1,0:T(8,128)(2,1)} %bitcast.34, bf16[8,8,8,32,256]{4,3,2,1,0:T(8,128)(2,1)} %bitcast.35, bf16[8,8,8,32,256]{4,3,2,1,0:T(8,128)(2,1)} %bitcast.36), custom_call_target="tpu_custom_call" | custom-call | flops 100000000 | bytes 12582912 | tf_op jit(solution)/shard_map/pack/pallas_call | solution.py:78
  77.2 3.3 collective-permute-start.1
  80.5 1.6 collective-permute-start.8
  82.1 23.4 %multiply_convert_fusion = bf16[8,256,2048]{1,2,0:T(8,128)(2,1)} fusion(bf16[2048,8,256]{2,1,0:T(8,128)(2,1)} %param.6, bf16[2048,2048]{1,0:T(8,128)(2,1)} %sort_by_class.1), kind=kOutput, calls=%fused_computation | convolution fusion | flops 17188257792 | bytes 25165824 | tf_op jit(solution)/shard_map/td,dhe->hte/dot_general | solution.py:382
  105.6 0.0 collective-permute-done.8.refs_5_
  105.6 0.7 collective-permute-start.7
  106.3 5.2 %pack.5.qa_ref = bf16[8,256,256]{2,1,0:T(8,128)(2,1)} custom-call(bf16[8,8,8,32,256]{4,3,2,1,0:T(8,128)(2,1)} %bitcast.39), custom_call_target="tpu_custom_call" | custom-call | flops 100000000 | bytes 12582912 | tf_op jit(solution)/shard_map/pack/pallas_call | solution.py:78
  111.5 0.0 collective-permute-done.3.refs_0_
  111.5 0.0 copy-start.1
  111.5 12.4 %collective-permute-start.2 = (bf16[8,256,256]{2,1,0:T(8,128)(2,1)}, bf16[8,256,256]{2,1,0:T(8,128)(2,1)}, u32[]{:S(2)}, u32[]{:S(2)}) collective-permute-start(bf16[8,256,256]{2,1,0:T(8,128)(2,1)} %pack.5.qa_ref), channel_id=1, source_target_pairs={{6,4},{7,5},{14,12},{15,13},{22,20},{23,21},{30,28},{31,29}} | collective-permute-start | bytes 3145736 | tf_op jit(solution)/shard_map/ppermute | solution.py:370
  123.9 0.0 collective-permute-done.4.refs_1_
  123.9 0.0 copy-start.2
  123.9 1.6 collective-permute-start.10
  125.5 0.0 collective-permute-done.7.refs_4_
  125.5 0.0 copy-done.2
  125.5 0.0 copy-start.3
  125.5 1.0 copy-done.3
  126.5 1.3 collective-permute-start.11
  127.8 18.0 %collective-permute-done.2.qb_ref = bf16[8,256,256]{2,1,0:T(8,128)(2,1)} collective-permute-done((bf16[8,256,256]{2,1,0:T(8,128)(2,1)}, bf16[8,256,256]{2,1,0:T(8,128)(2,1)}, u32[]{:S(2)}, u32[]{:S(2)}) %collective-permute-start.2) | collective-permute-done | bytes 1048608 | tf_op jit(solution)/shard_map/ppermute | solution.py:370
  145.8 1.3 collective-permute-start.13
  147.1 0.0 collective-permute-done.10.refs_7_
  147.1 1.6 collective-permute-start.5
  148.8 0.0 collective-permute-done.refs_4_
  148.8 1.8 collective-permute-start.6
  150.6 0.0 collective-permute-done.1.refs_5_
  150.6 1.6 collective-permute-start.9
  152.3 0.6 pad_add_fusion.refs_0_.flag_ref
  152.9 15.9 %local_attention.2 = (bf16[8,256,2048]{2,1,0:T(8,128)(2,1)}, f32[8,256,512]{2,1,0:T(8,128)}, f32[8,8,512]{2,1,0:T(8,128)}, bf16[8,512,256]{2,1,0:T(8,128)(2,1)}) custom-call(s32[4]{0:T(128)} %pad_add_fusion.refs_0_.flag_ref, bf16[8,2048,256]{2,1,0:T(8,128)(2,1)} %bitcast.40, bf16[8,2048,256]{2,1,0:T(8,128)(2,1)} %bitcast.31, bf16[8,2048,256]{2,1,0:T(8,128)(2,1)} %bitcast.37, ...), custom_call_target="tpu_custom_call" | custom-call | flops 10000000000 | bytes 20000000 | tf_op jit(solution)/shard_map/local_attention/pallas_call | solution.py:203
  168.8 0.0 copy-done.1
  168.8 22.7 %collective-permute-done.11.refs_5_ = bf16[8,512,256]{2,1,0:T(8,128)(2,1)S(1)} collective-permute-done((bf16[8,512,256]{2,1,0:T(8,128)(2,1)}, bf16[8,512,256]{2,1,0:T(8,128)(2,1)S(1)}, u32[]{:S(2)}, u32[]{:S(2)}) %collective-permute-start.11) | collective-permute-done | bytes 2097184 | tf_op jit(solution)/shard_map/ppermute | solution.py:370
  191.5 0.0 copy-start
  191.5 1.9 collective-permute-start.12
  193.4 41.6 %collective-permute-done.13.refs_7_ = bf16[8,512,256]{2,1,0:T(8,128)(2,1)} collective-permute-done((bf16[8,512,256]{2,1,0:T(8,128)(2,1)}, bf16[8,512,256]{2,1,0:T(8,128)(2,1)}, u32[]{:S(2)}, u32[]{:S(2)}) %collective-permute-start.13) | collective-permute-done | bytes 2097184 | tf_op jit(solution)/shard_map/ppermute | solution.py:370
  235.0 1.9 collective-permute-start.14
  236.9 0.0 collective-permute-done.5.refs_2_
  236.9 0.0 collective-permute-done.6.refs_3_
  236.9 0.0 collective-permute-done.9.refs_6_
  237.0 8.5 %far_attention.1 = (f32[8,256,256]{2,1,0:T(8,128)}, f32[8,8,256]{2,1,0:T(8,128)}, f32[8,256,256]{2,1,0:T(8,128)}, f32[8,8,256]{2,1,0:T(8,128)}) custom-call(s32[4]{0:T(128)} %pad_add_fusion.refs_0_.flag_ref, bf16[8,256,256]{2,1,0:T(8,128)(2,1)} %pack.5.qa_ref, bf16[8,256,256]{2,1,0:T(8,128)(2,1)} %collective-permute-done.2.qb_ref, ...), custom_call_target="tpu_custom_call" | custom-call | flops 5000000000 | bytes 20000000 | tf_op jit(solution)/shard_map/far_attention/pallas_call | solution.py:249
  245.4 0.0 copy-done
  245.4 1.3 collective-permute-start.15
  246.7 1.5 collective-permute-start.16
  248.3 39.8 %local_attention.3 = (bf16[8,256,2048]{2,1,0:T(8,128)(2,1)}, f32[8,256,512]{2,1,0:T(8,128)}, f32[8,8,512]{2,1,0:T(8,128)}, bf16[8,512,256]{2,1,0:T(8,128)(2,1)}) custom-call(s32[4]{0:T(128)} %pad_add_fusion.refs_0_.flag_ref, bf16[8,2048,256]{2,1,0:T(8,128)(2,1)} %bitcast.41, ...), custom_call_target="tpu_custom_call", output_to_operand_aliasing={{0}: (6, {}), {1}: (7, {}), {2}: (8, {}), {3}: (9, {})} | custom-call | flops 30000001024 | bytes 60000000 | tf_op jit(solution)/shard_map/local_attention/pallas_call | solution.py:203
  288.1 0.0 collective-permute-done.12.refs_6_
  288.1 0.0 collective-permute-done.14.refs_8_
  288.1 10.7 %collective-permute-done.16.refs_12_ = f32[8,8,256]{2,1,0:T(8,128)S(1)} collective-permute-done((f32[8,8,256]{2,1,0:T(8,128)}, f32[8,8,256]{2,1,0:T(8,128)S(1)}, u32[]{:S(2)}, u32[]{:S(2)}) %collective-permute-start.16) | collective-permute-done | bytes 65568 | tf_op jit(solution)/shard_map/ppermute | solution.py:370
  298.8 0.0 copy-start.4
  298.8 0.0 collective-permute-done.15.refs_11_
  298.8 0.6 copy-done.4
  299.4 41.1 %final_attention.1 = bf16[2048,2048]{1,0:T(8,128)(2,1)} custom-call(s32[4]{0:T(128)} %pad_add_fusion.refs_0_.flag_ref, bf16[8,512,256]{2,1,0:T(8,128)(2,1)} %get-tuple-element.32.refs_1_, bf16[8,256,2048]{2,1,0:T(8,128)(2,1)} %get-tuple-element.33.refs_2_, f32[8,256,512]{2,1,0:T(8,128)} %get-tuple-element.34.refs_3_, ...), custom_call_target="tpu_custom_call" | custom-call | flops 30000001024 | bytes 60000000 | tf_op jit(solution)/shard_map/final_attention/pallas_call | solution.py:342
Async XLA Ops:
  41.1 70.4 %collective-permute-start.3 = (bf16[8,256,256]{2,1,0:T(8,128)(2,1)}, bf16[8,256,256]{2,1,0:T(8,128)(2,1)S(1)}, u32[]{:S(2)}, u32[]{:S(2)}) collective-permute-start(bf16[8,256,256]{2,1,0:T(8,128)(2,1)} %get-tuple-element.29), channel_id=1, source_target_pairs={{0,4},{1,5},{8,12},{9,13},{16,20},{17,21},{24,28},{25,29}} | collective-permute-start | bytes 3145736 | tf_op jit(solution)/shard_map/ppermute | solution.py:370
  41.8 82.0 %collective-permute-start.4 = (bf16[8,256,256]{2,1,0:T(8,128)(2,1)}, bf16[8,256,256]{2,1,0:T(8,128)(2,1)S(1)}, u32[]{:S(2)}, u32[]{:S(2)}) collective-permute-start(bf16[8,256,256]{2,1,0:T(8,128)(2,1)} %get-tuple-element.29), channel_id=1, source_target_pairs={{2,4},{3,5},{10,12},{11,13},{18,20},{19,21},{26,28},{27,29}} | collective-permute-start | bytes 3145736 | tf_op jit(solution)/shard_map/ppermute | solution.py:370
  42.6 106.2 %collective-permute-start = (bf16[8,1024,256]{2,1,0:T(8,128)(2,1)}, bf16[8,1024,256]{2,1,0:T(8,128)(2,1)}, u32[]{:S(2)}, u32[]{:S(2)}) collective-permute-start(bf16[8,1024,256]{2,1,0:T(8,128)(2,1)} %get-tuple-element.23), channel_id=1, source_target_pairs={{0,1},{2,3},{4,5},{6,7},{8,9},{10,11},{12,13},{14,15},{16,17},{18,... | collective-permute-start | bytes 12582920 | tf_op jit(solution)/shard_map/ppermute | solution.py:370
  77.2 73.4 %collective-permute-start.1 = (bf16[8,1024,256]{2,1,0:T(8,128)(2,1)}, bf16[8,1024,256]{2,1,0:T(8,128)(2,1)}, u32[]{:S(2)}, u32[]{:S(2)}) collective-permute-start(bf16[8,1024,256]{2,1,0:T(8,128)(2,1)} %get-tuple-element.24), channel_id=1, source_target_pairs={{0,1},{2,3},{4,5},{6,7},{8,9},{10,11},{12,13},{14,15},{16,17},{18,... | collective-permute-start | bytes 12582920 | tf_op jit(solution)/shard_map/ppermute | solution.py:370
  80.5 25.1 %collective-permute-start.8 = (bf16[8,256,256]{2,1,0:T(8,128)(2,1)}, bf16[8,256,256]{2,1,0:T(8,128)(2,1)}, u32[]{:S(2)}, u32[]{:S(2)}) collective-permute-start(bf16[8,256,256]{2,1,0:T(8,128)(2,1)} %get-tuple-element.30), channel_id=1, source_target_pairs={{2,4},{3,5},{10,12},{11,13},{18,20},{19,21},{26,28},{27,29}} | collective-permute-start | bytes 3145736 | tf_op jit(solution)/shard_map/ppermute | solution.py:370
  105.6 20.0 %collective-permute-start.7 = (bf16[8,256,256]{2,1,0:T(8,128)(2,1)}, bf16[8,256,256]{2,1,0:T(8,128)(2,1)S(1)}, u32[]{:S(2)}, u32[]{:S(2)}) collective-permute-start(bf16[8,256,256]{2,1,0:T(8,128)(2,1)} %get-tuple-element.30), channel_id=1, source_target_pairs={{0,4},{1,5},{8,12},{9,13},{16,20},{17,21},{24,28},{25,29}} | collective-permute-start | bytes 3145736 | tf_op jit(solution)/shard_map/ppermute | solution.py:370
  111.5 57.3 %copy-start.1 = (bf16[8,256,256]{2,1,0:T(8,128)(2,1)}, bf16[8,256,256]{2,1,0:T(8,128)(2,1)S(1)}, u32[]{:S(2)}) copy-start(bf16[8,256,256]{2,1,0:T(8,128)(2,1)S(1)} %collective-permute-done.3.refs_0_) | copy-start | bytes 3145732
  111.5 34.3 %collective-permute-start.2 = (bf16[8,256,256]{2,1,0:T(8,128)(2,1)}, bf16[8,256,256]{2,1,0:T(8,128)(2,1)}, u32[]{:S(2)}, u32[]{:S(2)}) collective-permute-start(bf16[8,256,256]{2,1,0:T(8,128)(2,1)} %pack.5.qa_ref), channel_id=1, source_target_pairs={{6,4},{7,5},{14,12},{15,13},{22,20},{23,21},{30,28},{31,29}} | collective-permute-start | bytes 3145736 | tf_op jit(solution)/shard_map/ppermute | solution.py:370
  123.9 1.6 copy-start.2
  123.9 23.3 %collective-permute-start.10 = (bf16[8,256,256]{2,1,0:T(8,128)(2,1)}, bf16[8,256,256]{2,1,0:T(8,128)(2,1)}, u32[]{:S(2)}, u32[]{:S(2)}) collective-permute-start(bf16[8,256,256]{2,1,0:T(8,128)(2,1)} %collective-permute-done.8.refs_5_), channel_id=1, source_target_pairs={{4,5},{5,4},{12,13},{13,12},{20,21},{21,20},{28,29},{29,28}} | collective-permute-start | bytes 3145736 | tf_op jit(solution)/shard_map/ppermute | solution.py:370
  125.5 1.0 copy-start.3
  126.5 65.0 %collective-permute-start.11 = (bf16[8,512,256]{2,1,0:T(8,128)(2,1)}, bf16[8,512,256]{2,1,0:T(8,128)(2,1)S(1)}, u32[]{:S(2)}, u32[]{:S(2)}) collective-permute-start(bf16[8,512,256]{2,1,0:T(8,128)(2,1)} %get-tuple-element.36), channel_id=1, source_target_pairs={{0,2},{1,3},{4,6},{5,7},{8,10},{9,11},{12,14},{13,15},{16,18},{17,... | collective-permute-start | bytes 6291464 | tf_op jit(solution)/shard_map/ppermute | solution.py:370
  145.8 89.2 %collective-permute-start.13 = (bf16[8,512,256]{2,1,0:T(8,128)(2,1)}, bf16[8,512,256]{2,1,0:T(8,128)(2,1)}, u32[]{:S(2)}, u32[]{:S(2)}) collective-permute-start(bf16[8,512,256]{2,1,0:T(8,128)(2,1)} %get-tuple-element.37), channel_id=1, source_target_pairs={{0,2},{1,3},{4,6},{5,7},{8,10},{9,11},{12,14},{13,15},{16,18},{17,... | collective-permute-start | bytes 6291464 | tf_op jit(solution)/shard_map/ppermute | solution.py:370
  147.1 89.8 %collective-permute-start.5 = (bf16[8,256,256]{2,1,0:T(8,128)(2,1)S(1)}, bf16[8,256,256]{2,1,0:T(8,128)(2,1)}, u32[]{:S(2)}, u32[]{:S(2)}) collective-permute-start(bf16[8,256,256]{2,1,0:T(8,128)(2,1)S(1)} %collective-permute-done.3.refs_0_), channel_id=1, source_target_pairs={{4,5},{5,4},{12,13},{13,12},{20,21},{21,20},{28,29},{29,28}} | collective-permute-start | bytes 3145736 | tf_op jit(solution)/shard_map/ppermute | solution.py:370
  148.8 88.2 %collective-permute-start.6 = (bf16[8,256,256]{2,1,0:T(8,128)(2,1)}, bf16[8,256,256]{2,1,0:T(8,128)(2,1)}, u32[]{:S(2)}, u32[]{:S(2)}) collective-permute-start(bf16[8,256,256]{2,1,0:T(8,128)(2,1)} %copy-done.2), channel_id=1, source_target_pairs={{4,5},{5,4},{12,13},{13,12},{20,21},{21,20},{28,29},{29,28}} | collective-permute-start | bytes 3145736 | tf_op jit(solution)/shard_map/ppermute | solution.py:370
  150.6 86.3 %collective-permute-start.9 = (bf16[8,256,256]{2,1,0:T(8,128)(2,1)}, bf16[8,256,256]{2,1,0:T(8,128)(2,1)}, u32[]{:S(2)}, u32[]{:S(2)}) collective-permute-start(bf16[8,256,256]{2,1,0:T(8,128)(2,1)} %copy-done.3), channel_id=1, source_target_pairs={{4,5},{5,4},{12,13},{13,12},{20,21},{21,20},{28,29},{29,28}} | collective-permute-start | bytes 3145736 | tf_op jit(solution)/shard_map/ppermute | solution.py:370
  191.5 53.9 %copy-start = (bf16[8,512,256]{2,1,0:T(8,128)(2,1)}, bf16[8,512,256]{2,1,0:T(8,128)(2,1)S(1)}, u32[]{:S(2)}) copy-start(bf16[8,512,256]{2,1,0:T(8,128)(2,1)S(1)} %collective-permute-done.11.refs_5_) | copy-start | bytes 6291460
  191.5 96.6 %collective-permute-start.12 = (bf16[8,512,256]{2,1,0:T(8,128)(2,1)S(1)}, bf16[8,512,256]{2,1,0:T(8,128)(2,1)}, u32[]{:S(2)}, u32[]{:S(2)}) collective-permute-start(bf16[8,512,256]{2,1,0:T(8,128)(2,1)S(1)} %collective-permute-done.11.refs_5_), channel_id=1, source_target_pairs={{2,3},{3,2},{6,7},{7,6},{10,11},{11,10},{14,15},{15,14},{18,19},{1... | collective-permute-start | bytes 6291464 | tf_op jit(solution)/shard_map/ppermute | solution.py:370
  235.0 53.1 %collective-permute-start.14 = (bf16[8,512,256]{2,1,0:T(8,128)(2,1)}, bf16[8,512,256]{2,1,0:T(8,128)(2,1)}, u32[]{:S(2)}, u32[]{:S(2)}) collective-permute-start(bf16[8,512,256]{2,1,0:T(8,128)(2,1)} %collective-permute-done.13.refs_7_), channel_id=1, source_target_pairs={{2,3},{3,2},{6,7},{7,6},{10,11},{11,10},{14,15},{15,14},{18,19},{1... | collective-permute-start | bytes 6291464 | tf_op jit(solution)/shard_map/ppermute | solution.py:370
  245.4 53.3 %collective-permute-start.15 = (f32[8,256,256]{2,1,0:T(8,128)}, f32[8,256,256]{2,1,0:T(8,128)}, u32[]{:S(2)}, u32[]{:S(2)}) collective-permute-start(f32[8,256,256]{2,1,0:T(8,128)} %get-tuple-element.39), channel_id=1, source_target_pairs={{4,6},{5,7},{12,14},{13,15},{20,22},{21,23},{28,30},{29,31}} | collective-permute-start | bytes 6291464 | tf_op jit(solution)/shard_map/ppermute | solution.py:370
  246.7 52.0 %collective-permute-start.16 = (f32[8,8,256]{2,1,0:T(8,128)}, f32[8,8,256]{2,1,0:T(8,128)S(1)}, u32[]{:S(2)}, u32[]{:S(2)}) collective-permute-start(f32[8,8,256]{2,1,0:T(8,128)} %get-tuple-element.40), channel_id=1, source_target_pairs={{4,6},{5,7},{12,14},{13,15},{20,22},{21,23},{28,30},{29,31}} | collective-permute-start | bytes 196616 | tf_op jit(solution)/shard_map/ppermute | solution.py:370
  298.8 0.6 copy-start.4

commit v4 on v3

--- a/solution.py
+++ b/solution.py
@@ -87,11 +87,14 @@
     )(*[runs] * n_groups)
 
 
-def sort_kernel(x_ref, y_ref):
-    row = lax.broadcasted_iota(jnp.int32, (CHUNK, CHUNK), 0)
-    col = lax.broadcasted_iota(jnp.int32, (CHUNK, CHUNK), 1)
-    perm = (col == (row % RUN) * CLASSES + row // RUN).astype(F32).astype(BF16)
-    y_ref[...] = dot_nn(perm, x_ref[...]).astype(BF16)
+def sort_kernel(x_ref, y_ref, perm_ref):
+    @pl.when(pl.program_id(0) == 0)
+    def _():
+        row = lax.broadcasted_iota(jnp.int32, (CHUNK, CHUNK), 0)
+        col = lax.broadcasted_iota(jnp.int32, (CHUNK, CHUNK), 1)
+        perm_ref[...] = (col == (row % RUN) * CLASSES + row // RUN).astype(F32).astype(BF16)
+
+    y_ref[...] = dot_nn(perm_ref[...], x_ref[...]).astype(BF16)
 
 
 def sort_by_class(x):
@@ -103,16 +106,19 @@
         out_shape=jax.ShapeDtypeStruct(x.shape, BF16),
         in_specs=[spec],
         out_specs=spec,
+        scratch_shapes=[pltpu.VMEM((CHUNK, CHUNK), BF16)],
         compiler_params=params(),
         cost_estimate=pl.CostEstimate(flops=2 * 10 ** 9, bytes_accessed=4 * x.size, transcendentals=0),
         name="sort_by_class",
     )(x)
 
 
-def head_spec(shape, first=0, last=None):
-    if last is None:
-        return pl.BlockSpec((1,) + shape[1:], lambda h, flags: (h + first, 0, 0))
-    return pl.BlockSpec((1,) + shape[1:], lambda h, flags: (jnp.minimum(h, last), 0, 0))
+def head_spec(shape, first=0, last=None, flag=None):
+    def index(h, flags):
+        block = h + first if last is None else jnp.minimum(h, last)
+        return (block if flag is None else block * flags[flag], 0, 0)
+
+    return pl.BlockSpec((1,) + shape[1:], index)
 
 
 def local_kernel(first_head, flag_ref, q_ref, k_ref, v_ref, pk_ref, pv_ref, *refs):
@@ -251,8 +257,8 @@
         grid_spec=pltpu.PrefetchScalarGridSpec(
             num_scalar_prefetch=1,
             grid=(num_heads,),
-            in_specs=[head_spec(a.shape) for a in ins] + [pl.BlockSpec(memory_space=pl.ANY)] * len(after),
-            out_specs=[head_spec(s.shape) for s in shapes],
+            in_specs=[head_spec(a.shape, flag=2) for a in ins] + [pl.BlockSpec(memory_space=pl.ANY)] * len(after),
+            out_specs=[head_spec(s.shape, flag=2) for s in shapes],
         ),
         out_shape=shapes,
         compiler_params=params(),
@@ -338,13 +344,14 @@
     num_heads, width, tokens = ot.shape
     d_model = w_out.shape[1]
     ins = (q, ot, st, lse, *keys, *values, *far)
+    use = (1, None, None, None, 1, 1, 1, 1, 2, 2, 3, 3)
     column = lambda h, flags: (0, jnp.maximum(h - num_heads, 0))
     return pl.pallas_call(
         lambda *refs: final_kernel(num_heads, *refs),
         grid_spec=pltpu.PrefetchScalarGridSpec(
             num_scalar_prefetch=1,
             grid=(num_heads + d_model // 256,),
-            in_specs=[head_spec(a.shape, last=num_heads - 1) for a in ins] + [pl.BlockSpec((w_out.shape[0], 256), column)],
+            in_specs=[head_spec(a.shape, last=num_heads - 1, flag=flag) for a, flag in zip(ins, use)] + [pl.BlockSpec((w_out.shape[0], 256), column)],
             out_specs=pl.BlockSpec((tokens, 256), column),
             scratch_shapes=[pltpu.VMEM((tokens, num_heads * width), BF16), pltpu.VMEM((width, tokens // 4), BF16)],
         ),
@@ -357,14 +364,12 @@
 
 def solution(mesh):
     row_spec = P(('dp', 'seq'), None)
-    pair_up = [(s, s + 1) for s in (0, 2, 4, 6)]
-    next_chip = [(0, 2), (1, 3), (4, 6), (5, 7)]
-    swap_upper = [(s, s ^ 1) for s in (2, 3, 6, 7)]
-    from_first = [(0, 4), (1, 5)]
-    from_second = [(2, 4), (3, 5)]
-    swap_third = [(4, 5), (5, 4)]
+    swap = [(s, s ^ 1) for s in range(8)]
+    next_chip = [(s, s ^ 2) for s in range(8)]
+    from_first = [(0, 4), (4, 0), (1, 5), (5, 1), (2, 3), (3, 2), (6, 7), (7, 6)]
+    from_second = [(2, 4), (4, 2), (3, 5), (5, 3), (0, 1), (1, 0), (6, 7), (7, 6)]
     to_third = [(6, 4), (7, 5)]
-    to_fourth = [(4, 6), (5, 7)]
+    to_fourth = [(4, 6), (6, 4), (5, 7), (7, 5), (0, 1), (1, 0), (2, 3), (3, 2)]
 
     def send(array, pairs):
         return lax.ppermute(array, 'seq', pairs)
@@ -386,9 +391,9 @@
             first = send(far_rows, from_first)
             second = send(far_rows, from_second)
             quad = send(quad_rows, next_chip)
-            pair = send(pair_rows, pair_up)
-            swapped = send(first, swap_third), send(second, swap_third)
-            return pair, (quad, send(quad, swap_upper)), (first, second, *swapped)
+            pair = send(pair_rows, swap)
+            swapped = send(first, swap), send(second, swap)
+            return pair, (quad, send(quad, swap)), (first, second, *swapped)
 
         k = project(w_key).astype(BF16)
         pair_k, quad_k, far_k = spread(pack(k, (1, 2, 4)))

time: 342 us -> 342 us (level)
  the two profiles are of different devices: /device:TPU:30 before, /device:TPU:31 now
where the time goes in v4:
time: 342 us; the launch traced here: 341 us
  Pallas kernels  133 us (39%)
  waiting for transfers between devices  73 us (21%)
  matrix products  70.2 us (21%)
  starting transfers between devices  62 us (18%)
    ppermute x17, waiting for transfers between devices, send(): return lax.ppermute(array, 'seq', pairs)  73 us
    dot_general x3, matrix products, project(): return jnp.einsum('td,dhe->hte', x, weight, preferred_element_type=F32)  70.2 us
    ppermute x17, starting transfers between devices, send(): return lax.ppermute(array, 'seq', pairs)  62 us
    pallas_call x2, Pallas kernels, local_attention(): pl.pallas_call(lambda *refs: local_kernel(first_head, *refs), grid_spec=p...  56 us
    pallas_call x1, Pallas kernels, final_attention(): pl.pallas_call(lambda *refs: final_kernel(num_heads, *refs), grid_spec=pl...  42.7 us
    pallas_call x3, Pallas kernels, pack(): pl.pallas_call(lambda *refs: pack_kernel(n_groups, *refs), grid=(num_head...  19.9 us
    pallas_call x1, Pallas kernels, sort_by_class(): pl.pallas_call(sort_kernel, grid=(tokens // CHUNK,), out_shape=jax.ShapeD...  10.4 us
  transfers between devices with their start and end apart: 17, of which 4 were waited for; matrix products, arithmetic and copies ran while one was open for 14% of the time, Pallas kernels for 21%

profile of v4, /device:TPU:31, one launch (start us, length us, event | category | flops | bytes accessed | tf_op | source)
XLA Modules:
  0.0 340.8 jit_solution(2827156895660046224)
XLA Ops:
  0.0 10.4 %sort_by_class.1 = bf16[2048,2048]{1,0:T(8,128)(2,1)} custom-call(bf16[2048,2048]{1,0:T(8,128)(2,1)} %x_ref.1), custom_call_target="tpu_custom_call" | custom-call | flops 2000000000 | bytes 16777216 | tf_op jit(solution)/shard_map/sort_by_class/pallas_call | solution.py:103
  10.4 23.4 %fusion.14 = bf16[8,256,2048]{1,2,0:T(8,128)(2,1)} fusion(bf16[2048,8,256]{2,1,0:T(8,128)(2,1)} %param.7, bf16[2048,2048]{1,0:T(8,128)(2,1)} %sort_by_class.1), kind=kOutput, calls=%fused_computation.11 | convolution fusion | flops 17184063488 | bytes 25165824 | tf_op jit(solution)/shard_map/td,dhe->hte/dot_general | solution.py:387
  33.8 7.3 %pack.3 = (bf16[8,256,256]{2,1,0:T(8,128)(2,1)}, bf16[8,512,256]{2,1,0:T(8,128)(2,1)}, bf16[8,1024,256]{2,1,0:T(8,128)(2,1)}) custom-call(bf16[8,8,8,32,256]{4,3,2,1,0:T(8,128)(2,1)} %bitcast.27, bf16[8,8,8,32,256]{4,3,2,1,0:T(8,128)(2,1)} %bitcast.28, bf16[8,8,8,32,256]{4,3,2,1,0:T(8,128)(2,1)} %bitcast.29, bf16[8,8,8,32,256]{4,3,2,1,0:T(8,128)(2,1)} %bitcast.30), custom_call_target="tpu_custom_call" | custom-call | flops 100000000 | bytes 12582912 | tf_op jit(solution)/shard_map/pack/pallas_call | solution.py:78
  41.2 0.7 collective-permute-start.3
  41.8 0.1 collective-permute-start.4
  41.9 0.4 collective-permute-start
  42.4 23.4 %fusion.9 = bf16[8,256,2048]{1,2,0:T(8,128)(2,1)} fusion(bf16[2048,8,256]{2,1,0:T(8,128)(2,1)} %param.8, bf16[2048,2048]{1,0:T(8,128)(2,1)} %sort_by_class.1), kind=kOutput, calls=%fused_computation.10 | convolution fusion | flops 17184063488 | bytes 25165824 | tf_op jit(solution)/shard_map/td,dhe->hte/dot_general | solution.py:387
  65.8 7.4 %pack.4 = (bf16[8,256,256]{2,1,0:T(8,128)(2,1)}, bf16[8,512,256]{2,1,0:T(8,128)(2,1)}, bf16[8,1024,256]{2,1,0:T(8,128)(2,1)}) custom-call(bf16[8,8,8,32,256]{4,3,2,1,0:T(8,128)(2,1)} %bitcast.33, bf16[8,8,8,32,256]{4,3,2,1,0:T(8,128)(2,1)} %bitcast.34, bf16[8,8,8,32,256]{4,3,2,1,0:T(8,128)(2,1)} %bitcast.35, bf16[8,8,8,32,256]{4,3,2,1,0:T(8,128)(2,1)} %bitcast.36), custom_call_target="tpu_custom_call" | custom-call | flops 100000000 | bytes 12582912 | tf_op jit(solution)/shard_map/pack/pallas_call | solution.py:78
  73.2 0.1 collective-permute-start.1
  73.2 0.5 collective-permute-start.8
  73.7 23.4 %multiply_convert_fusion = bf16[8,256,2048]{1,2,0:T(8,128)(2,1)} fusion(bf16[2048,8,256]{2,1,0:T(8,128)(2,1)} %param.6, bf16[2048,2048]{1,0:T(8,128)(2,1)} %sort_by_class.1), kind=kOutput, calls=%fused_computation | convolution fusion | flops 17188257792 | bytes 25165824 | tf_op jit(solution)/shard_map/td,dhe->hte/dot_general | solution.py:387
  97.1 0.0 collective-permute-done.8.refs_5_
  97.1 0.1 collective-permute-start.7
  97.2 5.2 %pack.5.qa_ref = bf16[8,256,256]{2,1,0:T(8,128)(2,1)} custom-call(bf16[8,8,8,32,256]{4,3,2,1,0:T(8,128)(2,1)} %bitcast.39), custom_call_target="tpu_custom_call" | custom-call | flops 100000000 | bytes 12582912 | tf_op jit(solution)/shard_map/pack/pallas_call | solution.py:78
  102.3 0.0 collective-permute-done.3.refs_0_
  102.3 0.0 copy-start.1
  102.4 16.6 %collective-permute-start.2 = (bf16[8,256,256]{2,1,0:T(8,128)(2,1)}, bf16[8,256,256]{2,1,0:T(8,128)(2,1)}, u32[]{:S(2)}, u32[]{:S(2)}) collective-permute-start(bf16[8,256,256]{2,1,0:T(8,128)(2,1)} %pack.5.qa_ref), channel_id=1, source_target_pairs={{6,4},{7,5},{14,12},{15,13},{22,20},{23,21},{30,28},{31,29}} | collective-permute-start | bytes 3145736 | tf_op jit(solution)/shard_map/ppermute | solution.py:375
  119.0 0.0 collective-permute-done.4.refs_1_
  119.0 0.0 copy-start.2
  119.0 1.6 collective-permute-start.10
  120.6 0.0 collective-permute-done.7.refs_4_
  120.6 0.0 copy-done.2
  120.6 0.0 copy-start.3
  120.6 1.0 copy-done.3
  121.5 14.8 %collective-permute-start.11 = (bf16[8,512,256]{2,1,0:T(8,128)(2,1)}, bf16[8,512,256]{2,1,0:T(8,128)(2,1)S(1)}, u32[]{:S(2)}, u32[]{:S(2)}) collective-permute-start(bf16[8,512,256]{2,1,0:T(8,128)(2,1)} %get-tuple-element.36), channel_id=1, source_target_pairs={{0,2},{1,3},{2,0},{3,1},{4,6},{5,7},{6,4},{7,5},{8,10},{9,11},{10,... | collective-permute-start | bytes 6291464 | tf_op jit(solution)/shard_map/ppermute | solution.py:375
  136.4 3.1 collective-permute-done.2.qb_ref
  139.5 2.2 collective-permute-start.13
  141.7 0.0 collective-permute-done.10.refs_7_
  141.7 4.3 %collective-permute-start.5 = (bf16[8,256,256]{2,1,0:T(8,128)(2,1)S(1)}, bf16[8,256,256]{2,1,0:T(8,128)(2,1)}, u32[]{:S(2)}, u32[]{:S(2)}) collective-permute-start(bf16[8,256,256]{2,1,0:T(8,128)(2,1)S(1)} %collective-permute-done.3.refs_0_), channel_id=1, source_target_pairs={{0,1},{1,0},{2,3},{3,2},{4,5},{5,4},{6,7},{7,6},{8,9},{9,8},{10,11... | collective-permute-start | bytes 3145736 | tf_op jit(solution)/shard_map/ppermute | solution.py:375
  145.9 0.0 collective-permute-done.refs_4_
  145.9 0.1 collective-permute-start.6
  146.0 0.0 collective-permute-done.1.refs_5_
  146.0 0.4 collective-permute-start.9
  146.5 0.6 pad_add_fusion.refs_0_.flag_ref
  147.1 15.9 %local_attention.2 = (bf16[8,256,2048]{2,1,0:T(8,128)(2,1)}, f32[8,256,512]{2,1,0:T(8,128)}, f32[8,8,512]{2,1,0:T(8,128)}, bf16[8,512,256]{2,1,0:T(8,128)(2,1)}) custom-call(s32[4]{0:T(128)} %pad_add_fusion.refs_0_.flag_ref, bf16[8,2048,256]{2,1,0:T(8,128)(2,1)} %bitcast.40, bf16[8,2048,256]{2,1,0:T(8,128)(2,1)} %bitcast.31, bf16[8,2048,256]{2,1,0:T(8,128)(2,1)} %bitcast.37, ...), custom_call_target="tpu_custom_call" | custom-call | flops 10000000000 | bytes 20000000 | tf_op jit(solution)/shard_map/local_attention/pallas_call | solution.py:209
  163.0 0.0 copy-done.1
  163.0 21.4 %collective-permute-done.11.refs_5_ = bf16[8,512,256]{2,1,0:T(8,128)(2,1)S(1)} collective-permute-done((bf16[8,512,256]{2,1,0:T(8,128)(2,1)}, bf16[8,512,256]{2,1,0:T(8,128)(2,1)S(1)}, u32[]{:S(2)}, u32[]{:S(2)}) %collective-permute-start.11) | collective-permute-done | bytes 2097184 | tf_op jit(solution)/shard_map/ppermute | solution.py:375
  184.4 0.0 copy-start
  184.4 4.0 %collective-permute-start.12 = (bf16[8,512,256]{2,1,0:T(8,128)(2,1)S(1)}, bf16[8,512,256]{2,1,0:T(8,128)(2,1)}, u32[]{:S(2)}, u32[]{:S(2)}) collective-permute-start(bf16[8,512,256]{2,1,0:T(8,128)(2,1)S(1)} %collective-permute-done.11.refs_5_), channel_id=1, source_target_pairs={{0,1},{1,0},{2,3},{3,2},{4,5},{5,4},{6,7},{7,6},{8,9},{9,8},{10,11... | collective-permute-start | bytes 6291464 | tf_op jit(solution)/shard_map/ppermute | solution.py:375
  188.4 41.0 %collective-permute-done.13.refs_7_ = bf16[8,512,256]{2,1,0:T(8,128)(2,1)} collective-permute-done((bf16[8,512,256]{2,1,0:T(8,128)(2,1)}, bf16[8,512,256]{2,1,0:T(8,128)(2,1)}, u32[]{:S(2)}, u32[]{:S(2)}) %collective-permute-start.13) | collective-permute-done | bytes 2097184 | tf_op jit(solution)/shard_map/ppermute | solution.py:375
  229.4 2.2 collective-permute-start.14
  231.6 0.0 collective-permute-done.5.refs_2_
  231.6 0.0 collective-permute-done.6.refs_3_
  231.6 0.0 collective-permute-done.9.refs_6_
  231.6 4.3 %far_attention.1 = (f32[8,256,256]{2,1,0:T(8,128)}, f32[8,8,256]{2,1,0:T(8,128)}, f32[8,256,256]{2,1,0:T(8,128)}, f32[8,8,256]{2,1,0:T(8,128)}) custom-call(s32[4]{0:T(128)} %pad_add_fusion.refs_0_.flag_ref, bf16[8,256,256]{2,1,0:T(8,128)(2,1)} %pack.5.qa_ref, bf16[8,256,256]{2,1,0:T(8,128)(2,1)} %collective-permute-done.2.qb_ref, ...), custom_call_target="tpu_custom_call" | custom-call | flops 5000000000 | bytes 20000000 | tf_op jit(solution)/shard_map/far_attention/pallas_call | solution.py:255
  235.8 0.0 copy-done
  235.8 14.0 %collective-permute-start.15 = (f32[8,256,256]{2,1,0:T(8,128)}, f32[8,256,256]{2,1,0:T(8,128)}, u32[]{:S(2)}, u32[]{:S(2)}) collective-permute-start(f32[8,256,256]{2,1,0:T(8,128)} %get-tuple-element.39), channel_id=1, source_target_pairs={{4,6},{6,4},{5,7},{7,5},{0,1},{1,0},{2,3},{3,2},{12,14},{14,12},{1... | collective-permute-start | bytes 6291464 | tf_op jit(solution)/shard_map/ppermute | solution.py:375
  249.8 0.1 collective-permute-start.16
  249.9 40.0 %local_attention.3 = (bf16[8,256,2048]{2,1,0:T(8,128)(2,1)}, f32[8,256,512]{2,1,0:T(8,128)}, f32[8,8,512]{2,1,0:T(8,128)}, bf16[8,512,256]{2,1,0:T(8,128)(2,1)}) custom-call(s32[4]{0:T(128)} %pad_add_fusion.refs_0_.flag_ref, bf16[8,2048,256]{2,1,0:T(8,128)(2,1)} %bitcast.41, ...), custom_call_target="tpu_custom_call", output_to_operand_aliasing={{0}: (6, {}), {1}: (7, {}), {2}: (8, {}), {3}: (9, {})} | custom-call | flops 30000001024 | bytes 60000000 | tf_op jit(solution)/shard_map/local_attention/pallas_call | solution.py:209
  290.0 0.0 collective-permute-done.12.refs_6_
  290.0 0.0 collective-permute-done.14.refs_8_
  290.0 7.5 %collective-permute-done.16.refs_12_ = f32[8,8,256]{2,1,0:T(8,128)S(1)} collective-permute-done((f32[8,8,256]{2,1,0:T(8,128)}, f32[8,8,256]{2,1,0:T(8,128)S(1)}, u32[]{:S(2)}, u32[]{:S(2)}) %collective-permute-start.16) | collective-permute-done | bytes 65568 | tf_op jit(solution)/shard_map/ppermute | solution.py:375
  297.4 0.0 copy-start.4
  297.4 0.0 collective-permute-done.15.refs_11_
  297.4 0.6 copy-done.4
  298.1 42.7 %final_attention.1 = bf16[2048,2048]{1,0:T(8,128)(2,1)} custom-call(s32[4]{0:T(128)} %pad_add_fusion.refs_0_.flag_ref, bf16[8,512,256]{2,1,0:T(8,128)(2,1)} %get-tuple-element.32.refs_1_, bf16[8,256,2048]{2,1,0:T(8,128)(2,1)} %get-tuple-element.33.refs_2_, f32[8,256,512]{2,1,0:T(8,128)} %get-tuple-element.34.refs_3_, ...), custom_call_target="tpu_custom_call" | custom-call | flops 30000001024 | bytes 60000000 | tf_op jit(solution)/shard_map/final_attention/pallas_call | solution.py:349
Async XLA Ops:
  41.2 61.2 %collective-permute-start.3 = (bf16[8,256,256]{2,1,0:T(8,128)(2,1)}, bf16[8,256,256]{2,1,0:T(8,128)(2,1)S(1)}, u32[]{:S(2)}, u32[]{:S(2)}) collective-permute-start(bf16[8,256,256]{2,1,0:T(8,128)(2,1)} %get-tuple-element.29), channel_id=1, source_target_pairs={{0,4},{4,0},{1,5},{5,1},{2,3},{3,2},{6,7},{7,6},{8,12},{12,8},{9,1... | collective-permute-start | bytes 3145736 | tf_op jit(solution)/shard_map/ppermute | solution.py:375
  41.8 77.1 %collective-permute-start.4 = (bf16[8,256,256]{2,1,0:T(8,128)(2,1)}, bf16[8,256,256]{2,1,0:T(8,128)(2,1)S(1)}, u32[]{:S(2)}, u32[]{:S(2)}) collective-permute-start(bf16[8,256,256]{2,1,0:T(8,128)(2,1)} %get-tuple-element.29), channel_id=1, source_target_pairs={{2,4},{4,2},{3,5},{5,3},{0,1},{1,0},{6,7},{7,6},{10,12},{12,10},{1... | collective-permute-start | bytes 3145736 | tf_op jit(solution)/shard_map/ppermute | solution.py:375
  41.9 104.0 %collective-permute-start = (bf16[8,1024,256]{2,1,0:T(8,128)(2,1)}, bf16[8,1024,256]{2,1,0:T(8,128)(2,1)}, u32[]{:S(2)}, u32[]{:S(2)}) collective-permute-start(bf16[8,1024,256]{2,1,0:T(8,128)(2,1)} %get-tuple-element.23), channel_id=1, source_target_pairs={{0,1},{1,0},{2,3},{3,2},{4,5},{5,4},{6,7},{7,6},{8,9},{9,8},{10,11... | collective-permute-start | bytes 12582920 | tf_op jit(solution)/shard_map/ppermute | solution.py:375
  73.2 72.9 %collective-permute-start.1 = (bf16[8,1024,256]{2,1,0:T(8,128)(2,1)}, bf16[8,1024,256]{2,1,0:T(8,128)(2,1)}, u32[]{:S(2)}, u32[]{:S(2)}) collective-permute-start(bf16[8,1024,256]{2,1,0:T(8,128)(2,1)} %get-tuple-element.24), channel_id=1, source_target_pairs={{0,1},{1,0},{2,3},{3,2},{4,5},{5,4},{6,7},{7,6},{8,9},{9,8},{10,11... | collective-permute-start | bytes 12582920 | tf_op jit(solution)/shard_map/ppermute | solution.py:375
  73.2 23.9 %collective-permute-start.8 = (bf16[8,256,256]{2,1,0:T(8,128)(2,1)}, bf16[8,256,256]{2,1,0:T(8,128)(2,1)}, u32[]{:S(2)}, u32[]{:S(2)}) collective-permute-start(bf16[8,256,256]{2,1,0:T(8,128)(2,1)} %get-tuple-element.30), channel_id=1, source_target_pairs={{2,4},{4,2},{3,5},{5,3},{0,1},{1,0},{6,7},{7,6},{10,12},{12,10},{1... | collective-permute-start | bytes 3145736 | tf_op jit(solution)/shard_map/ppermute | solution.py:375
  97.1 23.5 %collective-permute-start.7 = (bf16[8,256,256]{2,1,0:T(8,128)(2,1)}, bf16[8,256,256]{2,1,0:T(8,128)(2,1)S(1)}, u32[]{:S(2)}, u32[]{:S(2)}) collective-permute-start(bf16[8,256,256]{2,1,0:T(8,128)(2,1)} %get-tuple-element.30), channel_id=1, source_target_pairs={{0,4},{4,0},{1,5},{5,1},{2,3},{3,2},{6,7},{7,6},{8,12},{12,8},{9,1... | collective-permute-start | bytes 3145736 | tf_op jit(solution)/shard_map/ppermute | solution.py:375
  102.3 60.6 %copy-start.1 = (bf16[8,256,256]{2,1,0:T(8,128)(2,1)}, bf16[8,256,256]{2,1,0:T(8,128)(2,1)S(1)}, u32[]{:S(2)}) copy-start(bf16[8,256,256]{2,1,0:T(8,128)(2,1)S(1)} %collective-permute-done.3.refs_0_) | copy-start | bytes 3145732
  102.4 37.1 %collective-permute-start.2 = (bf16[8,256,256]{2,1,0:T(8,128)(2,1)}, bf16[8,256,256]{2,1,0:T(8,128)(2,1)}, u32[]{:S(2)}, u32[]{:S(2)}) collective-permute-start(bf16[8,256,256]{2,1,0:T(8,128)(2,1)} %pack.5.qa_ref), channel_id=1, source_target_pairs={{6,4},{7,5},{14,12},{15,13},{22,20},{23,21},{30,28},{31,29}} | collective-permute-start | bytes 3145736 | tf_op jit(solution)/shard_map/ppermute | solution.py:375
  119.0 1.6 copy-start.2
  119.0 22.7 %collective-permute-start.10 = (bf16[8,256,256]{2,1,0:T(8,128)(2,1)}, bf16[8,256,256]{2,1,0:T(8,128)(2,1)}, u32[]{:S(2)}, u32[]{:S(2)}) collective-permute-start(bf16[8,256,256]{2,1,0:T(8,128)(2,1)} %collective-permute-done.8.refs_5_), channel_id=1, source_target_pairs={{0,1},{1,0},{2,3},{3,2},{4,5},{5,4},{6,7},{7,6},{8,9},{9,8},{10,11... | collective-permute-start | bytes 3145736 | tf_op jit(solution)/shard_map/ppermute | solution.py:375
  120.6 1.0 copy-start.3
  121.5 62.9 %collective-permute-start.11 = (bf16[8,512,256]{2,1,0:T(8,128)(2,1)}, bf16[8,512,256]{2,1,0:T(8,128)(2,1)S(1)}, u32[]{:S(2)}, u32[]{:S(2)}) collective-permute-start(bf16[8,512,256]{2,1,0:T(8,128)(2,1)} %get-tuple-element.36), channel_id=1, source_target_pairs={{0,2},{1,3},{2,0},{3,1},{4,6},{5,7},{6,4},{7,5},{8,10},{9,11},{10,... | collective-permute-start | bytes 6291464 | tf_op jit(solution)/shard_map/ppermute | solution.py:375
  139.5 89.9 %collective-permute-start.13 = (bf16[8,512,256]{2,1,0:T(8,128)(2,1)}, bf16[8,512,256]{2,1,0:T(8,128)(2,1)}, u32[]{:S(2)}, u32[]{:S(2)}) collective-permute-start(bf16[8,512,256]{2,1,0:T(8,128)(2,1)} %get-tuple-element.37), channel_id=1, source_target_pairs={{0,2},{1,3},{2,0},{3,1},{4,6},{5,7},{6,4},{7,5},{8,10},{9,11},{10,... | collective-permute-start | bytes 6291464 | tf_op jit(solution)/shard_map/ppermute | solution.py:375
  141.7 89.9 %collective-permute-start.5 = (bf16[8,256,256]{2,1,0:T(8,128)(2,1)S(1)}, bf16[8,256,256]{2,1,0:T(8,128)(2,1)}, u32[]{:S(2)}, u32[]{:S(2)}) collective-permute-start(bf16[8,256,256]{2,1,0:T(8,128)(2,1)S(1)} %collective-permute-done.3.refs_0_), channel_id=1, source_target_pairs={{0,1},{1,0},{2,3},{3,2},{4,5},{5,4},{6,7},{7,6},{8,9},{9,8},{10,11... | collective-permute-start | bytes 3145736 | tf_op jit(solution)/shard_map/ppermute | solution.py:375
  145.9 85.6 %collective-permute-start.6 = (bf16[8,256,256]{2,1,0:T(8,128)(2,1)}, bf16[8,256,256]{2,1,0:T(8,128)(2,1)}, u32[]{:S(2)}, u32[]{:S(2)}) collective-permute-start(bf16[8,256,256]{2,1,0:T(8,128)(2,1)} %copy-done.2), channel_id=1, source_target_pairs={{0,1},{1,0},{2,3},{3,2},{4,5},{5,4},{6,7},{7,6},{8,9},{9,8},{10,11... | collective-permute-start | bytes 3145736 | tf_op jit(solution)/shard_map/ppermute | solution.py:375
  146.0 85.5 %collective-permute-start.9 = (bf16[8,256,256]{2,1,0:T(8,128)(2,1)}, bf16[8,256,256]{2,1,0:T(8,128)(2,1)}, u32[]{:S(2)}, u32[]{:S(2)}) collective-permute-start(bf16[8,256,256]{2,1,0:T(8,128)(2,1)} %copy-done.3), channel_id=1, source_target_pairs={{0,1},{1,0},{2,3},{3,2},{4,5},{5,4},{6,7},{7,6},{8,9},{9,8},{10,11... | collective-permute-start | bytes 3145736 | tf_op jit(solution)/shard_map/ppermute | solution.py:375
  184.4 51.4 %copy-start = (bf16[8,512,256]{2,1,0:T(8,128)(2,1)}, bf16[8,512,256]{2,1,0:T(8,128)(2,1)S(1)}, u32[]{:S(2)}) copy-start(bf16[8,512,256]{2,1,0:T(8,128)(2,1)S(1)} %collective-permute-done.11.refs_5_) | copy-start | bytes 6291460
  184.4 105.5 %collective-permute-start.12 = (bf16[8,512,256]{2,1,0:T(8,128)(2,1)S(1)}, bf16[8,512,256]{2,1,0:T(8,128)(2,1)}, u32[]{:S(2)}, u32[]{:S(2)}) collective-permute-start(bf16[8,512,256]{2,1,0:T(8,128)(2,1)S(1)} %collective-permute-done.11.refs_5_), channel_id=1, source_target_pairs={{0,1},{1,0},{2,3},{3,2},{4,5},{5,4},{6,7},{7,6},{8,9},{9,8},{10,11... | collective-permute-start | bytes 6291464 | tf_op jit(solution)/shard_map/ppermute | solution.py:375
  229.4 60.6 %collective-permute-start.14 = (bf16[8,512,256]{2,1,0:T(8,128)(2,1)}, bf16[8,512,256]{2,1,0:T(8,128)(2,1)}, u32[]{:S(2)}, u32[]{:S(2)}) collective-permute-start(bf16[8,512,256]{2,1,0:T(8,128)(2,1)} %collective-permute-done.13.refs_7_), channel_id=1, source_target_pairs={{0,1},{1,0},{2,3},{3,2},{4,5},{5,4},{6,7},{7,6},{8,9},{9,8},{10,11... | collective-permute-start | bytes 6291464 | tf_op jit(solution)/shard_map/ppermute | solution.py:375
  235.8 61.6 %collective-permute-start.15 = (f32[8,256,256]{2,1,0:T(8,128)}, f32[8,256,256]{2,1,0:T(8,128)}, u32[]{:S(2)}, u32[]{:S(2)}) collective-permute-start(f32[8,256,256]{2,1,0:T(8,128)} %get-tuple-element.39), channel_id=1, source_target_pairs={{4,6},{6,4},{5,7},{7,5},{0,1},{1,0},{2,3},{3,2},{12,14},{14,12},{1... | collective-permute-start | bytes 6291464 | tf_op jit(solution)/shard_map/ppermute | solution.py:375
  249.8 47.6 %collective-permute-start.16 = (f32[8,8,256]{2,1,0:T(8,128)}, f32[8,8,256]{2,1,0:T(8,128)S(1)}, u32[]{:S(2)}, u32[]{:S(2)}) collective-permute-start(f32[8,8,256]{2,1,0:T(8,128)} %get-tuple-element.40), channel_id=1, source_target_pairs={{4,6},{6,4},{5,7},{7,5},{0,1},{1,0},{2,3},{3,2},{12,14},{14,12},{1... | collective-permute-start | bytes 196616 | tf_op jit(solution)/shard_map/ppermute | solution.py:375
  297.4 0.6 copy-start.4

commit v5 on v4

--- a/solution.py
+++ b/solution.py
@@ -365,11 +365,11 @@
 def solution(mesh):
     row_spec = P(('dp', 'seq'), None)
     swap = [(s, s ^ 1) for s in range(8)]
-    next_chip = [(s, s ^ 2) for s in range(8)]
-    from_first = [(0, 4), (4, 0), (1, 5), (5, 1), (2, 3), (3, 2), (6, 7), (7, 6)]
-    from_second = [(2, 4), (4, 2), (3, 5), (5, 3), (0, 1), (1, 0), (6, 7), (7, 6)]
+    next_chip = [(0, 2), (1, 3), (4, 6), (5, 7)]
+    from_first = [(0, 4), (1, 5), (2, 3), (3, 2), (6, 7), (7, 6)]
+    from_second = [(2, 4), (3, 5), (0, 1), (1, 0), (6, 7), (7, 6)]
     to_third = [(6, 4), (7, 5)]
-    to_fourth = [(4, 6), (6, 4), (5, 7), (7, 5), (0, 1), (1, 0), (2, 3), (3, 2)]
+    to_fourth = [(4, 6), (5, 7), (0, 1), (1, 0), (2, 3), (3, 2)]
 
     def send(array, pairs):
         return lax.ppermute(array, 'seq', pairs)

time: 342 us -> 344 us (level)
  waiting for transfers between devices: 73 us -> 101 us
  starting transfers between devices: 62 us -> 36.8 us
    ppermute x17, waiting for transfers between devices: 73 us -> 101 us  [send(): return lax.ppermute(array, 'seq', pairs)]
    ppermute x17, starting transfers between devices: 62 us -> 36.8 us  [send(): return lax.ppermute(array, 'seq', pairs)]
where the time goes in v5:
time: 344 us; the launch traced here: 343 us
  Pallas kernels  133 us (39%)
  waiting for transfers between devices  101 us (29%)
  matrix products  70.3 us (20%)
  starting transfers between devices  36.8 us (11%)
    ppermute x17, waiting for transfers between devices, send(): return lax.ppermute(array, 'seq', pairs)  101 us
    dot_general x3, matrix products, project(): return jnp.einsum('td,dhe->hte', x, weight, preferred_element_type=F32)  70.3 us
    pallas_call x2, Pallas kernels, local_attention(): pl.pallas_call(lambda *refs: local_kernel(first_head, *refs), grid_spec=p...  55.7 us
    pallas_call x1, Pallas kernels, final_attention(): pl.pallas_call(lambda *refs: final_kernel(num_heads, *refs), grid_spec=pl...  42.8 us
    ppermute x17, starting transfers between devices, send(): return lax.ppermute(array, 'seq', pairs)  36.8 us
    pallas_call x3, Pallas kernels, pack(): pl.pallas_call(lambda *refs: pack_kernel(n_groups, *refs), grid=(num_head...  19.9 us
    pallas_call x1, Pallas kernels, sort_by_class(): pl.pallas_call(sort_kernel, grid=(tokens // CHUNK,), out_shape=jax.ShapeD...  10.4 us
  transfers between devices with their start and end apart: 17, of which 4 were waited for; matrix products, arithmetic and copies ran while one was open for 14% of the time, Pallas kernels for 21%

profile of v5, /device:TPU:31, one launch (start us, length us, event | category | flops | bytes accessed | tf_op | source)
XLA Modules:
  0.0 343.3 jit_solution(2616800503430756159)
XLA Ops:
  0.0 10.4 %sort_by_class.1 = bf16[2048,2048]{1,0:T(8,128)(2,1)} custom-call(bf16[2048,2048]{1,0:T(8,128)(2,1)} %x_ref.1), custom_call_target="tpu_custom_call" | custom-call | flops 2000000000 | bytes 16777216 | tf_op jit(solution)/shard_map/sort_by_class/pallas_call | solution.py:103
  10.4 23.4 %fusion.14 = bf16[8,256,2048]{1,2,0:T(8,128)(2,1)} fusion(bf16[2048,8,256]{2,1,0:T(8,128)(2,1)} %param.7, bf16[2048,2048]{1,0:T(8,128)(2,1)} %sort_by_class.1), kind=kOutput, calls=%fused_computation.11 | convolution fusion | flops 17184063488 | bytes 25165824 | tf_op jit(solution)/shard_map/td,dhe->hte/dot_general | solution.py:387
  33.8 7.3 %pack.3 = (bf16[8,256,256]{2,1,0:T(8,128)(2,1)}, bf16[8,512,256]{2,1,0:T(8,128)(2,1)}, bf16[8,1024,256]{2,1,0:T(8,128)(2,1)}) custom-call(bf16[8,8,8,32,256]{4,3,2,1,0:T(8,128)(2,1)} %bitcast.27, bf16[8,8,8,32,256]{4,3,2,1,0:T(8,128)(2,1)} %bitcast.28, bf16[8,8,8,32,256]{4,3,2,1,0:T(8,128)(2,1)} %bitcast.29, bf16[8,8,8,32,256]{4,3,2,1,0:T(8,128)(2,1)} %bitcast.30), custom_call_target="tpu_custom_call" | custom-call | flops 100000000 | bytes 12582912 | tf_op jit(solution)/shard_map/pack/pallas_call | solution.py:78
  41.2 2.6 collective-permute-start.3
  43.7 1.9 collective-permute-start.4
  45.7 0.6 collective-permute-start
  46.2 23.4 %fusion.9 = bf16[8,256,2048]{1,2,0:T(8,128)(2,1)} fusion(bf16[2048,8,256]{2,1,0:T(8,128)(2,1)} %param.8, bf16[2048,2048]{1,0:T(8,128)(2,1)} %sort_by_class.1), kind=kOutput, calls=%fused_computation.10 | convolution fusion | flops 17184063488 | bytes 25165824 | tf_op jit(solution)/shard_map/td,dhe->hte/dot_general | solution.py:387
  69.7 7.4 %pack.4 = (bf16[8,256,256]{2,1,0:T(8,128)(2,1)}, bf16[8,512,256]{2,1,0:T(8,128)(2,1)}, bf16[8,1024,256]{2,1,0:T(8,128)(2,1)}) custom-call(bf16[8,8,8,32,256]{4,3,2,1,0:T(8,128)(2,1)} %bitcast.33, bf16[8,8,8,32,256]{4,3,2,1,0:T(8,128)(2,1)} %bitcast.34, bf16[8,8,8,32,256]{4,3,2,1,0:T(8,128)(2,1)} %bitcast.35, bf16[8,8,8,32,256]{4,3,2,1,0:T(8,128)(2,1)} %bitcast.36), custom_call_target="tpu_custom_call" | custom-call | flops 100000000 | bytes 12582912 | tf_op jit(solution)/shard_map/pack/pallas_call | solution.py:78
  77.0 0.0 collective-permute-start.1
  77.1 2.4 collective-permute-start.8
  79.5 23.4 %multiply_convert_fusion = bf16[8,256,2048]{1,2,0:T(8,128)(2,1)} fusion(bf16[2048,8,256]{2,1,0:T(8,128)(2,1)} %param.6, bf16[2048,2048]{1,0:T(8,128)(2,1)} %sort_by_class.1), kind=kOutput, calls=%fused_computation | convolution fusion | flops 17188257792 | bytes 25165824 | tf_op jit(solution)/shard_map/td,dhe->hte/dot_general | solution.py:387
  102.9 0.0 collective-permute-done.8.refs_5_
  102.9 1.9 collective-permute-start.7
  104.8 5.2 %pack.5.qa_ref = bf16[8,256,256]{2,1,0:T(8,128)(2,1)} custom-call(bf16[8,8,8,32,256]{4,3,2,1,0:T(8,128)(2,1)} %bitcast.39), custom_call_target="tpu_custom_call" | custom-call | flops 100000000 | bytes 12582912 | tf_op jit(solution)/shard_map/pack/pallas_call | solution.py:78
  110.0 0.0 collective-permute-done.3.refs_0_
  110.0 0.0 copy-start.1
  110.0 13.8 %collective-permute-start.2 = (bf16[8,256,256]{2,1,0:T(8,128)(2,1)}, bf16[8,256,256]{2,1,0:T(8,128)(2,1)}, u32[]{:S(2)}, u32[]{:S(2)}) collective-permute-start(bf16[8,256,256]{2,1,0:T(8,128)(2,1)} %pack.5.qa_ref), channel_id=1, source_target_pairs={{6,4},{7,5},{14,12},{15,13},{22,20},{23,21},{30,28},{31,29}} | collective-permute-start | bytes 3145736 | tf_op jit(solution)/shard_map/ppermute | solution.py:375
  123.8 0.0 collective-permute-done.4.refs_1_
  123.8 0.0 copy-start.2
  123.8 0.8 collective-permute-start.10
  124.6 0.0 collective-permute-done.7.refs_4_
  124.6 0.2 copy-done.2
  124.8 0.0 copy-start.3
  124.8 0.9 copy-done.3
  125.8 1.3 collective-permute-start.11
  127.1 18.1 %collective-permute-done.2.qb_ref = bf16[8,256,256]{2,1,0:T(8,128)(2,1)} collective-permute-done((bf16[8,256,256]{2,1,0:T(8,128)(2,1)}, bf16[8,256,256]{2,1,0:T(8,128)(2,1)}, u32[]{:S(2)}, u32[]{:S(2)}) %collective-permute-start.2) | collective-permute-done | bytes 1048608 | tf_op jit(solution)/shard_map/ppermute | solution.py:375
  145.2 1.5 collective-permute-start.13
  146.7 0.0 collective-permute-done.10.refs_7_
  146.7 1.4 collective-permute-start.5
  148.1 0.0 collective-permute-done.refs_4_
  148.1 0.1 collective-permute-start.6
  148.2 0.0 collective-permute-done.1.refs_5_
  148.2 0.4 collective-permute-start.9
  148.6 0.6 pad_add_fusion.refs_0_.flag_ref
  149.3 15.9 %local_attention.2 = (bf16[8,256,2048]{2,1,0:T(8,128)(2,1)}, f32[8,256,512]{2,1,0:T(8,128)}, f32[8,8,512]{2,1,0:T(8,128)}, bf16[8,512,256]{2,1,0:T(8,128)(2,1)}) custom-call(s32[4]{0:T(128)} %pad_add_fusion.refs_0_.flag_ref, bf16[8,2048,256]{2,1,0:T(8,128)(2,1)} %bitcast.40, bf16[8,2048,256]{2,1,0:T(8,128)(2,1)} %bitcast.31, bf16[8,2048,256]{2,1,0:T(8,128)(2,1)} %bitcast.37, ...), custom_call_target="tpu_custom_call" | custom-call | flops 10000000000 | bytes 20000000 | tf_op jit(solution)/shard_map/local_attention/pallas_call | solution.py:209
  165.2 0.0 copy-done.1
  165.2 23.6 %collective-permute-done.11.refs_5_ = bf16[8,512,256]{2,1,0:T(8,128)(2,1)S(1)} collective-permute-done((bf16[8,512,256]{2,1,0:T(8,128)(2,1)}, bf16[8,512,256]{2,1,0:T(8,128)(2,1)S(1)}, u32[]{:S(2)}, u32[]{:S(2)}) %collective-permute-start.11) | collective-permute-done | bytes 2097184 | tf_op jit(solution)/shard_map/ppermute | solution.py:375
  188.8 0.0 copy-start
  188.8 3.5 %collective-permute-start.12 = (bf16[8,512,256]{2,1,0:T(8,128)(2,1)S(1)}, bf16[8,512,256]{2,1,0:T(8,128)(2,1)}, u32[]{:S(2)}, u32[]{:S(2)}) collective-permute-start(bf16[8,512,256]{2,1,0:T(8,128)(2,1)S(1)} %collective-permute-done.11.refs_5_), channel_id=1, source_target_pairs={{0,1},{1,0},{2,3},{3,2},{4,5},{5,4},{6,7},{7,6},{8,9},{9,8},{10,11... | collective-permute-start | bytes 6291464 | tf_op jit(solution)/shard_map/ppermute | solution.py:375
  192.2 41.6 %collective-permute-done.13.refs_7_ = bf16[8,512,256]{2,1,0:T(8,128)(2,1)} collective-permute-done((bf16[8,512,256]{2,1,0:T(8,128)(2,1)}, bf16[8,512,256]{2,1,0:T(8,128)(2,1)}, u32[]{:S(2)}, u32[]{:S(2)}) %collective-permute-start.13) | collective-permute-done | bytes 2097184 | tf_op jit(solution)/shard_map/ppermute | solution.py:375
  233.8 1.9 collective-permute-start.14
  235.7 0.0 collective-permute-done.5.refs_2_
  235.7 0.0 collective-permute-done.6.refs_3_
  235.7 0.0 collective-permute-done.9.refs_6_
  235.7 4.3 %far_attention.1 = (f32[8,256,256]{2,1,0:T(8,128)}, f32[8,8,256]{2,1,0:T(8,128)}, f32[8,256,256]{2,1,0:T(8,128)}, f32[8,8,256]{2,1,0:T(8,128)}) custom-call(s32[4]{0:T(128)} %pad_add_fusion.refs_0_.flag_ref, bf16[8,256,256]{2,1,0:T(8,128)(2,1)} %pack.5.qa_ref, bf16[8,256,256]{2,1,0:T(8,128)(2,1)} %collective-permute-done.2.qb_ref, ...), custom_call_target="tpu_custom_call" | custom-call | flops 5000000000 | bytes 20000000 | tf_op jit(solution)/shard_map/far_attention/pallas_call | solution.py:255
  240.0 0.0 copy-done
  240.0 1.3 collective-permute-start.15
  241.3 1.5 collective-permute-start.16
  242.8 39.8 %local_attention.3 = (bf16[8,256,2048]{2,1,0:T(8,128)(2,1)}, f32[8,256,512]{2,1,0:T(8,128)}, f32[8,8,512]{2,1,0:T(8,128)}, bf16[8,512,256]{2,1,0:T(8,128)(2,1)}) custom-call(s32[4]{0:T(128)} %pad_add_fusion.refs_0_.flag_ref, bf16[8,2048,256]{2,1,0:T(8,128)(2,1)} %bitcast.41, ...), custom_call_target="tpu_custom_call", output_to_operand_aliasing={{0}: (6, {}), {1}: (7, {}), {2}: (8, {}), {3}: (9, {})} | custom-call | flops 30000001024 | bytes 60000000 | tf_op jit(solution)/shard_map/local_attention/pallas_call | solution.py:209
  282.7 0.0 collective-permute-done.12.refs_6_
  282.7 0.0 collective-permute-done.14.refs_8_
  282.7 17.2 %collective-permute-done.16.refs_12_ = f32[8,8,256]{2,1,0:T(8,128)S(1)} collective-permute-done((f32[8,8,256]{2,1,0:T(8,128)}, f32[8,8,256]{2,1,0:T(8,128)S(1)}, u32[]{:S(2)}, u32[]{:S(2)}) %collective-permute-start.16) | collective-permute-done | bytes 65568 | tf_op jit(solution)/shard_map/ppermute | solution.py:375
  299.9 0.0 copy-start.4
  299.9 0.0 collective-permute-done.15.refs_11_
  299.9 0.6 copy-done.4
  300.5 42.8 %final_attention.1 = bf16[2048,2048]{1,0:T(8,128)(2,1)} custom-call(s32[4]{0:T(128)} %pad_add_fusion.refs_0_.flag_ref, bf16[8,512,256]{2,1,0:T(8,128)(2,1)} %get-tuple-element.32.refs_1_, bf16[8,256,2048]{2,1,0:T(8,128)(2,1)} %get-tuple-element.33.refs_2_, f32[8,256,512]{2,1,0:T(8,128)} %get-tuple-element.34.refs_3_, ...), custom_call_target="tpu_custom_call" | custom-call | flops 30000001024 | bytes 60000000 | tf_op jit(solution)/shard_map/final_attention/pallas_call | solution.py:349
Async XLA Ops:
  41.2 68.9 %collective-permute-start.3 = (bf16[8,256,256]{2,1,0:T(8,128)(2,1)}, bf16[8,256,256]{2,1,0:T(8,128)(2,1)S(1)}, u32[]{:S(2)}, u32[]{:S(2)}) collective-permute-start(bf16[8,256,256]{2,1,0:T(8,128)(2,1)} %get-tuple-element.29), channel_id=1, source_target_pairs={{0,4},{1,5},{2,3},{3,2},{6,7},{7,6},{8,12},{9,13},{10,11},{11,10},... | collective-permute-start | bytes 3145736 | tf_op jit(solution)/shard_map/ppermute | solution.py:375
  43.7 80.1 %collective-permute-start.4 = (bf16[8,256,256]{2,1,0:T(8,128)(2,1)}, bf16[8,256,256]{2,1,0:T(8,128)(2,1)S(1)}, u32[]{:S(2)}, u32[]{:S(2)}) collective-permute-start(bf16[8,256,256]{2,1,0:T(8,128)(2,1)} %get-tuple-element.29), channel_id=1, source_target_pairs={{2,4},{3,5},{0,1},{1,0},{6,7},{7,6},{10,12},{11,13},{8,9},{9,8},{1... | collective-permute-start | bytes 3145736 | tf_op jit(solution)/shard_map/ppermute | solution.py:375
  45.7 102.4 %collective-permute-start = (bf16[8,1024,256]{2,1,0:T(8,128)(2,1)}, bf16[8,1024,256]{2,1,0:T(8,128)(2,1)}, u32[]{:S(2)}, u32[]{:S(2)}) collective-permute-start(bf16[8,1024,256]{2,1,0:T(8,128)(2,1)} %get-tuple-element.23), channel_id=1, source_target_pairs={{0,1},{1,0},{2,3},{3,2},{4,5},{5,4},{6,7},{7,6},{8,9},{9,8},{10,11... | collective-permute-start | bytes 12582920 | tf_op jit(solution)/shard_map/ppermute | solution.py:375
  77.0 71.2 %collective-permute-start.1 = (bf16[8,1024,256]{2,1,0:T(8,128)(2,1)}, bf16[8,1024,256]{2,1,0:T(8,128)(2,1)}, u32[]{:S(2)}, u32[]{:S(2)}) collective-permute-start(bf16[8,1024,256]{2,1,0:T(8,128)(2,1)} %get-tuple-element.24), channel_id=1, source_target_pairs={{0,1},{1,0},{2,3},{3,2},{4,5},{5,4},{6,7},{7,6},{8,9},{9,8},{10,11... | collective-permute-start | bytes 12582920 | tf_op jit(solution)/shard_map/ppermute | solution.py:375
  77.1 25.8 %collective-permute-start.8 = (bf16[8,256,256]{2,1,0:T(8,128)(2,1)}, bf16[8,256,256]{2,1,0:T(8,128)(2,1)}, u32[]{:S(2)}, u32[]{:S(2)}) collective-permute-start(bf16[8,256,256]{2,1,0:T(8,128)(2,1)} %get-tuple-element.30), channel_id=1, source_target_pairs={{2,4},{3,5},{0,1},{1,0},{6,7},{7,6},{10,12},{11,13},{8,9},{9,8},{1... | collective-permute-start | bytes 3145736 | tf_op jit(solution)/shard_map/ppermute | solution.py:375
  102.9 21.7 %collective-permute-start.7 = (bf16[8,256,256]{2,1,0:T(8,128)(2,1)}, bf16[8,256,256]{2,1,0:T(8,128)(2,1)S(1)}, u32[]{:S(2)}, u32[]{:S(2)}) collective-permute-start(bf16[8,256,256]{2,1,0:T(8,128)(2,1)} %get-tuple-element.30), channel_id=1, source_target_pairs={{0,4},{1,5},{2,3},{3,2},{6,7},{7,6},{8,12},{9,13},{10,11},{11,10},... | collective-permute-start | bytes 3145736 | tf_op jit(solution)/shard_map/ppermute | solution.py:375
  110.0 55.1 %copy-start.1 = (bf16[8,256,256]{2,1,0:T(8,128)(2,1)}, bf16[8,256,256]{2,1,0:T(8,128)(2,1)S(1)}, u32[]{:S(2)}) copy-start(bf16[8,256,256]{2,1,0:T(8,128)(2,1)S(1)} %collective-permute-done.3.refs_0_) | copy-start | bytes 3145732
  110.0 35.1 %collective-permute-start.2 = (bf16[8,256,256]{2,1,0:T(8,128)(2,1)}, bf16[8,256,256]{2,1,0:T(8,128)(2,1)}, u32[]{:S(2)}, u32[]{:S(2)}) collective-permute-start(bf16[8,256,256]{2,1,0:T(8,128)(2,1)} %pack.5.qa_ref), channel_id=1, source_target_pairs={{6,4},{7,5},{14,12},{15,13},{22,20},{23,21},{30,28},{31,29}} | collective-permute-start | bytes 3145736 | tf_op jit(solution)/shard_map/ppermute | solution.py:375
  123.8 1.0 copy-start.2
  123.8 22.9 %collective-permute-start.10 = (bf16[8,256,256]{2,1,0:T(8,128)(2,1)}, bf16[8,256,256]{2,1,0:T(8,128)(2,1)}, u32[]{:S(2)}, u32[]{:S(2)}) collective-permute-start(bf16[8,256,256]{2,1,0:T(8,128)(2,1)} %collective-permute-done.8.refs_5_), channel_id=1, source_target_pairs={{0,1},{1,0},{2,3},{3,2},{4,5},{5,4},{6,7},{7,6},{8,9},{9,8},{10,11... | collective-permute-start | bytes 3145736 | tf_op jit(solution)/shard_map/ppermute | solution.py:375
  124.8 1.0 copy-start.3
  125.8 63.0 %collective-permute-start.11 = (bf16[8,512,256]{2,1,0:T(8,128)(2,1)}, bf16[8,512,256]{2,1,0:T(8,128)(2,1)S(1)}, u32[]{:S(2)}, u32[]{:S(2)}) collective-permute-start(bf16[8,512,256]{2,1,0:T(8,128)(2,1)} %get-tuple-element.36), channel_id=1, source_target_pairs={{0,2},{1,3},{4,6},{5,7},{8,10},{9,11},{12,14},{13,15},{16,18},{17,... | collective-permute-start | bytes 6291464 | tf_op jit(solution)/shard_map/ppermute | solution.py:375
  145.2 88.6 %collective-permute-start.13 = (bf16[8,512,256]{2,1,0:T(8,128)(2,1)}, bf16[8,512,256]{2,1,0:T(8,128)(2,1)}, u32[]{:S(2)}, u32[]{:S(2)}) collective-permute-start(bf16[8,512,256]{2,1,0:T(8,128)(2,1)} %get-tuple-element.37), channel_id=1, source_target_pairs={{0,2},{1,3},{4,6},{5,7},{8,10},{9,11},{12,14},{13,15},{16,18},{17,... | collective-permute-start | bytes 6291464 | tf_op jit(solution)/shard_map/ppermute | solution.py:375
  146.7 89.0 %collective-permute-start.5 = (bf16[8,256,256]{2,1,0:T(8,128)(2,1)S(1)}, bf16[8,256,256]{2,1,0:T(8,128)(2,1)}, u32[]{:S(2)}, u32[]{:S(2)}) collective-permute-start(bf16[8,256,256]{2,1,0:T(8,128)(2,1)S(1)} %collective-permute-done.3.refs_0_), channel_id=1, source_target_pairs={{0,1},{1,0},{2,3},{3,2},{4,5},{5,4},{6,7},{7,6},{8,9},{9,8},{10,11... | collective-permute-start | bytes 3145736 | tf_op jit(solution)/shard_map/ppermute | solution.py:375
  148.1 87.6 %collective-permute-start.6 = (bf16[8,256,256]{2,1,0:T(8,128)(2,1)}, bf16[8,256,256]{2,1,0:T(8,128)(2,1)}, u32[]{:S(2)}, u32[]{:S(2)}) collective-permute-start(bf16[8,256,256]{2,1,0:T(8,128)(2,1)} %copy-done.2), channel_id=1, source_target_pairs={{0,1},{1,0},{2,3},{3,2},{4,5},{5,4},{6,7},{7,6},{8,9},{9,8},{10,11... | collective-permute-start | bytes 3145736 | tf_op jit(solution)/shard_map/ppermute | solution.py:375
  148.2 87.5 %collective-permute-start.9 = (bf16[8,256,256]{2,1,0:T(8,128)(2,1)}, bf16[8,256,256]{2,1,0:T(8,128)(2,1)}, u32[]{:S(2)}, u32[]{:S(2)}) collective-permute-start(bf16[8,256,256]{2,1,0:T(8,128)(2,1)} %copy-done.3), channel_id=1, source_target_pairs={{0,1},{1,0},{2,3},{3,2},{4,5},{5,4},{6,7},{7,6},{8,9},{9,8},{10,11... | collective-permute-start | bytes 3145736 | tf_op jit(solution)/shard_map/ppermute | solution.py:375
  188.8 51.2 %copy-start = (bf16[8,512,256]{2,1,0:T(8,128)(2,1)}, bf16[8,512,256]{2,1,0:T(8,128)(2,1)S(1)}, u32[]{:S(2)}) copy-start(bf16[8,512,256]{2,1,0:T(8,128)(2,1)S(1)} %collective-permute-done.11.refs_5_) | copy-start | bytes 6291460
  188.8 93.9 %collective-permute-start.12 = (bf16[8,512,256]{2,1,0:T(8,128)(2,1)S(1)}, bf16[8,512,256]{2,1,0:T(8,128)(2,1)}, u32[]{:S(2)}, u32[]{:S(2)}) collective-permute-start(bf16[8,512,256]{2,1,0:T(8,128)(2,1)S(1)} %collective-permute-done.11.refs_5_), channel_id=1, source_target_pairs={{0,1},{1,0},{2,3},{3,2},{4,5},{5,4},{6,7},{7,6},{8,9},{9,8},{10,11... | collective-permute-start | bytes 6291464 | tf_op jit(solution)/shard_map/ppermute | solution.py:375
  233.8 48.9 %collective-permute-start.14 = (bf16[8,512,256]{2,1,0:T(8,128)(2,1)}, bf16[8,512,256]{2,1,0:T(8,128)(2,1)}, u32[]{:S(2)}, u32[]{:S(2)}) collective-permute-start(bf16[8,512,256]{2,1,0:T(8,128)(2,1)} %collective-permute-done.13.refs_7_), channel_id=1, source_target_pairs={{0,1},{1,0},{2,3},{3,2},{4,5},{5,4},{6,7},{7,6},{8,9},{9,8},{10,11... | collective-permute-start | bytes 6291464 | tf_op jit(solution)/shard_map/ppermute | solution.py:375
  240.0 59.9 %collective-permute-start.15 = (f32[8,256,256]{2,1,0:T(8,128)}, f32[8,256,256]{2,1,0:T(8,128)}, u32[]{:S(2)}, u32[]{:S(2)}) collective-permute-start(f32[8,256,256]{2,1,0:T(8,128)} %get-tuple-element.39), channel_id=1, source_target_pairs={{4,6},{5,7},{0,1},{1,0},{2,3},{3,2},{12,14},{13,15},{8,9},{9,8},{1... | collective-permute-start | bytes 6291464 | tf_op jit(solution)/shard_map/ppermute | solution.py:375
  241.3 58.6 %collective-permute-start.16 = (f32[8,8,256]{2,1,0:T(8,128)}, f32[8,8,256]{2,1,0:T(8,128)S(1)}, u32[]{:S(2)}, u32[]{:S(2)}) collective-permute-start(f32[8,8,256]{2,1,0:T(8,128)} %get-tuple-element.40), channel_id=1, source_target_pairs={{4,6},{5,7},{0,1},{1,0},{2,3},{3,2},{12,14},{13,15},{8,9},{9,8},{1... | collective-permute-start | bytes 196616 | tf_op jit(solution)/shard_map/ppermute | solution.py:375
  299.9 0.6 copy-start.4

commit v6 on v5

--- a/solution.py
+++ b/solution.py
@@ -85,32 +85,6 @@
         cost_estimate=pl.CostEstimate(flops=10 ** 8, bytes_accessed=3 * src.size, transcendentals=0),
         name="pack",
     )(*[runs] * n_groups)
-
-
-def sort_kernel(x_ref, y_ref, perm_ref):
-    @pl.when(pl.program_id(0) == 0)
-    def _():
-        row = lax.broadcasted_iota(jnp.int32, (CHUNK, CHUNK), 0)
-        col = lax.broadcasted_iota(jnp.int32, (CHUNK, CHUNK), 1)
-        perm_ref[...] = (col == (row % RUN) * CLASSES + row // RUN).astype(F32).astype(BF16)
-
-    y_ref[...] = dot_nn(perm_ref[...], x_ref[...]).astype(BF16)
-
-
-def sort_by_class(x):
-    tokens, width = x.shape
-    spec = pl.BlockSpec((CHUNK, width), lambda i: (i, 0))
-    return pl.pallas_call(
-        sort_kernel,
-        grid=(tokens // CHUNK,),
-        out_shape=jax.ShapeDtypeStruct(x.shape, BF16),
-        in_specs=[spec],
-        out_specs=spec,
-        scratch_shapes=[pltpu.VMEM((CHUNK, CHUNK), BF16)],
-        compiler_params=params(),
-        cost_estimate=pl.CostEstimate(flops=2 * 10 ** 9, bytes_accessed=4 * x.size, transcendentals=0),
-        name="sort_by_class",
-    )(x)
 
 
 def head_spec(shape, first=0, last=None, flag=None):
@@ -366,22 +340,27 @@
     row_spec = P(('dp', 'seq'), None)
     swap = [(s, s ^ 1) for s in range(8)]
     next_chip = [(0, 2), (1, 3), (4, 6), (5, 7)]
-    from_first = [(0, 4), (1, 5), (2, 3), (3, 2), (6, 7), (7, 6)]
-    from_second = [(2, 4), (3, 5), (0, 1), (1, 0), (6, 7), (7, 6)]
+    swap_upper = [(s, s ^ 1) for s in (2, 3, 6, 7)]
+    from_first = [(0, 4), (1, 5)]
+    from_second = [(2, 4), (3, 5)]
+    swap_third = [(4, 5), (5, 4)]
     to_third = [(6, 4), (7, 5)]
-    to_fourth = [(4, 6), (5, 7), (0, 1), (1, 0), (2, 3), (3, 2)]
+    to_fourth = [(4, 6), (5, 7)]
 
     def send(array, pairs):
         return lax.ppermute(array, 'seq', pairs)
 
     def layer(hidden, w_query, w_key, w_value, w_out):
-        _, d_model = hidden.shape
+        tokens, d_model = hidden.shape
         num_heads, head_dim = w_query.shape[1:]
         index = lax.axis_index('seq')
         chip = index // 2
         flags = jnp.stack([index % 2, chip % 2, (chip == 2).astype(jnp.int32), (chip == 3).astype(jnp.int32)]).astype(jnp.int32)
 
-        x = sort_by_class(hidden)
+        order = jnp.arange(CHUNK)
+        perm = ((order % RUN) * CLASSES + order // RUN)[:, None] == order[None, :]
+        x = jnp.einsum('pq,cqd->cpd', perm.astype(BF16), hidden.reshape(tokens // CHUNK, CHUNK, d_model),
+                       preferred_element_type=F32).astype(BF16).reshape(tokens, d_model)
 
         def project(weight):
             return jnp.einsum('td,dhe->hte', x, weight, preferred_element_type=F32)
@@ -392,8 +371,8 @@
             second = send(far_rows, from_second)
             quad = send(quad_rows, next_chip)
             pair = send(pair_rows, swap)
-            swapped = send(first, swap), send(second, swap)
-            return pair, (quad, send(quad, swap)), (first, second, *swapped)
+            swapped = send(first, swap_third), send(second, swap_third)
+            return pair, (quad, send(quad, swap_upper)), (first, second, *swapped)
 
         k = project(w_key).astype(BF16)
         pair_k, quad_k, far_k = spread(pack(k, (1, 2, 4)))

time: 344 us -> 338 us (0.983)
  the two profiles are of different devices: /device:TPU:31 before, /device:TPU:26 now
where the time goes in v6:
time: 338 us; the launch traced here: 337 us
  Pallas kernels  123 us (36%)
  waiting for transfers between devices  98.5 us (29%)
  matrix products  74.2 us (22%)
  starting transfers between devices  39 us (12%)
    ppermute x17, waiting for transfers between devices, send(): return lax.ppermute(array, 'seq', pairs)  98.5 us
    dot_general x3, matrix products, project(): return jnp.einsum('td,dhe->hte', x, weight, preferred_element_type=F32)  68.2 us
    pallas_call x2, Pallas kernels, local_attention(): pl.pallas_call(lambda *refs: local_kernel(first_head, *refs), grid_spec=p...  55.7 us
    pallas_call x1, Pallas kernels, final_attention(): pl.pallas_call(lambda *refs: final_kernel(num_heads, *refs), grid_spec=pl...  42.7 us
    ppermute x17, starting transfers between devices, send(): return lax.ppermute(array, 'seq', pairs)  39 us
    pallas_call x3, Pallas kernels, pack(): pl.pallas_call(lambda *refs: pack_kernel(n_groups, *refs), grid=(num_head...  19.9 us
  transfers between devices with their start and end apart: 17, of which 4 were waited for; matrix products, arithmetic and copies ran while one was open for 14% of the time, Pallas kernels for 22%

profile of v6, /device:TPU:26, one launch (start us, length us, event | category | flops | bytes accessed | tf_op | source)
XLA Modules:
  0.0 336.8 jit_solution(7671554311883243795)
XLA Ops:
  0.0 0.0 copy-start.1
  0.0 5.9 %convolution_convert_fusion = bf16[256,8,2048]{2,0,1:T(8,128)(2,1)S(1)} fusion(bf16[8,256,2048]{2,1,0:T(8,128)(2,1)} %bitcast.42, s32[256]{0:T(256)S(1)} %fusion.20), kind=kOutput, calls=%fused_computation.9 | convolution fusion | flops 2151743488 | bytes 16778240 | tf_op jit(solution)/shard_map/pq,cqd->cpd/dot_general | solution.py:362
  5.9 0.0 copy-start
  5.9 0.0 copy-done.1
  5.9 21.4 %fusion.6 = bf16[2048,8,256]{2,0,1:T(8,128)(2,1)} fusion(bf16[2048,2048,1]{1,0,2:T(8,128)(2,1)S(1)} %bitcast.43, bf16[2048,8,256]{2,1,0:T(8,128)(2,1)S(1)} %copy-done.1), kind=kOutput, calls=%fused_computation.7 | convolution fusion | flops 17184063488 | bytes 25165824 | tf_op jit(solution)/shard_map/td,dhe->hte/dot_general | solution.py:366
  27.4 0.0 copy-done
  27.4 7.3 %pack.3 = (bf16[8,256,256]{2,1,0:T(8,128)(2,1)}, bf16[8,512,256]{2,1,0:T(8,128)(2,1)}, bf16[8,1024,256]{2,1,0:T(8,128)(2,1)}) custom-call(bf16[8,8,8,32,256]{4,3,2,1,0:T(8,128)(2,1)} %bitcast.27, bf16[8,8,8,32,256]{4,3,2,1,0:T(8,128)(2,1)} %bitcast.28, bf16[8,8,8,32,256]{4,3,2,1,0:T(8,128)(2,1)} %bitcast.29, bf16[8,8,8,32,256]{4,3,2,1,0:T(8,128)(2,1)} %bitcast.30), custom_call_target="tpu_custom_call" | custom-call | flops 100000000 | bytes 12582912 | tf_op jit(solution)/shard_map/pack/pallas_call | solution.py:78
  34.7 0.7 collective-permute-start.3
  35.4 0.7 collective-permute-start.4
  36.2 0.1 collective-permute-start
  36.2 23.4 %fusion.9 = bf16[2048,8,256]{2,0,1:T(8,128)(2,1)} fusion(bf16[2048,2048,1]{1,0,2:T(8,128)(2,1)} %bitcast.44, bf16[2048,8,256]{2,1,0:T(8,128)(2,1)} %param.8), kind=kOutput, calls=%fused_computation.8 | convolution fusion | flops 17184063488 | bytes 25165824 | tf_op jit(solution)/shard_map/td,dhe->hte/dot_general | solution.py:366
  59.7 7.4 %pack.4 = (bf16[8,256,256]{2,1,0:T(8,128)(2,1)}, bf16[8,512,256]{2,1,0:T(8,128)(2,1)}, bf16[8,1024,256]{2,1,0:T(8,128)(2,1)}) custom-call(bf16[8,8,8,32,256]{4,3,2,1,0:T(8,128)(2,1)} %bitcast.33, bf16[8,8,8,32,256]{4,3,2,1,0:T(8,128)(2,1)} %bitcast.34, bf16[8,8,8,32,256]{4,3,2,1,0:T(8,128)(2,1)} %bitcast.35, bf16[8,8,8,32,256]{4,3,2,1,0:T(8,128)(2,1)} %bitcast.36), custom_call_target="tpu_custom_call" | custom-call | flops 100000000 | bytes 12582912 | tf_op jit(solution)/shard_map/pack/pallas_call | solution.py:78
  67.1 0.5 collective-permute-start.1
  67.5 1.6 collective-permute-start.8
  69.2 23.4 %multiply_convert_fusion = bf16[2048,8,256]{2,0,1:T(8,128)(2,1)} fusion(bf16[2048,2048,1]{1,0,2:T(8,128)(2,1)} %bitcast.45, bf16[2048,8,256]{2,1,0:T(8,128)(2,1)} %param.6), kind=kOutput, calls=%fused_computation | convolution fusion | flops 17188257792 | bytes 25165824 | tf_op jit(solution)/shard_map/td,dhe->hte/dot_general | solution.py:366
  92.6 0.0 collective-permute-done.8.refs_5_
  92.6 0.7 collective-permute-start.7
  93.3 5.2 %pack.5.qa_ref = bf16[8,256,256]{2,1,0:T(8,128)(2,1)} custom-call(bf16[8,8,8,32,256]{4,3,2,1,0:T(8,128)(2,1)} %bitcast.39), custom_call_target="tpu_custom_call" | custom-call | flops 100000000 | bytes 12582912 | tf_op jit(solution)/shard_map/pack/pallas_call | solution.py:78
  98.5 0.0 collective-permute-done.3.refs_0_
  98.5 0.0 copy-start.3
  98.5 18.9 %collective-permute-start.2 = (bf16[8,256,256]{2,1,0:T(8,128)(2,1)}, bf16[8,256,256]{2,1,0:T(8,128)(2,1)}, u32[]{:S(2)}, u32[]{:S(2)}) collective-permute-start(bf16[8,256,256]{2,1,0:T(8,128)(2,1)} %pack.5.qa_ref), channel_id=1, source_target_pairs={{6,4},{7,5},{14,12},{15,13},{22,20},{23,21},{30,28},{31,29}} | collective-permute-start | bytes 3145736 | tf_op jit(solution)/shard_map/ppermute | solution.py:351
  117.4 0.0 collective-permute-done.4.refs_1_
  117.4 0.0 copy-start.4
  117.4 1.6 collective-permute-start.10
  119.1 0.0 collective-permute-done.7.refs_4_
  119.1 0.0 copy-done.4
  119.1 0.0 copy-start.5
  119.1 1.0 copy-done.5
  120.1 1.3 collective-permute-start.11
  121.4 18.0 %collective-permute-done.2.qb_ref = bf16[8,256,256]{2,1,0:T(8,128)(2,1)} collective-permute-done((bf16[8,256,256]{2,1,0:T(8,128)(2,1)}, bf16[8,256,256]{2,1,0:T(8,128)(2,1)}, u32[]{:S(2)}, u32[]{:S(2)}) %collective-permute-start.2) | collective-permute-done | bytes 1048608 | tf_op jit(solution)/shard_map/ppermute | solution.py:351
  139.4 1.3 collective-permute-start.13
  140.7 0.0 collective-permute-done.10.refs_7_
  140.7 1.6 collective-permute-start.5
  142.3 0.0 collective-permute-done.refs_4_
  142.3 1.7 collective-permute-start.6
  144.0 0.0 collective-permute-done.1.refs_5_
  144.0 1.6 collective-permute-start.9
  145.6 0.7 pad_add_fusion.refs_0_.flag_ref
  146.3 15.9 %local_attention.2 = (bf16[8,256,2048]{2,1,0:T(8,128)(2,1)}, f32[8,256,512]{2,1,0:T(8,128)}, f32[8,8,512]{2,1,0:T(8,128)}, bf16[8,512,256]{2,1,0:T(8,128)(2,1)}) custom-call(s32[4]{0:T(128)} %pad_add_fusion.refs_0_.flag_ref, bf16[8,2048,256]{2,1,0:T(8,128)(2,1)} %bitcast.40, bf16[8,2048,256]{2,1,0:T(8,128)(2,1)} %bitcast.31, bf16[8,2048,256]{2,1,0:T(8,128)(2,1)} %bitcast.37, ...), custom_call_target="tpu_custom_call" | custom-call | flops 10000000000 | bytes 20000000 | tf_op jit(solution)/shard_map/local_attention/pallas_call | solution.py:183
  162.2 0.0 copy-done.3
  162.2 22.8 %collective-permute-done.11.refs_5_ = bf16[8,512,256]{2,1,0:T(8,128)(2,1)S(1)} collective-permute-done((bf16[8,512,256]{2,1,0:T(8,128)(2,1)}, bf16[8,512,256]{2,1,0:T(8,128)(2,1)S(1)}, u32[]{:S(2)}, u32[]{:S(2)}) %collective-permute-start.11) | collective-permute-done | bytes 2097184 | tf_op jit(solution)/shard_map/ppermute | solution.py:351
  185.1 0.0 copy-start.2
  185.1 1.9 collective-permute-start.12
  187.0 41.6 %collective-permute-done.13.refs_7_ = bf16[8,512,256]{2,1,0:T(8,128)(2,1)} collective-permute-done((bf16[8,512,256]{2,1,0:T(8,128)(2,1)}, bf16[8,512,256]{2,1,0:T(8,128)(2,1)}, u32[]{:S(2)}, u32[]{:S(2)}) %collective-permute-start.13) | collective-permute-done | bytes 2097184 | tf_op jit(solution)/shard_map/ppermute | solution.py:351
  228.6 1.9 collective-permute-start.14
  230.5 0.0 collective-permute-done.5.refs_2_
  230.5 0.0 collective-permute-done.6.refs_3_
  230.6 0.0 collective-permute-done.9.refs_6_
  230.6 4.3 %far_attention.1 = (f32[8,256,256]{2,1,0:T(8,128)}, f32[8,8,256]{2,1,0:T(8,128)}, f32[8,256,256]{2,1,0:T(8,128)}, f32[8,8,256]{2,1,0:T(8,128)}) custom-call(s32[4]{0:T(128)} %pad_add_fusion.refs_0_.flag_ref, bf16[8,256,256]{2,1,0:T(8,128)(2,1)} %pack.5.qa_ref, bf16[8,256,256]{2,1,0:T(8,128)(2,1)} %collective-permute-done.2.qb_ref, ...), custom_call_target="tpu_custom_call" | custom-call | flops 5000000000 | bytes 20000000 | tf_op jit(solution)/shard_map/far_attention/pallas_call | solution.py:229
  234.8 0.0 copy-done.2
  234.8 1.3 collective-permute-start.15
  236.1 1.5 collective-permute-start.16
  237.7 39.8 %local_attention.3 = (bf16[8,256,2048]{2,1,0:T(8,128)(2,1)}, f32[8,256,512]{2,1,0:T(8,128)}, f32[8,8,512]{2,1,0:T(8,128)}, bf16[8,512,256]{2,1,0:T(8,128)(2,1)}) custom-call(s32[4]{0:T(128)} %pad_add_fusion.refs_0_.flag_ref, bf16[8,2048,256]{2,1,0:T(8,128)(2,1)} %bitcast.41, ...), custom_call_target="tpu_custom_call", output_to_operand_aliasing={{0}: (6, {}), {1}: (7, {}), {2}: (8, {}), {3}: (9, {})} | custom-call | flops 30000001024 | bytes 60000000 | tf_op jit(solution)/shard_map/local_attention/pallas_call | solution.py:183
  277.5 0.0 collective-permute-done.12.refs_6_
  277.5 0.0 collective-permute-done.14.refs_8_
  277.5 16.0 %collective-permute-done.16.refs_12_ = f32[8,8,256]{2,1,0:T(8,128)S(1)} collective-permute-done((f32[8,8,256]{2,1,0:T(8,128)}, f32[8,8,256]{2,1,0:T(8,128)S(1)}, u32[]{:S(2)}, u32[]{:S(2)}) %collective-permute-start.16) | collective-permute-done | bytes 65568 | tf_op jit(solution)/shard_map/ppermute | solution.py:351
  293.5 0.0 copy-start.6
  293.5 0.0 collective-permute-done.15.refs_11_
  293.5 0.6 copy-done.6
  294.1 42.7 %final_attention.1 = bf16[2048,2048]{1,0:T(8,128)(2,1)} custom-call(s32[4]{0:T(128)} %pad_add_fusion.refs_0_.flag_ref, bf16[8,512,256]{2,1,0:T(8,128)(2,1)} %get-tuple-element.32.refs_1_, bf16[8,256,2048]{2,1,0:T(8,128)(2,1)} %get-tuple-element.33.refs_2_, f32[8,256,512]{2,1,0:T(8,128)} %get-tuple-element.34.refs_3_, ...), custom_call_target="tpu_custom_call" | custom-call | flops 30000001024 | bytes 60000000 | tf_op jit(solution)/shard_map/final_attention/pallas_call | solution.py:323
  (1 shorter events, 0.0 us)
Async XLA Ops:
  0.0 5.9 %copy-start.1 = (bf16[2048,8,256]{2,1,0:T(8,128)(2,1)S(1)}, bf16[2048,8,256]{2,1,0:T(8,128)(2,1)}, u32[]{:S(2)}) copy-start(bf16[2048,8,256]{2,1,0:T(8,128)(2,1)} %param.7) | copy-start | bytes 25165828
  5.9 21.4 %copy-start = (bf16[256,8,2048]{2,0,1:T(8,128)(2,1)}, bf16[256,8,2048]{2,0,1:T(8,128)(2,1)S(1)}, u32[]{:S(2)}) copy-start(bf16[256,8,2048]{2,0,1:T(8,128)(2,1)S(1)} %convolution_convert_fusion) | copy-start | bytes 25165828
  34.7 63.8 %collective-permute-start.3 = (bf16[8,256,256]{2,1,0:T(8,128)(2,1)}, bf16[8,256,256]{2,1,0:T(8,128)(2,1)S(1)}, u32[]{:S(2)}, u32[]{:S(2)}) collective-permute-start(bf16[8,256,256]{2,1,0:T(8,128)(2,1)} %get-tuple-element.29), channel_id=1, source_target_pairs={{0,4},{1,5},{8,12},{9,13},{16,20},{17,21},{24,28},{25,29}} | collective-permute-start | bytes 3145736 | tf_op jit(solution)/shard_map/ppermute | solution.py:351
  35.4 82.0 %collective-permute-start.4 = (bf16[8,256,256]{2,1,0:T(8,128)(2,1)}, bf16[8,256,256]{2,1,0:T(8,128)(2,1)S(1)}, u32[]{:S(2)}, u32[]{:S(2)}) collective-permute-start(bf16[8,256,256]{2,1,0:T(8,128)(2,1)} %get-tuple-element.29), channel_id=1, source_target_pairs={{2,4},{3,5},{10,12},{11,13},{18,20},{19,21},{26,28},{27,29}} | collective-permute-start | bytes 3145736 | tf_op jit(solution)/shard_map/ppermute | solution.py:351
  36.2 106.2 %collective-permute-start = (bf16[8,1024,256]{2,1,0:T(8,128)(2,1)}, bf16[8,1024,256]{2,1,0:T(8,128)(2,1)}, u32[]{:S(2)}, u32[]{:S(2)}) collective-permute-start(bf16[8,1024,256]{2,1,0:T(8,128)(2,1)} %get-tuple-element.23), channel_id=1, source_target_pairs={{0,1},{1,0},{2,3},{3,2},{4,5},{5,4},{6,7},{7,6},{8,9},{9,8},{10,11... | collective-permute-start | bytes 12582920 | tf_op jit(solution)/shard_map/ppermute | solution.py:351
  67.1 77.0 %collective-permute-start.1 = (bf16[8,1024,256]{2,1,0:T(8,128)(2,1)}, bf16[8,1024,256]{2,1,0:T(8,128)(2,1)}, u32[]{:S(2)}, u32[]{:S(2)}) collective-permute-start(bf16[8,1024,256]{2,1,0:T(8,128)(2,1)} %get-tuple-element.24), channel_id=1, source_target_pairs={{0,1},{1,0},{2,3},{3,2},{4,5},{5,4},{6,7},{7,6},{8,9},{9,8},{10,11... | collective-permute-start | bytes 12582920 | tf_op jit(solution)/shard_map/ppermute | solution.py:351
  67.5 25.1 %collective-permute-start.8 = (bf16[8,256,256]{2,1,0:T(8,128)(2,1)}, bf16[8,256,256]{2,1,0:T(8,128)(2,1)}, u32[]{:S(2)}, u32[]{:S(2)}) collective-permute-start(bf16[8,256,256]{2,1,0:T(8,128)(2,1)} %get-tuple-element.30), channel_id=1, source_target_pairs={{2,4},{3,5},{10,12},{11,13},{18,20},{19,21},{26,28},{27,29}} | collective-permute-start | bytes 3145736 | tf_op jit(solution)/shard_map/ppermute | solution.py:351
  92.6 26.5 %collective-permute-start.7 = (bf16[8,256,256]{2,1,0:T(8,128)(2,1)}, bf16[8,256,256]{2,1,0:T(8,128)(2,1)S(1)}, u32[]{:S(2)}, u32[]{:S(2)}) collective-permute-start(bf16[8,256,256]{2,1,0:T(8,128)(2,1)} %get-tuple-element.30), channel_id=1, source_target_pairs={{0,4},{1,5},{8,12},{9,13},{16,20},{17,21},{24,28},{25,29}} | collective-permute-start | bytes 3145736 | tf_op jit(solution)/shard_map/ppermute | solution.py:351
  98.5 63.7 %copy-start.3 = (bf16[8,256,256]{2,1,0:T(8,128)(2,1)}, bf16[8,256,256]{2,1,0:T(8,128)(2,1)S(1)}, u32[]{:S(2)}) copy-start(bf16[8,256,256]{2,1,0:T(8,128)(2,1)S(1)} %collective-permute-done.3.refs_0_) | copy-start | bytes 3145732
  98.5 40.9 %collective-permute-start.2 = (bf16[8,256,256]{2,1,0:T(8,128)(2,1)}, bf16[8,256,256]{2,1,0:T(8,128)(2,1)}, u32[]{:S(2)}, u32[]{:S(2)}) collective-permute-start(bf16[8,256,256]{2,1,0:T(8,128)(2,1)} %pack.5.qa_ref), channel_id=1, source_target_pairs={{6,4},{7,5},{14,12},{15,13},{22,20},{23,21},{30,28},{31,29}} | collective-permute-start | bytes 3145736 | tf_op jit(solution)/shard_map/ppermute | solution.py:351
  117.4 1.7 copy-start.4
  117.4 23.3 %collective-permute-start.10 = (bf16[8,256,256]{2,1,0:T(8,128)(2,1)}, bf16[8,256,256]{2,1,0:T(8,128)(2,1)}, u32[]{:S(2)}, u32[]{:S(2)}) collective-permute-start(bf16[8,256,256]{2,1,0:T(8,128)(2,1)} %collective-permute-done.8.refs_5_), channel_id=1, source_target_pairs={{4,5},{5,4},{12,13},{13,12},{20,21},{21,20},{28,29},{29,28}} | collective-permute-start | bytes 3145736 | tf_op jit(solution)/shard_map/ppermute | solution.py:351
  119.1 1.0 copy-start.5
  120.1 65.0 %collective-permute-start.11 = (bf16[8,512,256]{2,1,0:T(8,128)(2,1)}, bf16[8,512,256]{2,1,0:T(8,128)(2,1)S(1)}, u32[]{:S(2)}, u32[]{:S(2)}) collective-permute-start(bf16[8,512,256]{2,1,0:T(8,128)(2,1)} %get-tuple-element.36), channel_id=1, source_target_pairs={{0,2},{1,3},{4,6},{5,7},{8,10},{9,11},{12,14},{13,15},{16,18},{17,... | collective-permute-start | bytes 6291464 | tf_op jit(solution)/shard_map/ppermute | solution.py:351
  139.4 89.2 %collective-permute-start.13 = (bf16[8,512,256]{2,1,0:T(8,128)(2,1)}, bf16[8,512,256]{2,1,0:T(8,128)(2,1)}, u32[]{:S(2)}, u32[]{:S(2)}) collective-permute-start(bf16[8,512,256]{2,1,0:T(8,128)(2,1)} %get-tuple-element.37), channel_id=1, source_target_pairs={{0,2},{1,3},{4,6},{5,7},{8,10},{9,11},{12,14},{13,15},{16,18},{17,... | collective-permute-start | bytes 6291464 | tf_op jit(solution)/shard_map/ppermute | solution.py:351
  140.7 89.8 %collective-permute-start.5 = (bf16[8,256,256]{2,1,0:T(8,128)(2,1)S(1)}, bf16[8,256,256]{2,1,0:T(8,128)(2,1)}, u32[]{:S(2)}, u32[]{:S(2)}) collective-permute-start(bf16[8,256,256]{2,1,0:T(8,128)(2,1)S(1)} %collective-permute-done.3.refs_0_), channel_id=1, source_target_pairs={{4,5},{5,4},{12,13},{13,12},{20,21},{21,20},{28,29},{29,28}} | collective-permute-start | bytes 3145736 | tf_op jit(solution)/shard_map/ppermute | solution.py:351
  142.3 88.2 %collective-permute-start.6 = (bf16[8,256,256]{2,1,0:T(8,128)(2,1)}, bf16[8,256,256]{2,1,0:T(8,128)(2,1)}, u32[]{:S(2)}, u32[]{:S(2)}) collective-permute-start(bf16[8,256,256]{2,1,0:T(8,128)(2,1)} %copy-done.4), channel_id=1, source_target_pairs={{4,5},{5,4},{12,13},{13,12},{20,21},{21,20},{28,29},{29,28}} | collective-permute-start | bytes 3145736 | tf_op jit(solution)/shard_map/ppermute | solution.py:351
  144.0 86.5 %collective-permute-start.9 = (bf16[8,256,256]{2,1,0:T(8,128)(2,1)}, bf16[8,256,256]{2,1,0:T(8,128)(2,1)}, u32[]{:S(2)}, u32[]{:S(2)}) collective-permute-start(bf16[8,256,256]{2,1,0:T(8,128)(2,1)} %copy-done.5), channel_id=1, source_target_pairs={{4,5},{5,4},{12,13},{13,12},{20,21},{21,20},{28,29},{29,28}} | collective-permute-start | bytes 3145736 | tf_op jit(solution)/shard_map/ppermute | solution.py:351
  185.1 49.7 %copy-start.2 = (bf16[8,512,256]{2,1,0:T(8,128)(2,1)}, bf16[8,512,256]{2,1,0:T(8,128)(2,1)S(1)}, u32[]{:S(2)}) copy-start(bf16[8,512,256]{2,1,0:T(8,128)(2,1)S(1)} %collective-permute-done.11.refs_5_) | copy-start | bytes 6291460
  185.1 92.4 %collective-permute-start.12 = (bf16[8,512,256]{2,1,0:T(8,128)(2,1)S(1)}, bf16[8,512,256]{2,1,0:T(8,128)(2,1)}, u32[]{:S(2)}, u32[]{:S(2)}) collective-permute-start(bf16[8,512,256]{2,1,0:T(8,128)(2,1)S(1)} %collective-permute-done.11.refs_5_), channel_id=1, source_target_pairs={{2,3},{3,2},{6,7},{7,6},{10,11},{11,10},{14,15},{15,14},{18,19},{1... | collective-permute-start | bytes 6291464 | tf_op jit(solution)/shard_map/ppermute | solution.py:351
  228.6 48.9 %collective-permute-start.14 = (bf16[8,512,256]{2,1,0:T(8,128)(2,1)}, bf16[8,512,256]{2,1,0:T(8,128)(2,1)}, u32[]{:S(2)}, u32[]{:S(2)}) collective-permute-start(bf16[8,512,256]{2,1,0:T(8,128)(2,1)} %collective-permute-done.13.refs_7_), channel_id=1, source_target_pairs={{2,3},{3,2},{6,7},{7,6},{10,11},{11,10},{14,15},{15,14},{18,19},{1... | collective-permute-start | bytes 6291464 | tf_op jit(solution)/shard_map/ppermute | solution.py:351
  234.8 58.6 %collective-permute-start.15 = (f32[8,256,256]{2,1,0:T(8,128)}, f32[8,256,256]{2,1,0:T(8,128)}, u32[]{:S(2)}, u32[]{:S(2)}) collective-permute-start(f32[8,256,256]{2,1,0:T(8,128)} %get-tuple-element.39), channel_id=1, source_target_pairs={{4,6},{5,7},{12,14},{13,15},{20,22},{21,23},{28,30},{29,31}} | collective-permute-start | bytes 6291464 | tf_op jit(solution)/shard_map/ppermute | solution.py:351
  236.1 57.3 %collective-permute-start.16 = (f32[8,8,256]{2,1,0:T(8,128)}, f32[8,8,256]{2,1,0:T(8,128)S(1)}, u32[]{:S(2)}, u32[]{:S(2)}) collective-permute-start(f32[8,8,256]{2,1,0:T(8,128)} %get-tuple-element.40), channel_id=1, source_target_pairs={{4,6},{5,7},{12,14},{13,15},{20,22},{21,23},{28,30},{29,31}} | collective-permute-start | bytes 196616 | tf_op jit(solution)/shard_map/ppermute | solution.py:351
  293.5 0.6 copy-start.6
